TPU v7x, 32 devices: a whole 2x2x4 slice. The times are simulated.
32 devices in a mesh: virt: 8 (over z, x), aux: 4 (over y, core).
Axes of the slice: x: 2, y: 2, z: 4, core: 2. Of those that a mesh axis runs over, the one named last changes fastest.
Arguments:
- three_index: bfloat16 [600, 5120], P('aux', 'virt'), may hold values from -0.0625 to 0.0625
- eps_occ: float32 [20], replicated, may hold values from -1.5 to -0.5
- eps_virt: float32 [256], replicated, may hold values from 0.3 to 3
Outputs:
- virt_energy: float32 [256], P('virt')
- pair_energy: float32 [20, 20], replicated
All inputs are finite; a program needn't handle non-finite values.
Results may differ from a plain program's by a relative error of at most 0.0003.
Values may be sent and summed in bfloat16 or wider, within the bound.
A program may use at most 128 MiB of HBM per device.

v0:
```python
import functools

import jax
import jax.numpy as jnp
from jax import lax
from jax.experimental import pallas as pl
from jax.experimental.pallas import tpu as pltpu
from jax.sharding import PartitionSpec as P

MESH = pl.DeviceIdType.MESH
F32 = jnp.float32
BF16 = jnp.bfloat16
EXACT = lax.Precision.HIGHEST
LANES = 128
NT = (((1,), (1,)), ((), ()))
NN = (((1,), (0,)), ((), ()))


def distances(n_aux):
    return list(range(1, n_aux + 1, 2)) + list(range(2, n_aux + 1, 2))


def pick(table, at):
    got = jnp.int32(table[0])
    for k in range(1, len(table)):
        got = jnp.where(at == k, jnp.int32(table[k]), got)
    return got


def label_of(virt, n_virt):
    return lax.rem(virt, 2) * (n_virt // 2) + virt // 2


def virt_of(label, n_virt):
    half = n_virt // 2
    return lax.rem(label, half) * 2 + label // half


def kernel(
    n_virt, n_aux, occ,
    x_ref, occ_ref, virt_ref,
    done_ref,
    held, lhs, rhs, order, order_t, ints, sums, parts, message, slots,
    own_sem, send_sem, recv_sem, msg_send, msg_recv,
):
    rows, cols = x_ref.shape
    pitch = -(-rows // 16) * 16
    width = cols // occ
    groups = LANES // width
    supers = occ // groups
    n = n_virt * n_aux
    v = lax.axis_index("virt")
    p = lax.axis_index("aux")
    me = v * n_aux + p
    table = distances(n_aux)
    label = label_of(v, n_virt)
    other = virt_of(lax.rem(label + pick(table, p), n_virt), n_virt)
    lower = label < n_virt // 2
    solo = jnp.logical_and(p == n_aux - 1, jnp.logical_not(lower))
    extra = jnp.logical_and(p == n_aux // 2 - 1, lower)

    barrier = pltpu.get_barrier_semaphore()

    def greet(k, c):
        t = lax.rem(me + k, n)
        pl.semaphore_signal(
            barrier, inc=1,
            device_id={"virt": t // n_aux, "aux": lax.rem(t, n_aux)},
            device_id_type=MESH,
        )
        return c

    lax.fori_loop(1, n, greet, 0)
    own = pltpu.make_async_copy(x_ref, held.at[0, p], own_sem)
    own.start()
    pl.semaphore_wait(barrier, n - 1)

    pairs = n_aux // 2

    def place(k):
        return lax.rem(p // 2 + k // 2, pairs) * 2 + lax.rem(p + k, 2)

    def share_own(k):
        return pltpu.make_async_remote_copy(
            src_ref=x_ref, dst_ref=held.at[0, p],
            send_sem=send_sem.at[0, k], recv_sem=recv_sem.at[0, p],
            device_id={"virt": v, "aux": place(k)}, device_id_type=MESH,
        )

    def hand_on(k):
        q = place(k)
        return pltpu.make_async_remote_copy(
            src_ref=held.at[0, q], dst_ref=held.at[0, q],
            send_sem=send_sem.at[2, k], recv_sem=recv_sem.at[0, q],
            device_id={"virt": v, "aux": place(1)}, device_id_type=MESH,
        )

    def share_other(k):
        q = place(k)
        target = lax.rem(label + n_virt - pick(table, q), n_virt)
        copy = pltpu.make_async_remote_copy(
            src_ref=x_ref, dst_ref=held.at[1, p],
            send_sem=send_sem.at[1, k], recv_sem=recv_sem.at[1, p],
            device_id={"virt": virt_of(target, n_virt), "aux": q}, device_id_type=MESH,
        )
        wanted = jnp.logical_or(q < n_aux - 1, target < n_virt // 2)
        return copy, wanted

    for k in list(range(2, n_aux, 2)) + [1]:
        share_own(k).start()
    for k in range(n_aux):
        copy, wanted = share_other(k)
        pl.when(wanted)(copy.start)

    def arrived(side, q):
        pltpu.make_async_copy(
            held.at[side, q], held.at[side, q], recv_sem.at[side, q]
        ).wait()

    row = lax.broadcasted_iota(jnp.int32, (cols, cols), 0)
    col = lax.broadcasted_iota(jnp.int32, (cols, cols), 1)
    hit = col == lax.rem(row, width) * occ + row // width
    order[...] = jnp.where(hit, 1.0, 0.0).astype(BF16)
    hit = row == lax.rem(col, width) * occ + col // width
    order_t[...] = jnp.where(hit, 1.0, 0.0).astype(BF16)
    lhs[...] = jnp.zeros_like(lhs)
    rhs[...] = jnp.zeros_like(rhs)

    def turn(k):
        lhs[:, k * pitch:k * pitch + rows] = lax.dot_general(
            order[...], held[0, place(k)], NT, preferred_element_type=F32
        ).astype(BF16)

    own.wait()
    turn(0)
    for k in range(2, n_aux, 2):
        arrived(0, place(k))
        hand_on(k).start()
        turn(k)
    for k in range(1, n_aux, 2):
        arrived(0, place(k))
        turn(k)

    lane = lax.broadcasted_iota(jnp.int32, (1, LANES), 1)
    part = lane // width
    down = lax.broadcasted_iota(jnp.int32, (width, 1), 0)
    lane_in = lax.rem(lane, width)

    def eps_down(which):
        got = jnp.zeros((width, 1), F32)
        for k in range(width):
            got = jnp.where(down == k, virt_ref[which * width + k], got)
        return got

    def eps_across(which):
        got = jnp.zeros((1, LANES), F32)
        for k in range(width):
            got = jnp.where(lane_in == k, virt_ref[which * width + k], got)
        return got

    occ_lane = []
    for cj in range(supers):
        got = jnp.zeros((1, LANES), F32)
        for t in range(groups):
            got = jnp.where(part == t, occ_ref[cj * groups + t], got)
        occ_lane.append(got)

    tall = -(-occ // 8)
    sums[...] = jnp.zeros_like(sums)
    n_tiles = jnp.where(extra, 2, 1)
    r8 = lax.broadcasted_iota(jnp.int32, (8, LANES), 0)
    l8 = lax.broadcasted_iota(jnp.int32, (8, LANES), 1)
    free = tall * width

    def tile(t, c):
        diag = jnp.logical_or(solo, jnp.logical_and(extra, t == 0))
        source = jnp.where(diag, 0, 1)

        for k in range(n_aux):

            @pl.when(source == 1)
            def _():
                arrived(1, place(k))

            rhs[k * pitch:k * pitch + rows, :] = lax.dot_general(
                held[source, place(k)], order_t[...], NN, preferred_element_type=F32
            ).astype(BF16)
        ints[...] = lax.dot_general(lhs[...], rhs[...], NN, preferred_element_type=F32)

        base = -(eps_down(v) + eps_across(jnp.where(diag, v, other)))
        total = jnp.zeros((width, LANES), F32)
        for ci in range(supers):
            for cj in range(ci, supers):
                turned = []
                for g in range(groups):
                    block = ints[pl.ds((cj * groups + g) * width, width), pl.ds(ci * LANES, LANES)]
                    turned.append([block if r == 0 else pltpu.roll(block, r * width, 1) for r in range(groups)])
                for s in range(groups):
                    i = ci * groups + s
                    direct = ints[pl.ds(i * width, width), pl.ds(cj * LANES, LANES)]
                    swapped = turned[0][(0 - s) % groups]
                    for g in range(1, groups):
                        swapped = jnp.where(part == g, turned[g][(g - s) % groups], swapped)
                    below = base + (occ_lane[cj] + occ_ref[i])
                    if ci == cj:
                        term = direct * (2.0 * direct - swapped) / below
                    else:
                        term = 2.0 * (direct * (direct - swapped) + swapped * swapped) / below
                    total = total + term
                    short = term[0:8]
                    for m in range(8, width, 8):
                        short = short + term[m:m + 8]
                    sums[i * 8:i * 8 + 8, cj * LANES:(cj + 1) * LANES] = short

        wide = lax.broadcasted_iota(jnp.int32, (cols, LANES), 0)
        thin = lax.broadcasted_iota(jnp.int32, (cols, LANES), 1)
        fold = jnp.where(wide // width == thin, 1.0, 0.0)
        by_j = lax.dot_general(sums[...], fold, NN, precision=EXACT, preferred_element_type=F32)
        ri = lax.broadcasted_iota(jnp.int32, (tall * 8, occ * 8), 0)
        rj = lax.broadcasted_iota(jnp.int32, (tall * 8, occ * 8), 1)
        by_ij = lax.dot_general(
            jnp.where(rj // 8 == ri, 1.0, 0.0), by_j, NN,
            precision=EXACT, preferred_element_type=F32,
        )
        packed = by_ij[0:8]
        for g in range(1, tall):
            packed = packed + pltpu.roll(by_ij[g * 8:g * 8 + 8], g * width, 1)
        pads = [jnp.zeros((free, LANES), F32), total]
        if free + width < LANES:
            pads.append(jnp.zeros((LANES - free - width, LANES), F32))
        spread = jnp.concatenate(pads, 0)
        by_row = lax.dot_general(
            jnp.ones((8, LANES), F32), spread, NT, precision=EXACT, preferred_element_type=F32)
        by_col = lax.dot_general(
            jnp.ones((8, width), F32), total, NN, precision=EXACT, preferred_element_type=F32)
        folded = by_col
        for g in range(1, groups):
            folded = folded + pltpu.roll(by_col, g * width, 1)
        packed = packed * jnp.where(diag, 0.5, 1.0)
        first = jnp.where(diag, (by_row + folded) * 0.5, by_row)
        second = jnp.where(diag, 0.0, folded)
        out = jnp.where(l8 < free, packed, jnp.where(r8 == 0, first, jnp.where(r8 == 1, second, 0.0)))

        @pl.when(t == 0)
        def _():
            message[...] = out

        @pl.when(t == 1)
        def _():
            message[...] += out

        return c

    lax.fori_loop(0, n_tiles, tile, 0)

    def tell(k, c):
        t = lax.rem(me + k, n)
        pltpu.make_async_remote_copy(
            src_ref=message, dst_ref=slots.at[me],
            send_sem=msg_send, recv_sem=msg_recv,
            device_id={"virt": t // n_aux, "aux": lax.rem(t, n_aux)},
            device_id_type=MESH,
        ).start()
        return c

    lax.fori_loop(1, n, tell, 0)
    slots[me] = message[...]
    for k in list(range(2, n_aux, 2)) + [1]:
        share_own(k).wait_send()
    for k in range(2, n_aux, 2):
        hand_on(k).wait_send()
    for k in range(n_aux):
        copy, wanted = share_other(k)
        pl.when(wanted)(copy.wait_send)
    everyone = slots.at[pl.ds(0, n - 1)]
    pltpu.make_async_copy(everyone, everyone, msg_send).wait()
    pltpu.make_async_copy(everyone, everyone, msg_recv).wait()

    keep = jnp.logical_or(l8 < free, r8 < 0)

    def add(k, acc):
        sv = k // n_aux
        so = virt_of(lax.rem(label_of(sv, n_virt) + pick(table, lax.rem(k, n_aux)), n_virt), n_virt)
        row0 = jnp.where(sv == v, 1.0, 0.0)
        row1 = jnp.where(so == v, 1.0, 0.0)
        weight = jnp.where(keep, 1.0, jnp.where(r8 == 0, row0, row1))
        return acc + slots[k] * weight

    done = lax.fori_loop(0, n, add, jnp.zeros((8, LANES), F32))
    done_ref[...] = done


def unpack(occ, width, done_ref, share_ref, pair_ref):
    tall = -(-occ // 8)
    free = tall * width
    done = done_ref[...]
    share = done[0:1] + done[1:2]
    share_ref[...] = share[0, free:free + width]
    blocks = [done] + [pltpu.roll(done, LANES - g * width, 1) for g in range(1, tall)]
    square = jnp.concatenate(blocks + [jnp.zeros((LANES - 8 * tall, LANES), F32)], 0)
    square = jnp.where(lax.broadcasted_iota(jnp.int32, (LANES, LANES), 1) < occ, square, 0.0)
    pair = square + square.T
    pair_ref[...] = pair[0:occ, 0:occ]


def on_device(n_virt, n_aux, three_index, eps_occ, eps_virt):
    occ = eps_occ.shape[0]
    rows, cols = three_index.shape
    width = cols // occ
    pitch = -(-rows // 16) * 16
    n = n_virt * n_aux
    vmem = pl.BlockSpec(memory_space=pltpu.VMEM)
    smem = pl.BlockSpec(memory_space=pltpu.SMEM)
    done = pl.pallas_call(
        functools.partial(kernel, n_virt, n_aux, occ),
        out_shape=jax.ShapeDtypeStruct((8, LANES), F32),
        in_specs=[vmem, smem, smem],
        out_specs=vmem,
        scratch_shapes=[
            pltpu.VMEM((2, n_aux, rows, cols), BF16),
            pltpu.VMEM((cols, n_aux * pitch), BF16),
            pltpu.VMEM((n_aux * pitch, cols), BF16),
            pltpu.VMEM((cols, cols), BF16),
            pltpu.VMEM((cols, cols), BF16),
            pltpu.VMEM((cols, cols), F32),
            pltpu.VMEM((occ * 8, cols), F32),
            pltpu.VMEM((8, LANES), F32),
            pltpu.VMEM((8, LANES), F32),
            pltpu.VMEM((n, 8, LANES), F32),
            pltpu.SemaphoreType.DMA,
            pltpu.SemaphoreType.DMA((3, n_aux)),
            pltpu.SemaphoreType.DMA((2, n_aux)),
            pltpu.SemaphoreType.DMA,
            pltpu.SemaphoreType.DMA,
        ],
        compiler_params=pltpu.CompilerParams(collective_id=0, has_side_effects=True),
    )(three_index, eps_occ, eps_virt)
    return pl.pallas_call(
        functools.partial(unpack, occ, width),
        out_shape=(
            jax.ShapeDtypeStruct((width,), F32),
            jax.ShapeDtypeStruct((occ, occ), F32),
        ),
        in_specs=[vmem],
        out_specs=(vmem, vmem),
    )(done)


def solution(mesh):
    n_virt, n_aux = mesh.shape["virt"], mesh.shape["aux"]
    assert n_virt == 2 * n_aux and n_aux % 2 == 0
    in_specs = (P("aux", "virt"), P(), P())
    out_specs = (P("virt"), P())
    return jax.shard_map(
        functools.partial(on_device, n_virt, n_aux), mesh=mesh,
        in_specs=in_specs, out_specs=out_specs, check_vma=False,
    )
```

profile of v0, /device:TPU:0, one launch (start us, length us, event | category | flops | bytes accessed | tf_op | source)
XLA Modules:
  0.0 38.6 jit_solution(16628554847428697774)
XLA Ops:
  0.6 36.5 %shard_map.50.done_ref = f32[8,128]{1,0:T(8,128)} custom-call(bf16[150,640]{1,0:T(8,128)(2,1)} %x_ref.1, f32[20]{0:T(128)} %occ_ref.1, f32[256]{0:T(256)} %virt_ref.1), custom_call_target="tpu_custom_call" | custom-call | tf_op jit(solution)/shard_map/pallas_call | solution.py:314
  37.2 1.4 %shard_map.51 = (f32[32]{0:T(128)}, f32[20,20]{1,0:T(8,128)}) custom-call(f32[8,128]{1,0:T(8,128)} %shard_map.50.done_ref), custom_call_target="tpu_custom_call" | custom-call | tf_op jit(solution)/shard_map/pallas_call | solution.py:338
where the time goes:
time: 38.8 us; the launch traced here: 38.6 us
  Pallas kernels  37.9 us (98%)
  between operations  0.64 us (2%)
    pallas_call x1, Pallas kernels, on_device(): pl.pallas_call(functools.partial(kernel, n_virt, n_aux, occ), out_shape=j...  36.5 us
    pallas_call x1, Pallas kernels, on_device(): pl.pallas_call(functools.partial(unpack, occ, width), out_shape=(jax.Shap...  1.42 us

commit v1 on v0

--- a/solution.py
+++ b/solution.py
@@ -21,9 +21,9 @@
 
 
 def pick(table, at):
-    got = jnp.int32(table[0])
+    got = table[0] + jnp.int32(0)
     for k in range(1, len(table)):
-        got = jnp.where(at == k, jnp.int32(table[k]), got)
+        got = jnp.where(at == k, table[k] + jnp.int32(0), got)
     return got
 
 
@@ -290,6 +290,408 @@
     done_ref[...] = done
 
 
+TILES = (
+    (0, 2, 1),
+    (0, 2, 0),
+    (0, 1, 0),
+    (1, 3, 0),
+    (1, 2, 0),
+    (1, 3, 1),
+    (0, 3, 0),
+    (2, 3, 0),
+    (0, 4, 0),
+    (1, 4, 0),
+    (2, 4, 0),
+    (0, 5, 0),
+    (2, 5, 0),
+    (1, 5, 0),
+    (3, 4, 0),
+    (3, 5, 0),
+    (0, 7, 0),
+    (0, 6, 0),
+    (2, 6, 0),
+    (2, 7, 0),
+    (1, 6, 0),
+    (1, 7, 0),
+    (3, 6, 0),
+    (3, 7, 0),
+    (6, 7, 0),
+    (7, 5, 1),
+    (6, 4, 1),
+    (7, 4, 0),
+    (6, 5, 0),
+    (6, 4, 0),
+    (7, 5, 0),
+    (4, 5, 0),
+)
+ROUTES = (
+    ((2, 16, 12), (16,), (), (2, 34, 16), (), (), (3, 9), (3, 9), ()),
+    ((4,), (0, 4), (), (), (1,), (1,), (), (), ()),
+    ((), (12, 22), (12, 16, 22, 2), (12, 22), (), (), (), (18,), ()),
+    ((5,), (5,), (5,), (5,), (), (), (), (), (4, 0)),
+    ((10,), (6,), (10,), (10,), (), (14,), (), (24, 14), ()),
+    ((26, 6), (8, 26), (26,), (), (), (), (7,), (), ()),
+    ((), (), (), (), (15, 7), (15, 7), (11,), (15,), (8, 6)),
+    ((), (), (), (), (), (), (13,), (7, 11), (6, 42, 8)),
+    ((34, 22), (), (32, 0), (), (21,), (19, 21), (19,), (19,), (20, 24, 3)),
+    ((), (), (), (), (17, 29), (), (), (), (9, 36, 24, 3)),
+    ((36, 38), (), (24, 36, 1), (), (), (29,), (17, 29), (17, 29), ()),
+    ((), (32,), (), (), (), (), (), (), (1, 20, 36)),
+    ((9,), (), (14,), (), (27,), (), (), (), (13, 46, 11)),
+    ((42, 18), (40, 18), (40, 18), (), (), (25, 31), (25,), (25,), (28, 11)),
+    ((), (30, 13), (15, 30, 46), (44,), (), (), (), (), ()),
+    ((28,), (44,), (44,), (28, 13), (), (23,), (27, 23), (23, 27), ()),
+    ((), (34,), (34,), (), (), (), (39,), (43, 50), (55, 19, 59)),
+    ((32,), (), (), (32,), (37,), (), (), (41,), (17, 55)),
+    ((14,), (38,), (38,), (38,), (52, 45), (45,), (35,), (), (21, 62, 55)),
+    ((), (20,), (), (), (), (), (), (), (21, 62)),
+    ((), (42,), (42,), (26,), (), (35,), (58,), (), (57, 25, 23, 51)),
+    ((40,), (), (), (40,), (47, 39), (33, 47), (), (47,), (27, 57)),
+    ((), (46,), (), (46,), (), (), (41, 37), (), (51, 31, 61)),
+    ((44, 30), (), (), (), (), (39,), (43,), (), (31, 57, 63)),
+    ((35, 58), (37, 52), (), (35, 58), (54,), (50,), (), (), ()),
+    ((49, 33), (), (49, 54), (49,), (), (), (57,), (), (48, 56)),
+    ((), (), (45, 48), (), (62,), (62,), (), (), ()),
+    ((), (), (), (39,), (53,), (53,), (53,), (53,), (52, 48, 45, 37)),
+    ((41,), (58, 41), (), (), (61,), (63, 51), (), (51,), (50, 43, 60)),
+    ((56,), (), (56,), (56,), (), (), (), (), (43, 60, 49)),
+    ((), (54,), (33, 50, 47), (), (63, 31), (), (63,), (), ()),
+    ((), (59,), (59,), (59, 55), (), (61,), (), (61,), (33, 60, 54)),
+)
+STEPS = (
+    (0, 1, 2, 3, 14, 15, 6, 7, 8, 9, 12, 10, 13, 4, 11, 5),
+    (2, 3, 0, 1, 14, 8, 15, 9, 6, 10, 7, 11, 12, 4, 13, 5),
+    (4, 5, 6, 7, 2, 3, 14, 15, 12, 8, 13, 9, 10, 0, 11, 1),
+    (6, 7, 4, 0, 5, 1, 8, 2, 9, 3, 14, 15, 12, 10, 13, 11),
+    (0, 1, 2, 3, 4, 10, 5, 11, 6, 7, 14, 15, 12, 8, 13, 9),
+    (2, 3, 0, 1, 4, 10, 5, 11, 6, 12, 7, 13, 8, 14, 9, 15),
+    (4, 8, 5, 12, 9, 6, 14, 13, 0, 2, 15, 1, 3, 10, 7, 11),
+    (12, 13, 8, 9, 14, 15, 4, 10, 5, 2, 11, 6, 0, 7, 1, 3),
+    (0, 10, 4, 1, 11, 5, 2, 14, 3, 8, 12, 9, 15, 13, 6, 7),
+    (10, 8, 11, 2, 9, 14, 3, 12, 15, 0, 13, 4, 6, 5, 7, 1),
+    (4, 5, 6, 7, 0, 14, 1, 12, 15, 10, 13, 11, 2, 3, 8, 9),
+    (6, 14, 2, 8, 15, 3, 12, 4, 10, 5, 9, 13, 11, 0, 1, 7),
+    (0, 4, 1, 10, 5, 2, 11, 3, 8, 14, 9, 15, 12, 6, 13, 7),
+    (2, 10, 3, 11, 0, 14, 1, 15, 4, 8, 12, 5, 9, 13, 6, 7),
+    (4, 5, 6, 7, 2, 3, 14, 12, 15, 0, 8, 10, 1, 9, 13, 11),
+    (6, 7, 4, 5, 14, 15, 2, 12, 3, 10, 13, 11, 0, 1, 8, 9),
+    (14, 15, 10, 4, 12, 0, 11, 13, 8, 6, 2, 9, 7, 3, 5, 1),
+    (8, 9, 0, 14, 4, 6, 15, 7, 1, 2, 12, 10, 3, 13, 5, 11),
+    (6, 2, 7, 3, 4, 0, 10, 1, 11, 8, 12, 5, 9, 13, 14, 15),
+    (6, 2, 7, 3, 4, 14, 5, 10, 8, 11, 15, 0, 9, 12, 1, 13),
+    (6, 2, 7, 3, 12, 10, 13, 11, 0, 8, 4, 1, 14, 9, 5, 15),
+    (10, 6, 11, 7, 8, 9, 2, 14, 0, 3, 15, 1, 12, 4, 13, 5),
+    (12, 0, 6, 13, 1, 7, 14, 2, 15, 3, 10, 11, 4, 8, 9, 5),
+    (0, 1, 6, 10, 7, 11, 12, 2, 8, 13, 4, 3, 9, 14, 5, 15),
+    (0, 1, 2, 3, 6, 8, 7, 10, 9, 11, 14, 12, 4, 15, 13, 5),
+    (0, 12, 1, 2, 13, 6, 3, 4, 8, 7, 5, 9, 14, 10, 11, 15),
+    (4, 5, 6, 7, 10, 11, 8, 2, 9, 12, 3, 13, 14, 0, 15, 1),
+    (10, 6, 11, 7, 8, 9, 12, 0, 13, 14, 1, 15, 2, 4, 3, 5),
+    (8, 2, 9, 3, 14, 10, 15, 11, 0, 1, 6, 12, 7, 4, 5, 13),
+    (2, 0, 3, 14, 1, 15, 6, 12, 7, 13, 4, 10, 5, 8, 11, 9),
+    (4, 5, 6, 7, 2, 3, 0, 8, 12, 9, 13, 14, 10, 1, 11, 15),
+    (6, 7, 4, 5, 2, 8, 14, 12, 10, 3, 9, 11, 0, 15, 13, 1),
+)
+PLANS = {(8, 4): (TILES, ROUTES, STEPS)}
+
+
+KIDS = 4
+CODE = 128
+
+
+def table_kernel(
+    n_virt, n_aux, occ, plan,
+    x_ref, occ_ref, virt_ref,
+    done_ref,
+    held, lhs, rhs, order, order_t, ints, sums, message, slots,
+    own_sem, send_sem, recv_sem, msg_send, msg_recv,
+):
+    rows, cols = x_ref.shape
+    pitch = -(-rows // 16) * 16
+    width = cols // occ
+    groups = LANES // width
+    supers = occ // groups
+    n = n_virt * n_aux
+    v = lax.axis_index("virt")
+    p = lax.axis_index("aux")
+    me = v * n_aux + p
+    tiles, routes, steps = plan
+    half = -(-rows // 32) * 16
+    cuts = ((0, half), (half, rows - half))
+    n_slots = 2 * n_aux
+
+    def device(t):
+        return {"virt": lax.div(t, n_aux), "aux": lax.rem(t, n_aux)}
+
+    barrier = pltpu.get_barrier_semaphore()
+
+    def greet(k, c):
+        t = me + k
+        t = jnp.where(t >= n, t - n, t)
+        pl.semaphore_signal(barrier, inc=1, device_id=device(t), device_id_type=MESH)
+        return c
+
+    side_a = pick([t[0] for t in tiles], me)
+    side_b = pick([t[1] for t in tiles], me)
+    diag = pick([t[2] for t in tiles], me) == 1
+    own_slot = jnp.where(side_a == v, p, jnp.where(side_b == v, n_aux + p, n_slots))
+    own = pltpu.make_async_copy(x_ref, held.at[own_slot], own_sem)
+    own.start()
+    lax.fori_loop(1, n, greet, 0)
+
+    def packed(codes):
+        got = 0
+        for c in reversed(codes):
+            got = got * CODE + c + 1
+        return got
+
+    kids = [pick([packed(r[s]) for r in routes], me) for s in range(n_slots + 1)]
+    todo = [pick([r[i] for r in steps], me) for i in range(2 * n_slots)]
+
+    row = lax.broadcasted_iota(jnp.int32, (cols, cols), 0)
+    col = lax.broadcasted_iota(jnp.int32, (cols, cols), 1)
+    hit = col == lax.rem(row, width) * occ + row // width
+    order[...] = jnp.where(hit, 1.0, 0.0).astype(BF16)
+    hit = row == lax.rem(col, width) * occ + col // width
+    order_t[...] = jnp.where(hit, 1.0, 0.0).astype(BF16)
+    lhs[...] = jnp.zeros_like(lhs)
+    rhs[...] = jnp.zeros_like(rhs)
+
+    own.wait()
+    pl.semaphore_wait(barrier, n - 1)
+
+    def piece(slot, part):
+        return held.at[slot, pl.ds(cuts[part][0], cuts[part][1])]
+
+    def copies(slot, part, act):
+        code = pick(kids, slot)
+        q = jnp.where(slot == n_slots, p, lax.rem(slot, n_aux))
+        for k in range(KIDS):
+            this = lax.rem(code, CODE)
+            code = lax.div(code, CODE)
+
+            @pl.when(this > 0)
+            def _():
+                t = this - 1
+                to = lax.rem(t, 2) * n_aux + q
+                copy = pltpu.make_async_remote_copy(
+                    src_ref=piece(slot, part), dst_ref=piece(to, part),
+                    send_sem=send_sem.at[slot, part, k], recv_sem=recv_sem.at[to, part],
+                    device_id=device(lax.div(t, 2)), device_id_type=MESH,
+                )
+                act(copy)
+
+    for part in range(2):
+        copies(own_slot, part, lambda copy: copy.start())
+
+    def take(i, c):
+        entry = pick(todo, i)
+        slot = lax.div(entry, 2)
+        later = lax.rem(entry, 2)
+        away = slot != own_slot
+        for part in range(2):
+
+            @pl.when(jnp.logical_and(later == part, away))
+            def _():
+                whole = piece(slot, part)
+                pltpu.make_async_copy(whole, whole, recv_sem.at[slot, part]).wait()
+                copies(slot, part, lambda copy: copy.start())
+
+        side = lax.div(slot, n_aux)
+        for q in range(n_aux):
+            here = jnp.logical_and(later == 1, lax.rem(slot, n_aux) == q)
+
+            @pl.when(jnp.logical_and(here, jnp.logical_or(side == 0, diag)))
+            def _():
+                lhs[side, :, q * pitch:q * pitch + rows] = lax.dot_general(
+                    order[...], held[slot], NT, preferred_element_type=F32
+                ).astype(BF16)
+
+            @pl.when(jnp.logical_and(here, jnp.logical_or(side == 1, diag)))
+            def _():
+                rhs[side, q * pitch:q * pitch + rows, :] = lax.dot_general(
+                    held[slot], order_t[...], NN, preferred_element_type=F32
+                ).astype(BF16)
+
+        return c
+
+    lax.fori_loop(0, 2 * n_slots, take, 0)
+
+    lane = lax.broadcasted_iota(jnp.int32, (1, LANES), 1)
+    part = lane // width
+    down = lax.broadcasted_iota(jnp.int32, (width, 1), 0)
+    lane_in = lax.rem(lane, width)
+
+    def eps_down(which):
+        got = jnp.zeros((width, 1), F32)
+        for k in range(width):
+            got = jnp.where(down == k, virt_ref[which * width + k], got)
+        return got
+
+    def eps_across(which):
+        got = jnp.zeros((1, LANES), F32)
+        for k in range(width):
+            got = jnp.where(lane_in == k, virt_ref[which * width + k], got)
+        return got
+
+    occ_lane = []
+    for cj in range(supers):
+        got = jnp.zeros((1, LANES), F32)
+        for t in range(groups):
+            got = jnp.where(part == t, occ_ref[cj * groups + t], got)
+        occ_lane.append(got)
+
+    tall = -(-occ // 8)
+    sums[...] = jnp.zeros_like(sums)
+    n_tiles = jnp.where(diag, 2, 1)
+    r8 = lax.broadcasted_iota(jnp.int32, (8, LANES), 0)
+    l8 = lax.broadcasted_iota(jnp.int32, (8, LANES), 1)
+    free = tall * width
+
+    def tile(t, c):
+        left = t
+        right = jnp.where(diag, t, 1)
+        ints[...] = lax.dot_general(lhs[left], rhs[right], NN, preferred_element_type=F32)
+        block_l = jnp.where(left == 0, side_a, side_b)
+        block_r = jnp.where(right == 0, side_a, side_b)
+        base = -(eps_down(block_l) + eps_across(block_r))
+        total = jnp.zeros((width, LANES), F32)
+        for ci in range(supers):
+            for cj in range(ci, supers):
+                turned = []
+                for g in range(groups):
+                    block = ints[pl.ds((cj * groups + g) * width, width), pl.ds(ci * LANES, LANES)]
+                    turned.append([block if r == 0 else pltpu.roll(block, r * width, 1) for r in range(groups)])
+                for s in range(groups):
+                    i = ci * groups + s
+                    direct = ints[pl.ds(i * width, width), pl.ds(cj * LANES, LANES)]
+                    swapped = turned[0][(0 - s) % groups]
+                    for g in range(1, groups):
+                        swapped = jnp.where(part == g, turned[g][(g - s) % groups], swapped)
+                    below = base + (occ_lane[cj] + occ_ref[i])
+                    if ci == cj:
+                        term = direct * (2.0 * direct - swapped) / below
+                    else:
+                        term = 2.0 * (direct * (direct - swapped) + swapped * swapped) / below
+                    total = total + term
+                    short = term[0:8]
+                    for m in range(8, width, 8):
+                        short = short + term[m:m + 8]
+                    sums[i * 8:i * 8 + 8, cj * LANES:(cj + 1) * LANES] = short
+
+        wide = lax.broadcasted_iota(jnp.int32, (cols, LANES), 0)
+        thin = lax.broadcasted_iota(jnp.int32, (cols, LANES), 1)
+        fold = jnp.where(wide // width == thin, 1.0, 0.0)
+        by_j = lax.dot_general(sums[...], fold, NN, precision=EXACT, preferred_element_type=F32)
+        ri = lax.broadcasted_iota(jnp.int32, (tall * 8, occ * 8), 0)
+        rj = lax.broadcasted_iota(jnp.int32, (tall * 8, occ * 8), 1)
+        by_ij = lax.dot_general(
+            jnp.where(rj // 8 == ri, 1.0, 0.0), by_j, NN,
+            precision=EXACT, preferred_element_type=F32,
+        )
+        packed_ij = by_ij[0:8]
+        for g in range(1, tall):
+            packed_ij = packed_ij + pltpu.roll(by_ij[g * 8:g * 8 + 8], g * width, 1)
+        pads = [jnp.zeros((free, LANES), F32), total]
+        if free + width < LANES:
+            pads.append(jnp.zeros((LANES - free - width, LANES), F32))
+        spread = jnp.concatenate(pads, 0)
+        by_row = lax.dot_general(
+            jnp.ones((8, LANES), F32), spread, NT, precision=EXACT, preferred_element_type=F32)
+        by_col = lax.dot_general(
+            jnp.ones((8, width), F32), total, NN, precision=EXACT, preferred_element_type=F32)
+        folded = by_col
+        for g in range(1, groups):
+            folded = folded + pltpu.roll(by_col, g * width, 1)
+        packed_ij = packed_ij * jnp.where(diag, 0.5, 1.0)
+        both = (by_row + folded) * 0.5
+        first = jnp.where(diag, jnp.where(t == 0, both, 0.0), by_row)
+        second = jnp.where(diag, jnp.where(t == 1, both, 0.0), folded)
+        out = jnp.where(l8 < free, packed_ij, jnp.where(r8 == 0, first, jnp.where(r8 == 1, second, 0.0)))
+
+        @pl.when(t == 0)
+        def _():
+            message[...] = out
+
+        @pl.when(t == 1)
+        def _():
+            message[...] += out
+
+        return c
+
+    lax.fori_loop(0, n_tiles, tile, 0)
+
+    def tell(k, c):
+        t = me + k
+        t = jnp.where(t >= n, t - n, t)
+        pltpu.make_async_remote_copy(
+            src_ref=message, dst_ref=slots.at[me],
+            send_sem=msg_send, recv_sem=msg_recv,
+            device_id=device(t), device_id_type=MESH,
+        ).start()
+        return c
+
+    lax.fori_loop(1, n, tell, 0)
+    slots[me] = message[...]
+    for part_at in range(2):
+        copies(own_slot, part_at, lambda copy: copy.wait_send())
+
+    def flush(s, c):
+        @pl.when(s != own_slot)
+        def _():
+            for part_at in range(2):
+                copies(s, part_at, lambda copy: copy.wait_send())
+
+        return c
+
+    lax.fori_loop(0, n_slots, flush, 0)
+    everyone = slots.at[pl.ds(0, n - 1)]
+    pltpu.make_async_copy(everyone, everyone, msg_send).wait()
+    pltpu.make_async_copy(everyone, everyone, msg_recv).wait()
+
+    keep = l8 < free
+    acc = None
+    for k in range(n):
+        a, b, _ = tiles[k]
+        row0 = jnp.where(v == a, 1.0, 0.0)
+        row1 = jnp.where(v == b, 1.0, 0.0)
+        term = slots[k] * jnp.where(keep, 1.0, jnp.where(r8 == 0, row0, row1))
+        acc = term if acc is None else acc + term
+    done_ref[...] = acc
+
+
+def table_call(n_virt, n_aux, occ, plan, three_index, eps_occ, eps_virt):
+    rows, cols = three_index.shape
+    pitch = -(-rows // 16) * 16
+    n = n_virt * n_aux
+    n_slots = 2 * n_aux
+    vmem = pl.BlockSpec(memory_space=pltpu.VMEM)
+    smem = pl.BlockSpec(memory_space=pltpu.SMEM)
+    return pl.pallas_call(
+        functools.partial(table_kernel, n_virt, n_aux, occ, plan),
+        out_shape=jax.ShapeDtypeStruct((8, LANES), F32),
+        in_specs=[pl.BlockSpec(memory_space=pltpu.HBM), smem, smem],
+        out_specs=vmem,
+        scratch_shapes=[
+            pltpu.VMEM((n_slots + 1, rows, cols), BF16),
+            pltpu.VMEM((2, cols, n_aux * pitch), BF16),
+            pltpu.VMEM((2, n_aux * pitch, cols), BF16),
+            pltpu.VMEM((cols, cols), BF16),
+            pltpu.VMEM((cols, cols), BF16),
+            pltpu.VMEM((cols, cols), F32),
+            pltpu.VMEM((occ * 8, cols), F32),
+            pltpu.VMEM((8, LANES), F32),
+            pltpu.VMEM((n, 8, LANES), F32),
+            pltpu.SemaphoreType.DMA,
+            pltpu.SemaphoreType.DMA((n_slots + 1, 2, KIDS)),
+            pltpu.SemaphoreType.DMA((n_slots, 2)),
+            pltpu.SemaphoreType.DMA,
+            pltpu.SemaphoreType.DMA,
+        ],
+        compiler_params=pltpu.CompilerParams(collective_id=0, has_side_effects=True),
+    )(three_index, eps_occ, eps_virt)
+
+
 def unpack(occ, width, done_ref, share_ref, pair_ref):
     tall = -(-occ // 8)
     free = tall * width
@@ -311,30 +713,34 @@
     n = n_virt * n_aux
     vmem = pl.BlockSpec(memory_space=pltpu.VMEM)
     smem = pl.BlockSpec(memory_space=pltpu.SMEM)
-    done = pl.pallas_call(
-        functools.partial(kernel, n_virt, n_aux, occ),
-        out_shape=jax.ShapeDtypeStruct((8, LANES), F32),
-        in_specs=[vmem, smem, smem],
-        out_specs=vmem,
-        scratch_shapes=[
-            pltpu.VMEM((2, n_aux, rows, cols), BF16),
-            pltpu.VMEM((cols, n_aux * pitch), BF16),
-            pltpu.VMEM((n_aux * pitch, cols), BF16),
-            pltpu.VMEM((cols, cols), BF16),
-            pltpu.VMEM((cols, cols), BF16),
-            pltpu.VMEM((cols, cols), F32),
-            pltpu.VMEM((occ * 8, cols), F32),
-            pltpu.VMEM((8, LANES), F32),
-            pltpu.VMEM((8, LANES), F32),
-            pltpu.VMEM((n, 8, LANES), F32),
-            pltpu.SemaphoreType.DMA,
-            pltpu.SemaphoreType.DMA((3, n_aux)),
-            pltpu.SemaphoreType.DMA((2, n_aux)),
-            pltpu.SemaphoreType.DMA,
-            pltpu.SemaphoreType.DMA,
-        ],
-        compiler_params=pltpu.CompilerParams(collective_id=0, has_side_effects=True),
-    )(three_index, eps_occ, eps_virt)
+    plan = PLANS.get((n_virt, n_aux))
+    if plan is not None:
+        done = table_call(n_virt, n_aux, occ, plan, three_index, eps_occ, eps_virt)
+    else:
+        done = pl.pallas_call(
+            functools.partial(kernel, n_virt, n_aux, occ),
+            out_shape=jax.ShapeDtypeStruct((8, LANES), F32),
+            in_specs=[vmem, smem, smem],
+            out_specs=vmem,
+            scratch_shapes=[
+                pltpu.VMEM((2, n_aux, rows, cols), BF16),
+                pltpu.VMEM((cols, n_aux * pitch), BF16),
+                pltpu.VMEM((n_aux * pitch, cols), BF16),
+                pltpu.VMEM((cols, cols), BF16),
+                pltpu.VMEM((cols, cols), BF16),
+                pltpu.VMEM((cols, cols), F32),
+                pltpu.VMEM((occ * 8, cols), F32),
+                pltpu.VMEM((8, LANES), F32),
+                pltpu.VMEM((8, LANES), F32),
+                pltpu.VMEM((n, 8, LANES), F32),
+                pltpu.SemaphoreType.DMA,
+                pltpu.SemaphoreType.DMA((3, n_aux)),
+                pltpu.SemaphoreType.DMA((2, n_aux)),
+                pltpu.SemaphoreType.DMA,
+                pltpu.SemaphoreType.DMA,
+            ],
+            compiler_params=pltpu.CompilerParams(collective_id=0, has_side_effects=True),
+        )(three_index, eps_occ, eps_virt)
     return pl.pallas_call(
         functools.partial(unpack, occ, width),
         out_shape=(

time: 38.8 us -> 36 us (0.928)
  Pallas kernels: 37.9 us -> 35.2 us
    pallas_call x1, Pallas kernels: 36.5 us -> 33.8 us  [table_call(): pl.pallas_call(functools.partial(table_kernel, n_virt, n_aux, occ, plan),...]
where the time goes in v1:
time: 36 us; the launch traced here: 35.9 us
  Pallas kernels  35.2 us (98%)
  between operations  0.64 us (2%)
    pallas_call x1, Pallas kernels, table_call(): pl.pallas_call(functools.partial(table_kernel, n_virt, n_aux, occ, plan),...  33.8 us
    pallas_call x1, Pallas kernels, on_device(): pl.pallas_call(functools.partial(unpack, occ, width), out_shape=(jax.Shap...  1.42 us

profile of v1, /device:TPU:0, one launch (start us, length us, event | category | flops | bytes accessed | tf_op | source)
XLA Modules:
  0.0 35.9 jit_solution(11703790703320777200)
XLA Ops:
  0.6 33.8 %shard_map.50.done_ref = f32[8,128]{1,0:T(8,128)} custom-call(bf16[150,640]{1,0:T(8,128)(2,1)} %x_ref.1, f32[20]{0:T(128)} %occ_ref.1, f32[256]{0:T(256)} %virt_ref.1), custom_call_target="tpu_custom_call" | custom-call | tf_op jit(solution)/shard_map/pallas_call | solution.py:670
  34.4 1.4 %shard_map.51 = (f32[32]{0:T(128)}, f32[20,20]{1,0:T(8,128)}) custom-call(f32[8,128]{1,0:T(8,128)} %shard_map.50.done_ref), custom_call_target="tpu_custom_call" | custom-call | tf_op jit(solution)/shard_map/pallas_call | solution.py:744

commit v2 on v1

--- a/solution.py
+++ b/solution.py
@@ -294,21 +294,21 @@
     (0, 2, 1),
     (0, 2, 0),
     (0, 1, 0),
+    (1, 2, 0),
     (1, 3, 0),
-    (1, 2, 0),
+    (0, 3, 0),
     (1, 3, 1),
-    (0, 3, 0),
     (2, 3, 0),
     (0, 4, 0),
+    (0, 5, 0),
+    (2, 4, 0),
+    (2, 5, 0),
     (1, 4, 0),
-    (2, 4, 0),
-    (0, 5, 0),
-    (2, 5, 0),
+    (3, 4, 0),
     (1, 5, 0),
-    (3, 4, 0),
     (3, 5, 0),
+    (0, 6, 0),
     (0, 7, 0),
-    (0, 6, 0),
     (2, 6, 0),
     (2, 7, 0),
     (1, 6, 0),
@@ -316,83 +316,152 @@
     (3, 6, 0),
     (3, 7, 0),
     (6, 7, 0),
-    (7, 5, 1),
+    (6, 4, 0),
+    (7, 4, 0),
     (6, 4, 1),
-    (7, 4, 0),
     (6, 5, 0),
-    (6, 4, 0),
     (7, 5, 0),
     (4, 5, 0),
+    (7, 5, 1),
 )
 ROUTES = (
-    ((2, 16, 12), (16,), (), (2, 34, 16), (), (), (3, 9), (3, 9), ()),
-    ((4,), (0, 4), (), (), (1,), (1,), (), (), ()),
-    ((), (12, 22), (12, 16, 22, 2), (12, 22), (), (), (), (18,), ()),
-    ((5,), (5,), (5,), (5,), (), (), (), (), (4, 0)),
-    ((10,), (6,), (10,), (10,), (), (14,), (), (24, 14), ()),
-    ((26, 6), (8, 26), (26,), (), (), (), (7,), (), ()),
-    ((), (), (), (), (15, 7), (15, 7), (11,), (15,), (8, 6)),
-    ((), (), (), (), (), (), (13,), (7, 11), (6, 42, 8)),
-    ((34, 22), (), (32, 0), (), (21,), (19, 21), (19,), (19,), (20, 24, 3)),
-    ((), (), (), (), (17, 29), (), (), (), (9, 36, 24, 3)),
-    ((36, 38), (), (24, 36, 1), (), (), (29,), (17, 29), (17, 29), ()),
-    ((), (32,), (), (), (), (), (), (), (1, 20, 36)),
-    ((9,), (), (14,), (), (27,), (), (), (), (13, 46, 11)),
-    ((42, 18), (40, 18), (40, 18), (), (), (25, 31), (25,), (25,), (28, 11)),
-    ((), (30, 13), (15, 30, 46), (44,), (), (), (), (), ()),
-    ((28,), (44,), (44,), (28, 13), (), (23,), (27, 23), (23, 27), ()),
-    ((), (34,), (34,), (), (), (), (39,), (43, 50), (55, 19, 59)),
-    ((32,), (), (), (32,), (37,), (), (), (41,), (17, 55)),
-    ((14,), (38,), (38,), (38,), (52, 45), (45,), (35,), (), (21, 62, 55)),
-    ((), (20,), (), (), (), (), (), (), (21, 62)),
-    ((), (42,), (42,), (26,), (), (35,), (58,), (), (57, 25, 23, 51)),
-    ((40,), (), (), (40,), (47, 39), (33, 47), (), (47,), (27, 57)),
-    ((), (46,), (), (46,), (), (), (41, 37), (), (51, 31, 61)),
-    ((44, 30), (), (), (), (), (39,), (43,), (), (31, 57, 63)),
-    ((35, 58), (37, 52), (), (35, 58), (54,), (50,), (), (), ()),
-    ((49, 33), (), (49, 54), (49,), (), (), (57,), (), (48, 56)),
-    ((), (), (45, 48), (), (62,), (62,), (), (), ()),
-    ((), (), (), (39,), (53,), (53,), (53,), (53,), (52, 48, 45, 37)),
-    ((41,), (58, 41), (), (), (61,), (63, 51), (), (51,), (50, 43, 60)),
-    ((56,), (), (56,), (56,), (), (), (), (), (43, 60, 49)),
-    ((), (54,), (33, 50, 47), (), (63, 31), (), (63,), (), ()),
-    ((), (59,), (59,), (59, 55), (), (61,), (), (61,), (33, 60, 54)),
+    ((2, 10, 34), (10, 4), (2,), (16, 10), (3,), (), (), (3,), ()),
+    ((4, 18), (0, 16), (), (), (14,), (1,), (1,), (), ()),
+    ((), (), (10, 18), (34,), (), (), (), (), ()),
+    ((), (), (5,), (5,), (), (14,), (3, 14, 22), (1, 14), (0, 4)),
+    ((5, 24, 12), (5, 40, 24), (), (24,), (), (11,), (), (11,), ()),
+    ((), (), (0,), (), (9, 13), (), (), (), (8, 12)),
+    ((28, 6), (6, 28), (6, 28), (28, 8), (15,), (15,), (15, 11), (15,), ()),
+    ((), (), (), (), (), (), (), (), (12, 6)),
+    ((), (18, 34), (32,), (2, 18), (21,), (), (25,), (), (1, 36, 22)),
+    ((16,), (), (16,), (), (23,), (), (), (), (20, 3)),
+    ((), (22, 38, 7), (7, 38), (7,), (), (), (17,), (25,), ()),
+    ((20, 7), (), (), (20, 36), (), (), (31, 19), (19,), ()),
+    ((42,), (), (8, 42), (), (17, 27), (), (27,), (27,), (11, 26, 44, 30)),
+    ((), (30, 9), (), (9,), (), (25,), (), (), ()),
+    ((), (), (24,), (42,), (), (23, 31), (), (31,), (13, 30)),
+    ((), (44, 13), (26, 44, 9), (26, 46, 13), (29,), (), (), (), ()),
+    ((), (), (34,), (), (37, 45), (37, 41), (), (48, 41), (25, 51)),
+    ((32,), (32,), (), (32,), (), (39,), (), (), (53, 27, 51, 17)),
+    ((38,), (), (), (38,), (), (54, 45), (), (33, 45), (21, 55)),
+    ((), (36,), (36,), (), (), (), (), (35,), (53, 21, 55)),
+    ((), (42,), (), (), (), (), (), (), (19, 59, 31)),
+    ((40,), (), (40,), (40,), (47, 35), (35, 47), (58, 35), (), (59, 29, 57, 19)),
+    ((46,), (46,), (46,), (), (), (), (37, 41), (), (23, 61, 29)),
+    ((), (), (), (44,), (), (62,), (), (39,), (63, 23, 29)),
+    ((50, 56, 54), (56,), (), (), (), (52,), (), (), ()),
+    ((33,), (33, 48), (48, 56, 33), (), (55, 60), (), (), (17,), ()),
+    ((39,), (), (49,), (), (), (55, 60, 21), (60,), (51, 60), (50, 54)),
+    ((), (), (45,), (37, 56), (53,), (), (51, 53), (), ()),
+    ((41,), (), (), (50,), (), (), (59,), (), (58, 62, 43)),
+    ((49,), (43, 49), (), (43, 49), (57, 63), (61,), (), (57,), ()),
+    ((), (), (), (), (), (63,), (63,), (59,), (52, 62, 39, 47)),
+    ((52,), (), (43,), (47, 52, 58), (61,), (), (57,), (61,), ()),
 )
 STEPS = (
-    (0, 1, 2, 3, 14, 15, 6, 7, 8, 9, 12, 10, 13, 4, 11, 5),
-    (2, 3, 0, 1, 14, 8, 15, 9, 6, 10, 7, 11, 12, 4, 13, 5),
-    (4, 5, 6, 7, 2, 3, 14, 15, 12, 8, 13, 9, 10, 0, 11, 1),
-    (6, 7, 4, 0, 5, 1, 8, 2, 9, 3, 14, 15, 12, 10, 13, 11),
-    (0, 1, 2, 3, 4, 10, 5, 11, 6, 7, 14, 15, 12, 8, 13, 9),
-    (2, 3, 0, 1, 4, 10, 5, 11, 6, 12, 7, 13, 8, 14, 9, 15),
-    (4, 8, 5, 12, 9, 6, 14, 13, 0, 2, 15, 1, 3, 10, 7, 11),
-    (12, 13, 8, 9, 14, 15, 4, 10, 5, 2, 11, 6, 0, 7, 1, 3),
-    (0, 10, 4, 1, 11, 5, 2, 14, 3, 8, 12, 9, 15, 13, 6, 7),
-    (10, 8, 11, 2, 9, 14, 3, 12, 15, 0, 13, 4, 6, 5, 7, 1),
-    (4, 5, 6, 7, 0, 14, 1, 12, 15, 10, 13, 11, 2, 3, 8, 9),
-    (6, 14, 2, 8, 15, 3, 12, 4, 10, 5, 9, 13, 11, 0, 1, 7),
-    (0, 4, 1, 10, 5, 2, 11, 3, 8, 14, 9, 15, 12, 6, 13, 7),
-    (2, 10, 3, 11, 0, 14, 1, 15, 4, 8, 12, 5, 9, 13, 6, 7),
-    (4, 5, 6, 7, 2, 3, 14, 12, 15, 0, 8, 10, 1, 9, 13, 11),
-    (6, 7, 4, 5, 14, 15, 2, 12, 3, 10, 13, 11, 0, 1, 8, 9),
-    (14, 15, 10, 4, 12, 0, 11, 13, 8, 6, 2, 9, 7, 3, 5, 1),
-    (8, 9, 0, 14, 4, 6, 15, 7, 1, 2, 12, 10, 3, 13, 5, 11),
-    (6, 2, 7, 3, 4, 0, 10, 1, 11, 8, 12, 5, 9, 13, 14, 15),
-    (6, 2, 7, 3, 4, 14, 5, 10, 8, 11, 15, 0, 9, 12, 1, 13),
-    (6, 2, 7, 3, 12, 10, 13, 11, 0, 8, 4, 1, 14, 9, 5, 15),
-    (10, 6, 11, 7, 8, 9, 2, 14, 0, 3, 15, 1, 12, 4, 13, 5),
-    (12, 0, 6, 13, 1, 7, 14, 2, 15, 3, 10, 11, 4, 8, 9, 5),
-    (0, 1, 6, 10, 7, 11, 12, 2, 8, 13, 4, 3, 9, 14, 5, 15),
-    (0, 1, 2, 3, 6, 8, 7, 10, 9, 11, 14, 12, 4, 15, 13, 5),
-    (0, 12, 1, 2, 13, 6, 3, 4, 8, 7, 5, 9, 14, 10, 11, 15),
-    (4, 5, 6, 7, 10, 11, 8, 2, 9, 12, 3, 13, 14, 0, 15, 1),
-    (10, 6, 11, 7, 8, 9, 12, 0, 13, 14, 1, 15, 2, 4, 3, 5),
-    (8, 2, 9, 3, 14, 10, 15, 11, 0, 1, 6, 12, 7, 4, 5, 13),
-    (2, 0, 3, 14, 1, 15, 6, 12, 7, 13, 4, 10, 5, 8, 11, 9),
-    (4, 5, 6, 7, 2, 3, 0, 8, 12, 9, 13, 14, 10, 1, 11, 15),
-    (6, 7, 4, 5, 2, 8, 14, 12, 10, 3, 9, 11, 0, 15, 13, 1),
+    (0, 1, 2, 3, 6, 8, 7, 9, 10, 12, 4, 11, 14, 13, 5, 15),
+    (2, 3, 0, 1, 8, 10, 9, 12, 11, 13, 4, 6, 14, 5, 7, 15),
+    (4, 5, 6, 7, 8, 12, 9, 14, 10, 13, 11, 2, 15, 3, 0, 1),
+    (4, 12, 6, 13, 5, 14, 7, 15, 2, 10, 3, 11, 0, 8, 1, 9),
+    (0, 1, 2, 3, 8, 6, 10, 9, 7, 14, 11, 15, 4, 12, 5, 13),
+    (0, 8, 4, 1, 9, 5, 2, 3, 10, 6, 12, 14, 7, 13, 11, 15),
+    (4, 5, 6, 7, 2, 12, 3, 13, 0, 14, 1, 15, 8, 10, 9, 11),
+    (12, 13, 4, 14, 5, 15, 6, 8, 10, 7, 11, 9, 0, 2, 1, 3),
+    (2, 3, 4, 12, 5, 6, 8, 13, 7, 10, 9, 11, 14, 0, 15, 1),
+    (4, 8, 2, 5, 9, 3, 6, 14, 7, 12, 0, 10, 15, 1, 11, 13),
+    (4, 5, 6, 7, 2, 12, 3, 13, 14, 15, 0, 1, 10, 11, 8, 9),
+    (6, 7, 12, 2, 14, 0, 3, 15, 1, 13, 4, 8, 5, 9, 10, 11),
+    (0, 8, 1, 9, 4, 10, 2, 5, 11, 3, 12, 14, 6, 13, 15, 7),
+    (2, 3, 0, 1, 6, 7, 8, 4, 10, 9, 11, 12, 14, 5, 13, 15),
+    (4, 5, 6, 10, 7, 11, 2, 14, 0, 15, 8, 1, 12, 9, 3, 13),
+    (6, 7, 4, 5, 2, 3, 12, 10, 8, 11, 14, 9, 0, 15, 1, 13),
+    (10, 11, 8, 9, 0, 14, 2, 12, 6, 15, 3, 13, 7, 4, 1, 5),
+    (0, 2, 10, 6, 3, 11, 7, 8, 1, 14, 12, 15, 4, 13, 5, 9),
+    (6, 14, 0, 7, 15, 1, 10, 11, 2, 8, 4, 3, 12, 5, 9, 13),
+    (6, 0, 7, 1, 14, 2, 15, 4, 3, 12, 10, 8, 5, 13, 11, 9),
+    (2, 10, 3, 11, 8, 0, 1, 6, 12, 4, 14, 9, 7, 13, 5, 15),
+    (10, 11, 8, 12, 9, 2, 0, 13, 3, 1, 14, 6, 4, 15, 7, 5),
+    (0, 6, 1, 4, 7, 2, 12, 3, 13, 14, 15, 8, 10, 9, 5, 11),
+    (6, 14, 7, 15, 0, 1, 4, 10, 2, 11, 12, 3, 8, 13, 5, 9),
+    (0, 1, 2, 3, 10, 11, 4, 8, 5, 9, 14, 6, 12, 15, 7, 13),
+    (2, 3, 0, 1, 4, 5, 8, 14, 9, 15, 10, 6, 12, 11, 7, 13),
+    (14, 4, 10, 15, 5, 11, 6, 12, 0, 2, 13, 1, 7, 8, 3, 9),
+    (6, 7, 4, 5, 10, 0, 12, 11, 1, 13, 14, 8, 15, 9, 2, 3),
+    (0, 6, 1, 7, 8, 2, 4, 10, 9, 5, 11, 3, 12, 14, 13, 15),
+    (2, 3, 0, 1, 10, 8, 11, 6, 9, 7, 14, 4, 12, 5, 15, 13),
+    (12, 14, 13, 6, 10, 2, 15, 3, 11, 8, 7, 4, 9, 0, 5, 1),
+    (6, 7, 4, 5, 14, 0, 1, 12, 15, 13, 8, 10, 9, 11, 2, 3),
 )
-PLANS = {(8, 4): (TILES, ROUTES, STEPS)}
+PARTNERS = (
+    (1, 2, 4, 8, 3, 5, 17),
+    (0, 3, 5, 9, 2, 7, 8),
+    (3, 0, 6, 10, 1, 4, 5, 9, 17),
+    (2, 1, 7, 11, 0, 6, 10),
+    (5, 6, 0, 12, 2, 13, 15, 20),
+    (4, 7, 1, 13, 0, 2, 6, 12),
+    (7, 4, 2, 14, 3, 5, 15),
+    (6, 5, 3, 15, 1),
+    (9, 10, 12, 0, 16, 1, 11, 17, 18, 25),
+    (8, 11, 13, 1, 17, 2, 10, 20, 21),
+    (11, 8, 14, 2, 18, 3, 9, 12, 19, 26),
+    (10, 9, 15, 3, 19, 8, 14, 18, 22, 23),
+    (13, 14, 8, 4, 20, 5, 10, 15, 16, 21, 22),
+    (12, 15, 9, 5, 21, 4, 17),
+    (15, 12, 10, 6, 22, 11, 21, 23),
+    (14, 13, 11, 7, 23, 4, 6, 12, 20, 22),
+    (17, 18, 20, 8, 24, 12, 22, 25),
+    (16, 19, 21, 9, 25, 0, 2, 8, 13, 26),
+    (19, 16, 22, 10, 26, 8, 11, 27),
+    (18, 17, 23, 11, 27, 10, 26, 30),
+    (21, 22, 16, 12, 28, 4, 9, 15, 29),
+    (20, 23, 17, 13, 29, 9, 12, 14, 28, 31),
+    (23, 20, 18, 14, 30, 11, 12, 15, 16, 27),
+    (22, 21, 19, 15, 31, 11, 14, 30),
+    (25, 26, 28, 16, 27, 29),
+    (24, 27, 29, 17, 8, 16, 26, 28, 30),
+    (27, 24, 30, 18, 10, 17, 19, 25, 31),
+    (26, 25, 31, 19, 18, 22, 24, 28),
+    (29, 30, 24, 20, 21, 25, 27, 31),
+    (28, 31, 25, 21, 20, 24, 30),
+    (31, 28, 26, 22, 19, 23, 25, 29),
+    (30, 29, 27, 23, 21, 26, 28),
+)
+NEAR = (4, 4, 4, 4, 4, 4, 4, 4, 5, 5, 5, 5, 5, 5, 5, 5, 5, 5, 5, 5, 5, 5, 5, 5, 4, 4, 4, 4, 4, 4, 4, 4)
+NEWS = (
+    (8, 8, 12),
+    (4, 9, 11),
+    (5, 7, 14),
+    (2, 8, 12),
+    (4, 10, 12),
+    (5, 9, 15),
+    (8, 12, 15),
+    (0, 4, 6),
+    (2, 6, 12),
+    (2, 6, 7),
+    (8, 11, 13),
+    (3, 9, 14),
+    (3, 5, 11),
+    (6, 10, 11),
+    (2, 3, 10),
+    (6, 6, 12),
+    (1, 3, 4),
+    (0, 0, 7),
+    (4, 7, 10),
+    (0, 5, 7),
+    (0, 0, 4),
+    (1, 2, 12),
+    (1, 7, 11),
+    (3, 8, 10),
+    (5, 7, 10),
+    (5, 9, 15),
+    (4, 8, 13),
+    (4, 10, 11),
+    (1, 4, 12),
+    (5, 9, 11),
+    (0, 5, 9),
+    (6, 10, 10),
+)
+PLANS = {(8, 4): (TILES, ROUTES, STEPS, PARTNERS, NEAR, NEWS)}
 
 
 KIDS = 4
@@ -401,10 +470,10 @@
 
 def table_kernel(
     n_virt, n_aux, occ, plan,
-    x_ref, occ_ref, virt_ref,
+    x_ref, occ_hbm, virt_hbm,
     done_ref,
-    held, lhs, rhs, order, order_t, ints, sums, message, slots,
-    own_sem, send_sem, recv_sem, msg_send, msg_recv,
+    held, lhs, rhs, order, order_t, ints, sums, message, slots, occ_ref, virt_ref,
+    own_sem, eps_sem, send_sem, recv_sem, msg_send, msg_recv, news_sem,
 ):
     rows, cols = x_ref.shape
     pitch = -(-rows // 16) * 16
@@ -415,7 +484,8 @@
     v = lax.axis_index("virt")
     p = lax.axis_index("aux")
     me = v * n_aux + p
-    tiles, routes, steps = plan
+    tiles, routes, steps, partners, n_near, news = plan
+    rounds = len(news[0]) + 1
     half = -(-rows // 32) * 16
     cuts = ((0, half), (half, rows - half))
     n_slots = 2 * n_aux
@@ -424,12 +494,6 @@
         return {"virt": lax.div(t, n_aux), "aux": lax.rem(t, n_aux)}
 
     barrier = pltpu.get_barrier_semaphore()
-
-    def greet(k, c):
-        t = me + k
-        t = jnp.where(t >= n, t - n, t)
-        pl.semaphore_signal(barrier, inc=1, device_id=device(t), device_id_type=MESH)
-        return c
 
     side_a = pick([t[0] for t in tiles], me)
     side_b = pick([t[1] for t in tiles], me)
@@ -437,7 +501,12 @@
     own_slot = jnp.where(side_a == v, p, jnp.where(side_b == v, n_aux + p, n_slots))
     own = pltpu.make_async_copy(x_ref, held.at[own_slot], own_sem)
     own.start()
-    lax.fori_loop(1, n, greet, 0)
+    eps = (
+        pltpu.make_async_copy(occ_hbm, occ_ref, eps_sem.at[0]),
+        pltpu.make_async_copy(virt_hbm, virt_ref, eps_sem.at[1]),
+    )
+    for copy in eps:
+        copy.start()
 
     def packed(codes):
         got = 0
@@ -445,7 +514,27 @@
             got = got * CODE + c + 1
         return got
 
+    most = max(len(r) for r in partners)
+    folk = [
+        pick([packed(r[at:at + KIDS]) for r in partners], me) for at in range(0, most, KIDS)
+    ]
+    n_folk = pick([len(r) for r in partners], me)
+    near = pick(n_near, me)
+
+    def signal(sem, amount, limit):
+        code = None
+        for k in range(amount):
+            code = folk[k // KIDS] if k % KIDS == 0 else lax.div(code, CODE)
+
+            @pl.when(k < limit)
+            def _():
+                t = lax.rem(code, CODE) - 1
+                pl.semaphore_signal(sem, inc=1, device_id=device(t), device_id_type=MESH)
+
+    signal(barrier, most, n_folk)
+
     kids = [pick([packed(r[s]) for r in routes], me) for s in range(n_slots + 1)]
+    spread_at = [pick([r[k] for r in news], me) for k in range(rounds - 1)]
     todo = [pick([r[i] for r in steps], me) for i in range(2 * n_slots)]
 
     row = lax.broadcasted_iota(jnp.int32, (cols, cols), 0)
@@ -454,11 +543,8 @@
     order[...] = jnp.where(hit, 1.0, 0.0).astype(BF16)
     hit = row == lax.rem(col, width) * occ + col // width
     order_t[...] = jnp.where(hit, 1.0, 0.0).astype(BF16)
-    lhs[...] = jnp.zeros_like(lhs)
-    rhs[...] = jnp.zeros_like(rhs)
-
     own.wait()
-    pl.semaphore_wait(barrier, n - 1)
+    pl.semaphore_wait(barrier, n_folk)
 
     def piece(slot, part):
         return held.at[slot, pl.ds(cuts[part][0], cuts[part][1])]
@@ -483,8 +569,21 @@
 
     for part in range(2):
         copies(own_slot, part, lambda copy: copy.start())
+    close = max(n_near)
+    signal(news_sem.at[0], close, near)
+    lhs[...] = jnp.zeros_like(lhs)
+    rhs[...] = jnp.zeros_like(rhs)
+    for copy in eps:
+        copy.wait()
 
     def take(i, c):
+        for r in range(1, rounds):
+
+            @pl.when(i == spread_at[r - 1])
+            def _():
+                pl.semaphore_wait(news_sem.at[r - 1], near)
+                signal(news_sem.at[r], close, near)
+
         entry = pick(todo, i)
         slot = lax.div(entry, 2)
         later = lax.rem(entry, 2)
@@ -620,6 +719,7 @@
         return c
 
     lax.fori_loop(0, n_tiles, tile, 0)
+    pl.semaphore_wait(news_sem.at[rounds - 1], near)
 
     def tell(k, c):
         t = me + k
@@ -666,11 +766,11 @@
     n = n_virt * n_aux
     n_slots = 2 * n_aux
     vmem = pl.BlockSpec(memory_space=pltpu.VMEM)
-    smem = pl.BlockSpec(memory_space=pltpu.SMEM)
+    hbm = pl.BlockSpec(memory_space=pltpu.HBM)
     return pl.pallas_call(
         functools.partial(table_kernel, n_virt, n_aux, occ, plan),
         out_shape=jax.ShapeDtypeStruct((8, LANES), F32),
-        in_specs=[pl.BlockSpec(memory_space=pltpu.HBM), smem, smem],
+        in_specs=[hbm, hbm, hbm],
         out_specs=vmem,
         scratch_shapes=[
             pltpu.VMEM((n_slots + 1, rows, cols), BF16),
@@ -682,11 +782,15 @@
             pltpu.VMEM((occ * 8, cols), F32),
             pltpu.VMEM((8, LANES), F32),
             pltpu.VMEM((n, 8, LANES), F32),
+            pltpu.SMEM(eps_occ.shape, F32),
+            pltpu.SMEM(eps_virt.shape, F32),
             pltpu.SemaphoreType.DMA,
+            pltpu.SemaphoreType.DMA((2,)),
             pltpu.SemaphoreType.DMA((n_slots + 1, 2, KIDS)),
             pltpu.SemaphoreType.DMA((n_slots, 2)),
             pltpu.SemaphoreType.DMA,
             pltpu.SemaphoreType.DMA,
+            pltpu.SemaphoreType.REGULAR((len(plan[5][0]) + 1,)),
         ],
         compiler_params=pltpu.CompilerParams(collective_id=0, has_side_effects=True),
     )(three_index, eps_occ, eps_virt)

time: 36 us -> 33.3 us (0.925)
  Pallas kernels: 35.2 us -> 32.5 us
    pallas_call x1, Pallas kernels: 33.8 us -> 31.1 us  [table_call(): pl.pallas_call(functools.partial(table_kernel, n_virt, n_aux, occ, plan),...]
where the time goes in v2:
time: 33.3 us; the launch traced here: 33.1 us
  Pallas kernels  32.5 us (98%)
  between operations  0.64 us (2%)
    pallas_call x1, Pallas kernels, table_call(): pl.pallas_call(functools.partial(table_kernel, n_virt, n_aux, occ, plan),...  31.1 us
    pallas_call x1, Pallas kernels, on_device(): pl.pallas_call(functools.partial(unpack, occ, width), out_shape=(jax.Shap...  1.42 us

profile of v2, /device:TPU:0, one launch (start us, length us, event | category | flops | bytes accessed | tf_op | source)
XLA Modules:
  0.0 33.1 jit_solution(10566151053508664566)
XLA Ops:
  0.6 31.1 %shard_map.50.done_ref = f32[8,128]{1,0:T(8,128)} custom-call(bf16[150,640]{1,0:T(8,128)(2,1)} %x_ref.1, f32[20]{0:T(128)} %occ_hbm.1, f32[256]{0:T(256)} %virt_hbm.1), custom_call_target="tpu_custom_call" | custom-call | tf_op jit(solution)/shard_map/pallas_call | solution.py:770
  31.7 1.4 %shard_map.51 = (f32[32]{0:T(128)}, f32[20,20]{1,0:T(8,128)}) custom-call(f32[8,128]{1,0:T(8,128)} %shard_map.50.done_ref), custom_call_target="tpu_custom_call" | custom-call | tf_op jit(solution)/shard_map/pallas_call | solution.py:848

commit v3 on v2

--- a/solution.py
+++ b/solution.py
@@ -359,38 +359,38 @@
     ((52,), (), (43,), (47, 52, 58), (61,), (), (57,), (61,), ()),
 )
 STEPS = (
-    (0, 1, 2, 3, 6, 8, 7, 9, 10, 12, 4, 11, 14, 13, 5, 15),
-    (2, 3, 0, 1, 8, 10, 9, 12, 11, 13, 4, 6, 14, 5, 7, 15),
-    (4, 5, 6, 7, 8, 12, 9, 14, 10, 13, 11, 2, 15, 3, 0, 1),
-    (4, 12, 6, 13, 5, 14, 7, 15, 2, 10, 3, 11, 0, 8, 1, 9),
-    (0, 1, 2, 3, 8, 6, 10, 9, 7, 14, 11, 15, 4, 12, 5, 13),
-    (0, 8, 4, 1, 9, 5, 2, 3, 10, 6, 12, 14, 7, 13, 11, 15),
-    (4, 5, 6, 7, 2, 12, 3, 13, 0, 14, 1, 15, 8, 10, 9, 11),
-    (12, 13, 4, 14, 5, 15, 6, 8, 10, 7, 11, 9, 0, 2, 1, 3),
-    (2, 3, 4, 12, 5, 6, 8, 13, 7, 10, 9, 11, 14, 0, 15, 1),
-    (4, 8, 2, 5, 9, 3, 6, 14, 7, 12, 0, 10, 15, 1, 11, 13),
-    (4, 5, 6, 7, 2, 12, 3, 13, 14, 15, 0, 1, 10, 11, 8, 9),
-    (6, 7, 12, 2, 14, 0, 3, 15, 1, 13, 4, 8, 5, 9, 10, 11),
-    (0, 8, 1, 9, 4, 10, 2, 5, 11, 3, 12, 14, 6, 13, 15, 7),
-    (2, 3, 0, 1, 6, 7, 8, 4, 10, 9, 11, 12, 14, 5, 13, 15),
-    (4, 5, 6, 10, 7, 11, 2, 14, 0, 15, 8, 1, 12, 9, 3, 13),
-    (6, 7, 4, 5, 2, 3, 12, 10, 8, 11, 14, 9, 0, 15, 1, 13),
-    (10, 11, 8, 9, 0, 14, 2, 12, 6, 15, 3, 13, 7, 4, 1, 5),
-    (0, 2, 10, 6, 3, 11, 7, 8, 1, 14, 12, 15, 4, 13, 5, 9),
-    (6, 14, 0, 7, 15, 1, 10, 11, 2, 8, 4, 3, 12, 5, 9, 13),
-    (6, 0, 7, 1, 14, 2, 15, 4, 3, 12, 10, 8, 5, 13, 11, 9),
-    (2, 10, 3, 11, 8, 0, 1, 6, 12, 4, 14, 9, 7, 13, 5, 15),
-    (10, 11, 8, 12, 9, 2, 0, 13, 3, 1, 14, 6, 4, 15, 7, 5),
-    (0, 6, 1, 4, 7, 2, 12, 3, 13, 14, 15, 8, 10, 9, 5, 11),
-    (6, 14, 7, 15, 0, 1, 4, 10, 2, 11, 12, 3, 8, 13, 5, 9),
-    (0, 1, 2, 3, 10, 11, 4, 8, 5, 9, 14, 6, 12, 15, 7, 13),
-    (2, 3, 0, 1, 4, 5, 8, 14, 9, 15, 10, 6, 12, 11, 7, 13),
-    (14, 4, 10, 15, 5, 11, 6, 12, 0, 2, 13, 1, 7, 8, 3, 9),
-    (6, 7, 4, 5, 10, 0, 12, 11, 1, 13, 14, 8, 15, 9, 2, 3),
-    (0, 6, 1, 7, 8, 2, 4, 10, 9, 5, 11, 3, 12, 14, 13, 15),
-    (2, 3, 0, 1, 10, 8, 11, 6, 9, 7, 14, 4, 12, 5, 15, 13),
-    (12, 14, 13, 6, 10, 2, 15, 3, 11, 8, 7, 4, 9, 0, 5, 1),
-    (6, 7, 4, 5, 14, 0, 1, 12, 15, 13, 8, 10, 9, 11, 2, 3),
+    (0, 17, 2, 19, 6, 8, 23, 25, 10, 12, 4, 27, 14, 29, 21, 31),
+    (2, 3, 0, 1, 8, 10, 25, 12, 27, 13, 4, 6, 14, 21, 7, 31),
+    (4, 5, 6, 7, 8, 12, 9, 14, 10, 29, 11, 2, 31, 19, 0, 17),
+    (4, 12, 6, 13, 21, 14, 7, 31, 2, 10, 3, 27, 0, 8, 1, 25),
+    (0, 1, 2, 3, 8, 6, 10, 25, 7, 14, 27, 31, 4, 12, 5, 29),
+    (0, 8, 4, 1, 25, 5, 2, 3, 10, 6, 12, 14, 7, 29, 27, 31),
+    (4, 21, 6, 23, 2, 12, 19, 29, 0, 14, 17, 31, 8, 10, 25, 27),
+    (12, 13, 4, 14, 21, 15, 6, 8, 10, 23, 11, 9, 0, 2, 17, 19),
+    (2, 3, 4, 12, 5, 6, 8, 29, 7, 10, 9, 27, 14, 0, 31, 17),
+    (4, 8, 2, 5, 9, 3, 6, 14, 7, 12, 0, 10, 31, 17, 27, 29),
+    (4, 5, 6, 7, 2, 12, 3, 29, 14, 31, 0, 1, 10, 27, 8, 25),
+    (6, 7, 12, 2, 14, 0, 3, 31, 1, 13, 4, 8, 21, 25, 10, 27),
+    (0, 8, 1, 25, 4, 10, 2, 5, 11, 19, 12, 14, 6, 29, 15, 23),
+    (2, 3, 0, 1, 6, 7, 8, 4, 10, 25, 27, 12, 14, 5, 29, 31),
+    (4, 5, 6, 10, 7, 11, 2, 14, 0, 31, 8, 1, 12, 25, 19, 29),
+    (6, 7, 4, 5, 2, 3, 12, 10, 8, 27, 14, 9, 0, 31, 17, 29),
+    (10, 11, 8, 9, 0, 14, 2, 12, 6, 15, 19, 13, 23, 4, 17, 21),
+    (0, 2, 10, 6, 3, 27, 7, 8, 1, 14, 12, 31, 4, 13, 21, 25),
+    (6, 14, 0, 7, 31, 1, 10, 11, 2, 8, 4, 19, 12, 5, 25, 29),
+    (6, 0, 7, 1, 14, 2, 31, 4, 3, 12, 10, 8, 5, 29, 27, 25),
+    (2, 10, 3, 27, 8, 0, 1, 6, 12, 4, 14, 25, 7, 13, 21, 31),
+    (10, 11, 8, 12, 9, 2, 0, 13, 19, 17, 14, 6, 4, 15, 23, 21),
+    (0, 6, 1, 4, 7, 2, 12, 3, 13, 14, 31, 8, 10, 25, 21, 27),
+    (6, 14, 7, 31, 0, 1, 4, 10, 2, 11, 12, 19, 8, 13, 21, 25),
+    (0, 1, 2, 3, 10, 27, 4, 8, 5, 25, 14, 6, 12, 15, 23, 29),
+    (2, 3, 0, 1, 4, 5, 8, 14, 25, 15, 10, 6, 12, 27, 23, 29),
+    (14, 4, 10, 15, 5, 11, 6, 12, 0, 2, 29, 1, 23, 8, 19, 25),
+    (6, 23, 4, 21, 10, 0, 12, 27, 17, 29, 14, 8, 31, 25, 2, 19),
+    (0, 6, 1, 7, 8, 2, 4, 10, 25, 5, 11, 19, 12, 14, 29, 31),
+    (2, 3, 0, 1, 10, 8, 27, 6, 25, 7, 14, 4, 12, 5, 31, 29),
+    (12, 14, 13, 6, 10, 2, 15, 3, 27, 8, 23, 4, 9, 0, 21, 17),
+    (6, 23, 4, 21, 14, 0, 17, 12, 31, 29, 8, 10, 25, 27, 2, 19),
 )
 PARTNERS = (
     (1, 2, 4, 8, 3, 5, 17),
@@ -472,11 +472,11 @@
     n_virt, n_aux, occ, plan,
     x_ref, occ_hbm, virt_hbm,
     done_ref,
-    held, lhs, rhs, order, order_t, ints, sums, message, slots, occ_ref, virt_ref,
+    held, lhs, rhs, order, order_t, ints, over, sums, message, slots, occ_ref, virt_ref,
     own_sem, eps_sem, send_sem, recv_sem, msg_send, msg_recv, news_sem,
 ):
     rows, cols = x_ref.shape
-    pitch = -(-rows // 16) * 16
+    deep = lhs.shape[2]
     width = cols // occ
     groups = LANES // width
     supers = occ // groups
@@ -571,55 +571,18 @@
         copies(own_slot, part, lambda copy: copy.start())
     close = max(n_near)
     signal(news_sem.at[0], close, near)
-    lhs[...] = jnp.zeros_like(lhs)
-    rhs[...] = jnp.zeros_like(rhs)
+    whole_rows = rows // 16 * 16
+    whole_lanes = rows // LANES * LANES
+    lhs[:, :, whole_lanes:] = jnp.zeros((n_slots, cols, deep - whole_lanes), BF16)
+    rhs[:, whole_rows:, :] = jnp.zeros((n_slots, deep - whole_rows, cols), BF16)
     for copy in eps:
         copy.wait()
-
-    def take(i, c):
-        for r in range(1, rounds):
-
-            @pl.when(i == spread_at[r - 1])
-            def _():
-                pl.semaphore_wait(news_sem.at[r - 1], near)
-                signal(news_sem.at[r], close, near)
-
-        entry = pick(todo, i)
-        slot = lax.div(entry, 2)
-        later = lax.rem(entry, 2)
-        away = slot != own_slot
-        for part in range(2):
-
-            @pl.when(jnp.logical_and(later == part, away))
-            def _():
-                whole = piece(slot, part)
-                pltpu.make_async_copy(whole, whole, recv_sem.at[slot, part]).wait()
-                copies(slot, part, lambda copy: copy.start())
-
-        side = lax.div(slot, n_aux)
-        for q in range(n_aux):
-            here = jnp.logical_and(later == 1, lax.rem(slot, n_aux) == q)
-
-            @pl.when(jnp.logical_and(here, jnp.logical_or(side == 0, diag)))
-            def _():
-                lhs[side, :, q * pitch:q * pitch + rows] = lax.dot_general(
-                    order[...], held[slot], NT, preferred_element_type=F32
-                ).astype(BF16)
-
-            @pl.when(jnp.logical_and(here, jnp.logical_or(side == 1, diag)))
-            def _():
-                rhs[side, q * pitch:q * pitch + rows, :] = lax.dot_general(
-                    held[slot], order_t[...], NN, preferred_element_type=F32
-                ).astype(BF16)
-
-        return c
-
-    lax.fori_loop(0, 2 * n_slots, take, 0)
 
     lane = lax.broadcasted_iota(jnp.int32, (1, LANES), 1)
     part = lane // width
     down = lax.broadcasted_iota(jnp.int32, (width, 1), 0)
     lane_in = lax.rem(lane, width)
+    n_tiles = jnp.where(diag, 2, 1)
 
     def eps_down(which):
         got = jnp.zeros((width, 1), F32)
@@ -640,65 +603,130 @@
             got = jnp.where(part == t, occ_ref[cj * groups + t], got)
         occ_lane.append(got)
 
-    tall = -(-occ // 8)
+    def prepare(t, c):
+        block_l = jnp.where(t == 0, side_a, side_b)
+        block_r = jnp.where(jnp.logical_and(diag, t == 0), side_a, side_b)
+        base = -(eps_down(block_l) + eps_across(block_r))
+        ints[t] = jnp.zeros((cols, cols), F32)
+        for i in range(occ):
+            for cj in range(i // groups, supers):
+                below = base + (occ_lane[cj] + occ_ref[i])
+                over[t, i * width:(i + 1) * width, cj * LANES:(cj + 1) * LANES] = (
+                    (1.0 if cj == i // groups else 2.0) / below
+                )
+        return c
+
+    lax.fori_loop(0, n_tiles, prepare, 0)
+
+    def take(i, c):
+        for r in range(1, rounds):
+
+            @pl.when(i == spread_at[r - 1])
+            def _():
+                pl.semaphore_wait(news_sem.at[r - 1], near)
+                signal(news_sem.at[r], close, near)
+
+        entry = pick(todo, i)
+        slot = lax.rem(lax.div(entry, 2), n_slots)
+        meets = lax.div(entry, 4 * n_aux) == 1
+        later = lax.rem(entry, 2)
+        away = slot != own_slot
+        for part in range(2):
+
+            @pl.when(jnp.logical_and(later == part, away))
+            def _():
+                whole = piece(slot, part)
+                pltpu.make_async_copy(whole, whole, recv_sem.at[slot, part]).wait()
+                copies(slot, part, lambda copy: copy.start())
+
+        side = lax.div(slot, n_aux)
+        mine = jnp.where(diag, side, 0)
+        left = jnp.where(diag, slot, lax.rem(slot, n_aux))
+        right = jnp.where(diag, slot, n_aux + lax.rem(slot, n_aux))
+
+        @pl.when(jnp.logical_and(later == 1, jnp.logical_or(side == 0, diag)))
+        def _():
+            lhs[slot, :, 0:rows] = lax.dot_general(
+                order[...], held[slot], NT, preferred_element_type=F32
+            ).astype(BF16)
+
+        @pl.when(jnp.logical_and(later == 1, jnp.logical_or(side == 1, diag)))
+        def _():
+            rhs[slot, 0:rows, :] = lax.dot_general(
+                held[slot], order_t[...], NN, preferred_element_type=F32
+            ).astype(BF16)
+
+        @pl.when(meets)
+        def _():
+            ints[mine] += lax.dot_general(lhs[left], rhs[right], NN, preferred_element_type=F32)
+
+        return c
+
+    lax.fori_loop(0, 2 * n_slots, take, 0)
+
+    tall = -(-occ // 4)
     sums[...] = jnp.zeros_like(sums)
-    n_tiles = jnp.where(diag, 2, 1)
     r8 = lax.broadcasted_iota(jnp.int32, (8, LANES), 0)
     l8 = lax.broadcasted_iota(jnp.int32, (8, LANES), 1)
-    free = tall * width
+    wide = lax.broadcasted_iota(jnp.int32, (cols, LANES), 0)
+    thin = lax.broadcasted_iota(jnp.int32, (cols, LANES), 1)
+    fold = jnp.where(wide // width == thin, 1.0, 0.0).astype(BF16)
+    ri = lax.broadcasted_iota(jnp.int32, (tall * 8, occ * 8), 0)
+    rj = lax.broadcasted_iota(jnp.int32, (tall * 8, occ * 8), 1)
+    gather = jnp.logical_and(lax.rem(ri, 8) < 4, rj // 8 == ri // 8 * 4 + lax.rem(ri, 8))
+    gather = jnp.where(gather, 1.0, 0.0).astype(BF16)
+    ones = jnp.ones((8, LANES), BF16)
+    free = tall * occ
+
+    def split(x):
+        high = x.astype(BF16)
+        return high, (x - high.astype(F32)).astype(BF16)
 
     def tile(t, c):
-        left = t
-        right = jnp.where(diag, t, 1)
-        ints[...] = lax.dot_general(lhs[left], rhs[right], NN, preferred_element_type=F32)
-        block_l = jnp.where(left == 0, side_a, side_b)
-        block_r = jnp.where(right == 0, side_a, side_b)
-        base = -(eps_down(block_l) + eps_across(block_r))
         total = jnp.zeros((width, LANES), F32)
         for ci in range(supers):
             for cj in range(ci, supers):
                 turned = []
                 for g in range(groups):
-                    block = ints[pl.ds((cj * groups + g) * width, width), pl.ds(ci * LANES, LANES)]
+                    block = ints[t, pl.ds((cj * groups + g) * width, width), pl.ds(ci * LANES, LANES)]
                     turned.append([block if r == 0 else pltpu.roll(block, r * width, 1) for r in range(groups)])
                 for s in range(groups):
                     i = ci * groups + s
-                    direct = ints[pl.ds(i * width, width), pl.ds(cj * LANES, LANES)]
+                    direct = ints[t, pl.ds(i * width, width), pl.ds(cj * LANES, LANES)]
+                    inverse = over[t, pl.ds(i * width, width), pl.ds(cj * LANES, LANES)]
                     swapped = turned[0][(0 - s) % groups]
                     for g in range(1, groups):
                         swapped = jnp.where(part == g, turned[g][(g - s) % groups], swapped)
-                    below = base + (occ_lane[cj] + occ_ref[i])
                     if ci == cj:
-                        term = direct * (2.0 * direct - swapped) / below
+                        term = direct * (2.0 * direct - swapped) * inverse
                     else:
-                        term = 2.0 * (direct * (direct - swapped) + swapped * swapped) / below
+                        term = (direct * (direct - swapped) + swapped * swapped) * inverse
                     total = total + term
                     short = term[0:8]
                     for m in range(8, width, 8):
                         short = short + term[m:m + 8]
                     sums[i * 8:i * 8 + 8, cj * LANES:(cj + 1) * LANES] = short
 
-        wide = lax.broadcasted_iota(jnp.int32, (cols, LANES), 0)
-        thin = lax.broadcasted_iota(jnp.int32, (cols, LANES), 1)
-        fold = jnp.where(wide // width == thin, 1.0, 0.0)
-        by_j = lax.dot_general(sums[...], fold, NN, precision=EXACT, preferred_element_type=F32)
-        ri = lax.broadcasted_iota(jnp.int32, (tall * 8, occ * 8), 0)
-        rj = lax.broadcasted_iota(jnp.int32, (tall * 8, occ * 8), 1)
-        by_ij = lax.dot_general(
-            jnp.where(rj // 8 == ri, 1.0, 0.0), by_j, NN,
-            precision=EXACT, preferred_element_type=F32,
-        )
+        rows_of = [
+            lax.dot_general(gather, x, NN, preferred_element_type=F32) for x in split(sums[...])
+        ]
+        pairs_of = [
+            lax.dot_general(x, fold, NN, preferred_element_type=F32)
+            for x in split(rows_of[0] + rows_of[1])
+        ]
+        by_ij = pairs_of[0] + pairs_of[1]
         packed_ij = by_ij[0:8]
         for g in range(1, tall):
-            packed_ij = packed_ij + pltpu.roll(by_ij[g * 8:g * 8 + 8], g * width, 1)
-        pads = [jnp.zeros((free, LANES), F32), total]
-        if free + width < LANES:
-            pads.append(jnp.zeros((LANES - free - width, LANES), F32))
-        spread = jnp.concatenate(pads, 0)
-        by_row = lax.dot_general(
-            jnp.ones((8, LANES), F32), spread, NT, precision=EXACT, preferred_element_type=F32)
-        by_col = lax.dot_general(
-            jnp.ones((8, width), F32), total, NN, precision=EXACT, preferred_element_type=F32)
+            packed_ij = packed_ij + pltpu.roll(by_ij[g * 8:g * 8 + 8], g * occ, 1)
+        spread = jnp.concatenate([jnp.zeros((LANES - width, LANES), F32), total], 0)
+        by_row = [
+            lax.dot_general(ones, x, NT, preferred_element_type=F32) for x in split(spread)
+        ]
+        by_row = by_row[0] + by_row[1]
+        by_col = [
+            lax.dot_general(ones[:, :width], x, NN, preferred_element_type=F32) for x in split(total)
+        ]
+        by_col = by_col[0] + by_col[1]
         folded = by_col
         for g in range(1, groups):
             folded = folded + pltpu.roll(by_col, g * width, 1)
@@ -706,7 +734,14 @@
         both = (by_row + folded) * 0.5
         first = jnp.where(diag, jnp.where(t == 0, both, 0.0), by_row)
         second = jnp.where(diag, jnp.where(t == 1, both, 0.0), folded)
-        out = jnp.where(l8 < free, packed_ij, jnp.where(r8 == 0, first, jnp.where(r8 == 1, second, 0.0)))
+        near_turn = free - (LANES - width)
+        far_turn = near_turn - width // 2
+        shares = jnp.where(r8 == 3, pltpu.roll(second, far_turn % LANES, 1), 0.0)
+        shares = jnp.where(r8 == 2, pltpu.roll(second, near_turn % LANES, 1), shares)
+        shares = jnp.where(r8 == 1, pltpu.roll(first, far_turn % LANES, 1), shares)
+        shares = jnp.where(r8 == 0, pltpu.roll(first, near_turn % LANES, 1), shares)
+        shares = jnp.where(l8 < free + width // 2, shares, 0.0)
+        out = jnp.where(l8 < free, packed_ij, shares)[0:4]
 
         @pl.when(t == 0)
         def _():
@@ -749,39 +784,57 @@
     pltpu.make_async_copy(everyone, everyone, msg_send).wait()
     pltpu.make_async_copy(everyone, everyone, msg_recv).wait()
 
-    keep = l8 < free
+    keep = l8[0:4] < free
+    upper = r8[0:4] < 2
     acc = None
     for k in range(n):
         a, b, _ = tiles[k]
         row0 = jnp.where(v == a, 1.0, 0.0)
         row1 = jnp.where(v == b, 1.0, 0.0)
-        term = slots[k] * jnp.where(keep, 1.0, jnp.where(r8 == 0, row0, row1))
+        term = slots[k] * jnp.where(keep, 1.0, jnp.where(upper, row0, row1))
         acc = term if acc is None else acc + term
     done_ref[...] = acc
 
 
+def table_unpack(occ, width, done_ref, share_ref, pair_ref):
+    tall = -(-occ // 4)
+    free = tall * occ
+    done = done_ref[...]
+    share = done[0:2] + done[2:4]
+    share_ref[...] = jnp.concatenate(
+        [share[0, free:free + width // 2], share[1, free:free + width // 2]], 0
+    )
+    blocks = [done] + [pltpu.roll(done, LANES - g * occ, 1) for g in range(1, tall)]
+    square = jnp.concatenate(blocks + [jnp.zeros((LANES - 4 * tall, LANES), F32)], 0)
+    square = jnp.where(lax.broadcasted_iota(jnp.int32, (LANES, LANES), 1) < occ, square, 0.0)
+    pair = square + square.T
+    pair_ref[...] = pair[0:occ, 0:occ]
+
+
 def table_call(n_virt, n_aux, occ, plan, three_index, eps_occ, eps_virt):
     rows, cols = three_index.shape
-    pitch = -(-rows // 16) * 16
+    width = cols // occ
+    deep = -(-rows // LANES) * LANES
     n = n_virt * n_aux
     n_slots = 2 * n_aux
     vmem = pl.BlockSpec(memory_space=pltpu.VMEM)
     hbm = pl.BlockSpec(memory_space=pltpu.HBM)
-    return pl.pallas_call(
+    done = pl.pallas_call(
         functools.partial(table_kernel, n_virt, n_aux, occ, plan),
-        out_shape=jax.ShapeDtypeStruct((8, LANES), F32),
+        out_shape=pltpu.VMEM((4, LANES), F32),
         in_specs=[hbm, hbm, hbm],
         out_specs=vmem,
         scratch_shapes=[
             pltpu.VMEM((n_slots + 1, rows, cols), BF16),
-            pltpu.VMEM((2, cols, n_aux * pitch), BF16),
-            pltpu.VMEM((2, n_aux * pitch, cols), BF16),
+            pltpu.VMEM((n_slots, cols, deep), BF16),
+            pltpu.VMEM((n_slots, deep, cols), BF16),
             pltpu.VMEM((cols, cols), BF16),
             pltpu.VMEM((cols, cols), BF16),
-            pltpu.VMEM((cols, cols), F32),
+            pltpu.VMEM((2, cols, cols), F32),
+            pltpu.VMEM((2, cols, cols), F32),
             pltpu.VMEM((occ * 8, cols), F32),
-            pltpu.VMEM((8, LANES), F32),
-            pltpu.VMEM((n, 8, LANES), F32),
+            pltpu.VMEM((4, LANES), F32),
+            pltpu.VMEM((n, 4, LANES), F32),
             pltpu.SMEM(eps_occ.shape, F32),
             pltpu.SMEM(eps_virt.shape, F32),
             pltpu.SemaphoreType.DMA,
@@ -794,6 +847,15 @@
         ],
         compiler_params=pltpu.CompilerParams(collective_id=0, has_side_effects=True),
     )(three_index, eps_occ, eps_virt)
+    return pl.pallas_call(
+        functools.partial(table_unpack, occ, width),
+        out_shape=(
+            jax.ShapeDtypeStruct((width,), F32),
+            jax.ShapeDtypeStruct((occ, occ), F32),
+        ),
+        in_specs=[vmem],
+        out_specs=(vmem, vmem),
+    )(pltpu.with_memory_space_constraint(done, pltpu.VMEM))
 
 
 def unpack(occ, width, done_ref, share_ref, pair_ref):
@@ -819,32 +881,31 @@
     smem = pl.BlockSpec(memory_space=pltpu.SMEM)
     plan = PLANS.get((n_virt, n_aux))
     if plan is not None:
-        done = table_call(n_virt, n_aux, occ, plan, three_index, eps_occ, eps_virt)
-    else:
-        done = pl.pallas_call(
-            functools.partial(kernel, n_virt, n_aux, occ),
-            out_shape=jax.ShapeDtypeStruct((8, LANES), F32),
-            in_specs=[vmem, smem, smem],
-            out_specs=vmem,
-            scratch_shapes=[
-                pltpu.VMEM((2, n_aux, rows, cols), BF16),
-                pltpu.VMEM((cols, n_aux * pitch), BF16),
-                pltpu.VMEM((n_aux * pitch, cols), BF16),
-                pltpu.VMEM((cols, cols), BF16),
-                pltpu.VMEM((cols, cols), BF16),
-                pltpu.VMEM((cols, cols), F32),
-                pltpu.VMEM((occ * 8, cols), F32),
-                pltpu.VMEM((8, LANES), F32),
-                pltpu.VMEM((8, LANES), F32),
-                pltpu.VMEM((n, 8, LANES), F32),
-                pltpu.SemaphoreType.DMA,
-                pltpu.SemaphoreType.DMA((3, n_aux)),
-                pltpu.SemaphoreType.DMA((2, n_aux)),
-                pltpu.SemaphoreType.DMA,
-                pltpu.SemaphoreType.DMA,
-            ],
-            compiler_params=pltpu.CompilerParams(collective_id=0, has_side_effects=True),
-        )(three_index, eps_occ, eps_virt)
+        return table_call(n_virt, n_aux, occ, plan, three_index, eps_occ, eps_virt)
+    done = pl.pallas_call(
+        functools.partial(kernel, n_virt, n_aux, occ),
+        out_shape=jax.ShapeDtypeStruct((8, LANES), F32),
+        in_specs=[vmem, smem, smem],
+        out_specs=vmem,
+        scratch_shapes=[
+            pltpu.VMEM((2, n_aux, rows, cols), BF16),
+            pltpu.VMEM((cols, n_aux * pitch), BF16),
+            pltpu.VMEM((n_aux * pitch, cols), BF16),
+            pltpu.VMEM((cols, cols), BF16),
+            pltpu.VMEM((cols, cols), BF16),
+            pltpu.VMEM((cols, cols), F32),
+            pltpu.VMEM((occ * 8, cols), F32),
+            pltpu.VMEM((8, LANES), F32),
+            pltpu.VMEM((8, LANES), F32),
+            pltpu.VMEM((n, 8, LANES), F32),
+            pltpu.SemaphoreType.DMA,
+            pltpu.SemaphoreType.DMA((3, n_aux)),
+            pltpu.SemaphoreType.DMA((2, n_aux)),
+            pltpu.SemaphoreType.DMA,
+            pltpu.SemaphoreType.DMA,
+        ],
+        compiler_params=pltpu.CompilerParams(collective_id=0, has_side_effects=True),
+    )(three_index, eps_occ, eps_virt)
     return pl.pallas_call(
         functools.partial(unpack, occ, width),
         out_shape=(

time: 33.3 us -> 32.6 us (0.979)
  Pallas kernels: 32.5 us -> 31.8 us
    pallas_call x1, Pallas kernels: 1.42 us -> 0.74 us  [table_call(): pl.pallas_call(functools.partial(table_unpack, occ, width), out_shape=(ja...]
where the time goes in v3:
time: 32.6 us; the launch traced here: 32.4 us
  Pallas kernels  31.8 us (98%)
  between operations  0.64 us (2%)
    pallas_call x1, Pallas kernels, table_call(): pl.pallas_call(functools.partial(table_kernel, n_virt, n_aux, occ, plan),...  31.1 us
    pallas_call x1, Pallas kernels, table_call(): pl.pallas_call(functools.partial(table_unpack, occ, width), out_shape=(ja...  0.74 us

profile of v3, /device:TPU:0, one launch (start us, length us, event | category | flops | bytes accessed | tf_op | source)
XLA Modules:
  0.0 32.4 jit_solution(1945656499949416965)
XLA Ops:
  0.6 31.1 %shard_map.50.done_ref = f32[4,128]{1,0:T(4,128)S(1)} custom-call(bf16[150,640]{1,0:T(8,128)(2,1)} %x_ref.1, f32[20]{0:T(128)} %occ_hbm.1, f32[256]{0:T(256)} %virt_hbm.1), custom_call_target="tpu_custom_call" | custom-call | tf_op jit(solution)/shard_map/pallas_call | solution.py:822
  31.7 0.7 %shard_map.51 = (f32[32]{0:T(128)}, f32[20,20]{1,0:T(8,128)}) custom-call(f32[4,128]{1,0:T(4,128)S(1)} %shard_map.50.done_ref), custom_call_target="tpu_custom_call" | custom-call | tf_op jit(solution)/shard_map/pallas_call | solution.py:850

commit v4 on v3

--- a/solution.py
+++ b/solution.py
@@ -291,21 +291,21 @@
 
 
 TILES = (
+    (1, 2, 0),
+    (0, 1, 0),
+    (0, 2, 0),
     (0, 2, 1),
-    (0, 2, 0),
-    (0, 1, 0),
-    (1, 2, 0),
+    (2, 3, 0),
     (1, 3, 0),
+    (1, 3, 1),
     (0, 3, 0),
-    (1, 3, 1),
-    (2, 3, 0),
     (0, 4, 0),
     (0, 5, 0),
     (2, 4, 0),
     (2, 5, 0),
     (1, 4, 0),
+    (1, 5, 0),
     (3, 4, 0),
-    (1, 5, 0),
     (3, 5, 0),
     (0, 6, 0),
     (0, 7, 0),
@@ -315,155 +315,156 @@
     (1, 7, 0),
     (3, 6, 0),
     (3, 7, 0),
+    (6, 4, 0),
     (6, 7, 0),
-    (6, 4, 0),
     (7, 4, 0),
     (6, 4, 1),
     (6, 5, 0),
+    (7, 5, 1),
+    (4, 5, 0),
     (7, 5, 0),
-    (4, 5, 0),
-    (7, 5, 1),
 )
 ROUTES = (
-    ((2, 10, 34), (10, 4), (2,), (16, 10), (3,), (), (), (3,), ()),
-    ((4, 18), (0, 16), (), (), (14,), (1,), (1,), (), ()),
-    ((), (), (10, 18), (34,), (), (), (), (), ()),
-    ((), (), (5,), (5,), (), (14,), (3, 14, 22), (1, 14), (0, 4)),
-    ((5, 24, 12), (5, 40, 24), (), (24,), (), (11,), (), (11,), ()),
-    ((), (), (0,), (), (9, 13), (), (), (), (8, 12)),
-    ((28, 6), (6, 28), (6, 28), (28, 8), (15,), (15,), (15, 11), (15,), ()),
-    ((), (), (), (), (), (), (), (), (12, 6)),
-    ((), (18, 34), (32,), (2, 18), (21,), (), (25,), (), (1, 36, 22)),
-    ((16,), (), (16,), (), (23,), (), (), (), (20, 3)),
-    ((), (22, 38, 7), (7, 38), (7,), (), (), (17,), (25,), ()),
-    ((20, 7), (), (), (20, 36), (), (), (31, 19), (19,), ()),
-    ((42,), (), (8, 42), (), (17, 27), (), (27,), (27,), (11, 26, 44, 30)),
-    ((), (30, 9), (), (9,), (), (25,), (), (), ()),
-    ((), (), (24,), (42,), (), (23, 31), (), (31,), (13, 30)),
-    ((), (44, 13), (26, 44, 9), (26, 46, 13), (29,), (), (), (), ()),
-    ((), (), (34,), (), (37, 45), (37, 41), (), (48, 41), (25, 51)),
-    ((32,), (32,), (), (32,), (), (39,), (), (), (53, 27, 51, 17)),
-    ((38,), (), (), (38,), (), (54, 45), (), (33, 45), (21, 55)),
-    ((), (36,), (36,), (), (), (), (), (35,), (53, 21, 55)),
-    ((), (42,), (), (), (), (), (), (), (19, 59, 31)),
-    ((40,), (), (40,), (40,), (47, 35), (35, 47), (58, 35), (), (59, 29, 57, 19)),
-    ((46,), (46,), (46,), (), (), (), (37, 41), (), (23, 61, 29)),
-    ((), (), (), (44,), (), (62,), (), (39,), (63, 23, 29)),
-    ((50, 56, 54), (56,), (), (), (), (52,), (), (), ()),
-    ((33,), (33, 48), (48, 56, 33), (), (55, 60), (), (), (17,), ()),
-    ((39,), (), (49,), (), (), (55, 60, 21), (60,), (51, 60), (50, 54)),
-    ((), (), (45,), (37, 56), (53,), (), (51, 53), (), ()),
-    ((41,), (), (), (50,), (), (), (59,), (), (58, 62, 43)),
-    ((49,), (43, 49), (), (43, 49), (57, 63), (61,), (), (57,), ()),
-    ((), (), (), (), (), (63,), (63,), (59,), (52, 62, 39, 47)),
-    ((52,), (), (43,), (47, 52, 58), (61,), (), (57,), (61,), ()),
+    ((3,), (), (3,), (3,), (8,), (), (8,), (), (2, 14)),
+    ((6, 32), (4, 18), (18,), (), (), (0,), (), (), ()),
+    ((), (6, 14), (6, 14, 32), (), (), (), (), (7,), ()),
+    ((4,), (), (2,), (4, 14, 18), (5,), (5,), (5, 1), (1, 8), ()),
+    ((), (1,), (), (), (11,), (), (), (11,), (0, 10, 24)),
+    ((12,), (3, 12, 42), (), (0, 24), (13,), (9,), (9,), (), ()),
+    ((), (), (0, 24), (40,), (), (15,), (15, 11), (9, 15), ()),
+    ((), (), (), (), (), (), (), (), (10, 12)),
+    ((), (), (), (), (21, 25), (25,), (), (25,), (1, 22)),
+    ((), (16, 34), (16,), (16, 34, 2), (23,), (), (), (), (8, 38, 7)),
+    ((7,), (22,), (7, 22), (5,), (), (29,), (17,), (17, 29), ()),
+    ((20, 36), (), (36,), (20, 38), (), (), (19,), (), ()),
+    ((26, 42), (), (26, 10), (26,), (29,), (), (), (), (9, 30, 46)),
+    ((), (), (42,), (), (19, 31), (19, 31), (), (19,), (11, 30)),
+    ((), (44,), (30, 44), (44,), (), (), (25,), (), ()),
+    ((28, 15), (28, 13), (13,), (13, 28), (), (23,), (23, 27), (23, 27), ()),
+    ((16, 34, 18), (), (34,), (), (37, 41), (37, 41), (), (), (17, 49)),
+    ((), (32,), (), (32,), (39,), (51,), (), (), (17, 53, 21)),
+    ((38,), (20,), (38,), (), (), (45,), (), (45,), (21, 55, 29)),
+    ((), (36,), (), (36,), (), (), (), (), (21, 53, 55)),
+    ((), (), (), (42,), (45,), (), (), (), (27, 59)),
+    ((40,), (24, 40, 26), (40,), (), (35, 47), (35, 47), (), (35,), (27, 59, 57)),
+    ((), (46,), (46,), (46,), (), (), (41,), (41,), (31, 63)),
+    ((44,), (), (), (), (62,), (39,), (39,), (39,), (31, 57, 63)),
+    ((50,), (), (33, 50), (), (55, 60), (), (), (), ()),
+    ((33, 56, 54), (33, 48, 54, 56), (56,), (48, 33, 56), (52,), (), (), (), ()),
+    ((), (), (35,), (), (), (49, 55, 60), (), (60,), (45, 54)),
+    ((), (), (48, 37), (37, 50), (53,), (), (53, 60, 49), (49,), ()),
+    ((), (), (), (), (), (), (), (59,), (58,)),
+    ((51, 43), (43, 62), (43, 51), (51, 43), (57, 61), (63,), (57,), (), ()),
+    ((), (), (), (), (63,), (), (), (), (52, 62)),
+    ((), (52,), (47, 58), (47, 52, 58), (), (61,), (61, 59), (61,), ()),
 )
 STEPS = (
-    (0, 17, 2, 19, 6, 8, 23, 25, 10, 12, 4, 27, 14, 29, 21, 31),
-    (2, 3, 0, 1, 8, 10, 25, 12, 27, 13, 4, 6, 14, 21, 7, 31),
-    (4, 5, 6, 7, 8, 12, 9, 14, 10, 29, 11, 2, 31, 19, 0, 17),
-    (4, 12, 6, 13, 21, 14, 7, 31, 2, 10, 3, 27, 0, 8, 1, 25),
-    (0, 1, 2, 3, 8, 6, 10, 25, 7, 14, 27, 31, 4, 12, 5, 29),
-    (0, 8, 4, 1, 25, 5, 2, 3, 10, 6, 12, 14, 7, 29, 27, 31),
-    (4, 21, 6, 23, 2, 12, 19, 29, 0, 14, 17, 31, 8, 10, 25, 27),
-    (12, 13, 4, 14, 21, 15, 6, 8, 10, 23, 11, 9, 0, 2, 17, 19),
-    (2, 3, 4, 12, 5, 6, 8, 29, 7, 10, 9, 27, 14, 0, 31, 17),
-    (4, 8, 2, 5, 9, 3, 6, 14, 7, 12, 0, 10, 31, 17, 27, 29),
-    (4, 5, 6, 7, 2, 12, 3, 29, 14, 31, 0, 1, 10, 27, 8, 25),
-    (6, 7, 12, 2, 14, 0, 3, 31, 1, 13, 4, 8, 21, 25, 10, 27),
-    (0, 8, 1, 25, 4, 10, 2, 5, 11, 19, 12, 14, 6, 29, 15, 23),
-    (2, 3, 0, 1, 6, 7, 8, 4, 10, 25, 27, 12, 14, 5, 29, 31),
-    (4, 5, 6, 10, 7, 11, 2, 14, 0, 31, 8, 1, 12, 25, 19, 29),
-    (6, 7, 4, 5, 2, 3, 12, 10, 8, 27, 14, 9, 0, 31, 17, 29),
-    (10, 11, 8, 9, 0, 14, 2, 12, 6, 15, 19, 13, 23, 4, 17, 21),
-    (0, 2, 10, 6, 3, 27, 7, 8, 1, 14, 12, 31, 4, 13, 21, 25),
-    (6, 14, 0, 7, 31, 1, 10, 11, 2, 8, 4, 19, 12, 5, 25, 29),
-    (6, 0, 7, 1, 14, 2, 31, 4, 3, 12, 10, 8, 5, 29, 27, 25),
-    (2, 10, 3, 27, 8, 0, 1, 6, 12, 4, 14, 25, 7, 13, 21, 31),
-    (10, 11, 8, 12, 9, 2, 0, 13, 19, 17, 14, 6, 4, 15, 23, 21),
-    (0, 6, 1, 4, 7, 2, 12, 3, 13, 14, 31, 8, 10, 25, 21, 27),
-    (6, 14, 7, 31, 0, 1, 4, 10, 2, 11, 12, 19, 8, 13, 21, 25),
-    (0, 1, 2, 3, 10, 27, 4, 8, 5, 25, 14, 6, 12, 15, 23, 29),
-    (2, 3, 0, 1, 4, 5, 8, 14, 25, 15, 10, 6, 12, 27, 23, 29),
-    (14, 4, 10, 15, 5, 11, 6, 12, 0, 2, 29, 1, 23, 8, 19, 25),
-    (6, 23, 4, 21, 10, 0, 12, 27, 17, 29, 14, 8, 31, 25, 2, 19),
-    (0, 6, 1, 7, 8, 2, 4, 10, 25, 5, 11, 19, 12, 14, 29, 31),
-    (2, 3, 0, 1, 10, 8, 27, 6, 25, 7, 14, 4, 12, 5, 31, 29),
-    (12, 14, 13, 6, 10, 2, 15, 3, 27, 8, 23, 4, 9, 0, 21, 17),
-    (6, 23, 4, 21, 14, 0, 17, 12, 31, 29, 8, 10, 25, 27, 2, 19),
+    (4, 0, 8, 2, 5, 1, 25, 3, 12, 6, 29, 10, 7, 14, 31, 27),
+    (2, 3, 0, 1, 10, 4, 12, 8, 5, 27, 29, 25, 14, 6, 15, 23),
+    (4, 5, 6, 7, 2, 12, 3, 29, 14, 31, 0, 10, 1, 8, 25, 27),
+    (6, 23, 4, 21, 12, 2, 29, 19, 0, 14, 10, 17, 8, 31, 25, 27),
+    (8, 2, 10, 14, 9, 11, 15, 0, 19, 12, 17, 13, 6, 4, 23, 21),
+    (2, 3, 0, 1, 6, 7, 10, 8, 27, 4, 14, 25, 12, 5, 31, 29),
+    (4, 21, 6, 23, 14, 2, 31, 12, 19, 29, 0, 10, 17, 8, 27, 25),
+    (6, 14, 4, 0, 15, 23, 12, 5, 1, 29, 2, 8, 3, 10, 25, 27),
+    (2, 10, 8, 3, 6, 9, 27, 14, 7, 12, 4, 31, 0, 5, 29, 17),
+    (2, 3, 6, 10, 7, 8, 4, 27, 5, 9, 0, 14, 12, 31, 17, 29),
+    (4, 5, 6, 7, 0, 14, 12, 1, 31, 10, 29, 8, 11, 25, 2, 19),
+    (6, 7, 4, 5, 0, 1, 14, 12, 31, 29, 8, 10, 2, 3, 27, 25),
+    (4, 0, 5, 1, 6, 10, 2, 7, 8, 25, 3, 27, 12, 14, 29, 31),
+    (10, 8, 4, 0, 11, 5, 9, 14, 17, 12, 6, 2, 15, 23, 19, 29),
+    (4, 5, 6, 7, 2, 0, 12, 14, 3, 1, 29, 31, 10, 8, 27, 25),
+    (6, 7, 4, 5, 2, 14, 0, 12, 3, 31, 1, 29, 10, 8, 27, 25),
+    (10, 11, 8, 4, 0, 9, 14, 2, 5, 17, 19, 15, 12, 6, 29, 23),
+    (10, 2, 4, 11, 0, 8, 19, 5, 9, 6, 12, 17, 14, 7, 31, 29),
+    (14, 2, 6, 3, 15, 10, 23, 4, 27, 5, 12, 8, 0, 9, 17, 29),
+    (2, 6, 3, 14, 7, 31, 12, 4, 13, 21, 10, 0, 8, 27, 1, 25),
+    (2, 10, 11, 6, 19, 8, 0, 12, 4, 9, 7, 13, 21, 14, 17, 31),
+    (10, 11, 2, 8, 9, 19, 14, 0, 4, 15, 6, 12, 5, 17, 29, 23),
+    (4, 5, 12, 0, 6, 29, 14, 1, 7, 2, 31, 3, 10, 27, 8, 25),
+    (14, 15, 4, 0, 12, 5, 29, 10, 1, 6, 11, 8, 23, 25, 2, 19),
+    (0, 1, 2, 3, 6, 8, 7, 4, 25, 5, 12, 10, 14, 27, 29, 31),
+    (2, 3, 0, 1, 6, 8, 7, 25, 4, 14, 31, 5, 10, 27, 12, 29),
+    (14, 6, 4, 10, 12, 7, 5, 11, 29, 31, 2, 19, 8, 0, 9, 17),
+    (6, 23, 4, 21, 12, 2, 10, 14, 29, 19, 31, 8, 0, 27, 17, 25),
+    (2, 3, 14, 8, 0, 10, 1, 25, 27, 6, 15, 12, 23, 4, 13, 21),
+    (2, 19, 0, 17, 10, 6, 8, 23, 14, 25, 4, 27, 21, 12, 31, 29),
+    (12, 14, 13, 4, 6, 10, 0, 8, 15, 21, 2, 9, 17, 3, 23, 27),
+    (6, 7, 4, 5, 2, 12, 3, 14, 29, 10, 31, 8, 0, 27, 9, 17),
 )
 PARTNERS = (
-    (1, 2, 4, 8, 3, 5, 17),
-    (0, 3, 5, 9, 2, 7, 8),
-    (3, 0, 6, 10, 1, 4, 5, 9, 17),
-    (2, 1, 7, 11, 0, 6, 10),
-    (5, 6, 0, 12, 2, 13, 15, 20),
-    (4, 7, 1, 13, 0, 2, 6, 12),
-    (7, 4, 2, 14, 3, 5, 15),
-    (6, 5, 3, 15, 1),
-    (9, 10, 12, 0, 16, 1, 11, 17, 18, 25),
-    (8, 11, 13, 1, 17, 2, 10, 20, 21),
-    (11, 8, 14, 2, 18, 3, 9, 12, 19, 26),
-    (10, 9, 15, 3, 19, 8, 14, 18, 22, 23),
-    (13, 14, 8, 4, 20, 5, 10, 15, 16, 21, 22),
-    (12, 15, 9, 5, 21, 4, 17),
-    (15, 12, 10, 6, 22, 11, 21, 23),
-    (14, 13, 11, 7, 23, 4, 6, 12, 20, 22),
-    (17, 18, 20, 8, 24, 12, 22, 25),
-    (16, 19, 21, 9, 25, 0, 2, 8, 13, 26),
-    (19, 16, 22, 10, 26, 8, 11, 27),
-    (18, 17, 23, 11, 27, 10, 26, 30),
-    (21, 22, 16, 12, 28, 4, 9, 15, 29),
-    (20, 23, 17, 13, 29, 9, 12, 14, 28, 31),
-    (23, 20, 18, 14, 30, 11, 12, 15, 16, 27),
-    (22, 21, 19, 15, 31, 11, 14, 30),
-    (25, 26, 28, 16, 27, 29),
-    (24, 27, 29, 17, 8, 16, 26, 28, 30),
-    (27, 24, 30, 18, 10, 17, 19, 25, 31),
-    (26, 25, 31, 19, 18, 22, 24, 28),
-    (29, 30, 24, 20, 21, 25, 27, 31),
-    (28, 31, 25, 21, 20, 24, 30),
-    (31, 28, 26, 22, 19, 23, 25, 29),
-    (30, 29, 27, 23, 21, 26, 28),
+    (1, 2, 4, 8, 3, 5, 6, 7),
+    (0, 3, 5, 9, 2, 16),
+    (3, 0, 6, 10, 1, 7, 16),
+    (2, 1, 7, 11, 0, 4, 9, 10),
+    (5, 6, 0, 12, 3, 9),
+    (4, 7, 1, 13, 0, 6, 12, 21),
+    (7, 4, 2, 14, 0, 5, 12, 15, 20),
+    (6, 5, 3, 15, 0, 2),
+    (9, 10, 12, 0, 16, 11, 17),
+    (8, 11, 13, 1, 17, 3, 4, 16, 19),
+    (11, 8, 14, 2, 18, 3, 17, 19),
+    (10, 9, 15, 3, 19, 8, 18),
+    (13, 14, 8, 4, 20, 5, 6, 15, 21, 23),
+    (12, 15, 9, 5, 21, 20),
+    (15, 12, 10, 6, 22, 18),
+    (14, 13, 11, 7, 23, 6, 12, 22),
+    (17, 18, 20, 8, 24, 1, 2, 9, 25),
+    (16, 19, 21, 9, 25, 8, 10, 26),
+    (19, 16, 22, 10, 26, 11, 14, 27),
+    (18, 17, 23, 11, 27, 9, 10, 26),
+    (21, 22, 16, 12, 28, 6, 13, 29),
+    (20, 23, 17, 13, 29, 5, 12, 28),
+    (23, 20, 18, 14, 30, 15, 26, 31),
+    (22, 21, 19, 15, 31, 12, 28),
+    (25, 26, 28, 16, 27, 30),
+    (24, 27, 29, 17, 16, 26, 28),
+    (27, 24, 30, 18, 17, 19, 22, 25, 31),
+    (26, 25, 31, 19, 18, 24, 30),
+    (29, 30, 24, 20, 21, 23, 25),
+    (28, 31, 25, 21, 20, 30),
+    (31, 28, 26, 22, 24, 27, 29),
+    (30, 29, 27, 23, 22, 26),
 )
 NEAR = (4, 4, 4, 4, 4, 4, 4, 4, 5, 5, 5, 5, 5, 5, 5, 5, 5, 5, 5, 5, 5, 5, 5, 5, 4, 4, 4, 4, 4, 4, 4, 4)
 NEWS = (
-    (8, 8, 12),
-    (4, 9, 11),
-    (5, 7, 14),
+    (3, 8, 14),
+    (5, 10, 13),
+    (7, 11, 14),
+    (7, 12, 15),
+    (1, 6, 10),
+    (7, 9, 15),
+    (7, 10, 15),
+    (3, 9, 14),
+    (3, 6, 13),
+    (2, 5, 9),
+    (7, 10, 14),
+    (6, 7, 9),
+    (2, 4, 10),
+    (2, 8, 14),
+    (4, 6, 12),
+    (8, 13, 15),
+    (2, 6, 12),
+    (0, 4, 12),
+    (1, 7, 14),
+    (2, 6, 10),
+    (0, 2, 10),
+    (2, 6, 11),
+    (2, 5, 11),
+    (3, 9, 14),
+    (6, 10, 12),
+    (7, 10, 13),
     (2, 8, 12),
-    (4, 10, 12),
-    (5, 9, 15),
-    (8, 12, 15),
-    (0, 4, 6),
-    (2, 6, 12),
-    (2, 6, 7),
-    (8, 11, 13),
-    (3, 9, 14),
-    (3, 5, 11),
-    (6, 10, 11),
-    (2, 3, 10),
-    (6, 6, 12),
-    (1, 3, 4),
-    (0, 0, 7),
-    (4, 7, 10),
-    (0, 5, 7),
-    (0, 0, 4),
-    (1, 2, 12),
-    (1, 7, 11),
-    (3, 8, 10),
-    (5, 7, 10),
-    (5, 9, 15),
-    (4, 8, 13),
-    (4, 10, 11),
-    (1, 4, 12),
-    (5, 9, 11),
-    (0, 5, 9),
-    (6, 10, 10),
+    (6, 10, 14),
+    (2, 7, 11),
+    (7, 12, 14),
+    (0, 2, 8),
+    (7, 9, 11),
 )
 PLANS = {(8, 4): (TILES, ROUTES, STEPS, PARTNERS, NEAR, NEWS)}
 
 
+TN = (((0,), (0,)), ((), ()))
 KIDS = 4
 CODE = 128
 
@@ -472,11 +473,11 @@
     n_virt, n_aux, occ, plan,
     x_ref, occ_hbm, virt_hbm,
     done_ref,
-    held, lhs, rhs, order, order_t, ints, over, sums, message, slots, occ_ref, virt_ref,
+    raw, held, order, ints, over, sums, message, slots, occ_ref, virt_ref,
     own_sem, eps_sem, send_sem, recv_sem, msg_send, msg_recv, news_sem,
 ):
     rows, cols = x_ref.shape
-    deep = lhs.shape[2]
+    deep = held.shape[1]
     width = cols // occ
     groups = LANES // width
     supers = occ // groups
@@ -487,7 +488,7 @@
     tiles, routes, steps, partners, n_near, news = plan
     rounds = len(news[0]) + 1
     half = -(-rows // 32) * 16
-    cuts = ((0, half), (half, rows - half))
+    cuts = ((0, half), (half, -(-rows // 8) * 8 - half))
     n_slots = 2 * n_aux
 
     def device(t):
@@ -499,7 +500,7 @@
     side_b = pick([t[1] for t in tiles], me)
     diag = pick([t[2] for t in tiles], me) == 1
     own_slot = jnp.where(side_a == v, p, jnp.where(side_b == v, n_aux + p, n_slots))
-    own = pltpu.make_async_copy(x_ref, held.at[own_slot], own_sem)
+    own = pltpu.make_async_copy(x_ref, raw, own_sem)
     own.start()
     eps = (
         pltpu.make_async_copy(occ_hbm, occ_ref, eps_sem.at[0]),
@@ -531,6 +532,8 @@
                 t = lax.rem(code, CODE) - 1
                 pl.semaphore_signal(sem, inc=1, device_id=device(t), device_id_type=MESH)
 
+    if deep > rows:
+        held[:, rows:, :] = jnp.zeros((n_slots + 1, deep - rows, cols), BF16)
     signal(barrier, most, n_folk)
 
     kids = [pick([packed(r[s]) for r in routes], me) for s in range(n_slots + 1)]
@@ -539,11 +542,12 @@
 
     row = lax.broadcasted_iota(jnp.int32, (cols, cols), 0)
     col = lax.broadcasted_iota(jnp.int32, (cols, cols), 1)
-    hit = col == lax.rem(row, width) * occ + row // width
+    hit = row == lax.rem(col, width) * occ + col // width
     order[...] = jnp.where(hit, 1.0, 0.0).astype(BF16)
-    hit = row == lax.rem(col, width) * occ + col // width
-    order_t[...] = jnp.where(hit, 1.0, 0.0).astype(BF16)
     own.wait()
+    held[own_slot, 0:rows, :] = lax.dot_general(
+        raw[...], order[...], NN, preferred_element_type=F32
+    ).astype(BF16)
     pl.semaphore_wait(barrier, n_folk)
 
     def piece(slot, part):
@@ -571,10 +575,6 @@
         copies(own_slot, part, lambda copy: copy.start())
     close = max(n_near)
     signal(news_sem.at[0], close, near)
-    whole_rows = rows // 16 * 16
-    whole_lanes = rows // LANES * LANES
-    lhs[:, :, whole_lanes:] = jnp.zeros((n_slots, cols, deep - whole_lanes), BF16)
-    rhs[:, whole_rows:, :] = jnp.zeros((n_slots, deep - whole_rows, cols), BF16)
     for copy in eps:
         copy.wait()
 
@@ -644,21 +644,9 @@
         left = jnp.where(diag, slot, lax.rem(slot, n_aux))
         right = jnp.where(diag, slot, n_aux + lax.rem(slot, n_aux))
 
-        @pl.when(jnp.logical_and(later == 1, jnp.logical_or(side == 0, diag)))
-        def _():
-            lhs[slot, :, 0:rows] = lax.dot_general(
-                order[...], held[slot], NT, preferred_element_type=F32
-            ).astype(BF16)
-
-        @pl.when(jnp.logical_and(later == 1, jnp.logical_or(side == 1, diag)))
-        def _():
-            rhs[slot, 0:rows, :] = lax.dot_general(
-                held[slot], order_t[...], NN, preferred_element_type=F32
-            ).astype(BF16)
-
         @pl.when(meets)
         def _():
-            ints[mine] += lax.dot_general(lhs[left], rhs[right], NN, preferred_element_type=F32)
+            ints[mine] += lax.dot_general(held[left], held[right], TN, preferred_element_type=F32)
 
         return c
 
@@ -686,17 +674,23 @@
         total = jnp.zeros((width, LANES), F32)
         for ci in range(supers):
             for cj in range(ci, supers):
+                block = [
+                    ints[t, pl.ds((cj * groups + g) * width, width), pl.ds(ci * LANES, LANES)]
+                    for g in range(groups)
+                ]
                 turned = []
-                for g in range(groups):
-                    block = ints[t, pl.ds((cj * groups + g) * width, width), pl.ds(ci * LANES, LANES)]
-                    turned.append([block if r == 0 else pltpu.roll(block, r * width, 1) for r in range(groups)])
+                for r in range(groups):
+                    mixed = block[r]
+                    for g in range(1, groups):
+                        mixed = jnp.where(part == g, block[(g + r) % groups], mixed)
+                    turned.append(mixed if r == 0 else pltpu.roll(mixed, r * width, 1))
                 for s in range(groups):
                     i = ci * groups + s
                     direct = ints[t, pl.ds(i * width, width), pl.ds(cj * LANES, LANES)]
                     inverse = over[t, pl.ds(i * width, width), pl.ds(cj * LANES, LANES)]
-                    swapped = turned[0][(0 - s) % groups]
+                    swapped = turned[(0 - s) % groups]
                     for g in range(1, groups):
-                        swapped = jnp.where(part == g, turned[g][(g - s) % groups], swapped)
+                        swapped = jnp.where(part == g, turned[(g - s) % groups], swapped)
                     if ci == cj:
                         term = direct * (2.0 * direct - swapped) * inverse
                     else:
@@ -814,7 +808,7 @@
 def table_call(n_virt, n_aux, occ, plan, three_index, eps_occ, eps_virt):
     rows, cols = three_index.shape
     width = cols // occ
-    deep = -(-rows // LANES) * LANES
+    deep = -(-rows // 16) * 16
     n = n_virt * n_aux
     n_slots = 2 * n_aux
     vmem = pl.BlockSpec(memory_space=pltpu.VMEM)
@@ -825,10 +819,8 @@
         in_specs=[hbm, hbm, hbm],
         out_specs=vmem,
         scratch_shapes=[
-            pltpu.VMEM((n_slots + 1, rows, cols), BF16),
-            pltpu.VMEM((n_slots, cols, deep), BF16),
-            pltpu.VMEM((n_slots, deep, cols), BF16),
-            pltpu.VMEM((cols, cols), BF16),
+            pltpu.VMEM((rows, cols), BF16),
+            pltpu.VMEM((n_slots + 1, deep, cols), BF16),
             pltpu.VMEM((cols, cols), BF16),
             pltpu.VMEM((2, cols, cols), F32),
             pltpu.VMEM((2, cols, cols), F32),

time: 32.6 us -> 27.1 us (0.83)
  Pallas kernels: 31.8 us -> 26.4 us
    pallas_call x1, Pallas kernels: 31.1 us -> 25.6 us  [table_call(): pl.pallas_call(functools.partial(table_kernel, n_virt, n_aux, occ, plan),...]
where the time goes in v4:
time: 27.1 us; the launch traced here: 27 us
  Pallas kernels  26.4 us (97%)
  between operations  0.64 us (2%)
    pallas_call x1, Pallas kernels, table_call(): pl.pallas_call(functools.partial(table_kernel, n_virt, n_aux, occ, plan),...  25.6 us
    pallas_call x1, Pallas kernels, table_call(): pl.pallas_call(functools.partial(table_unpack, occ, width), out_shape=(ja...  0.74 us

profile of v4, /device:TPU:0, one launch (start us, length us, event | category | flops | bytes accessed | tf_op | source)
XLA Modules:
  0.0 27.0 jit_solution(1105690348289903500)
XLA Ops:
  0.6 25.6 %shard_map.50.done_ref = f32[4,128]{1,0:T(4,128)S(1)} custom-call(bf16[150,640]{1,0:T(8,128)(2,1)} %x_ref.1, f32[20]{0:T(128)} %occ_hbm.1, f32[256]{0:T(256)} %virt_hbm.1), custom_call_target="tpu_custom_call" | custom-call | tf_op jit(solution)/shard_map/pallas_call | solution.py:816
  26.2 0.7 %shard_map.51 = (f32[32]{0:T(128)}, f32[20,20]{1,0:T(8,128)}) custom-call(f32[4,128]{1,0:T(4,128)S(1)} %shard_map.50.done_ref), custom_call_target="tpu_custom_call" | custom-call | tf_op jit(solution)/shard_map/pallas_call | solution.py:842

commit v5 on v4

--- a/solution.py
+++ b/solution.py
@@ -291,13 +291,13 @@
 
 
 TILES = (
+    (0, 2, 0),
+    (0, 1, 0),
+    (0, 2, 1),
     (1, 2, 0),
-    (0, 1, 0),
-    (0, 2, 0),
-    (0, 2, 1),
     (2, 3, 0),
+    (1, 3, 1),
     (1, 3, 0),
-    (1, 3, 1),
     (0, 3, 0),
     (0, 4, 0),
     (0, 5, 0),
@@ -325,141 +325,141 @@
     (7, 5, 0),
 )
 ROUTES = (
-    ((3,), (), (3,), (3,), (8,), (), (8,), (), (2, 14)),
-    ((6, 32), (4, 18), (18,), (), (), (0,), (), (), ()),
-    ((), (6, 14), (6, 14, 32), (), (), (), (), (7,), ()),
-    ((4,), (), (2,), (4, 14, 18), (5,), (5,), (5, 1), (1, 8), ()),
-    ((), (1,), (), (), (11,), (), (), (11,), (0, 10, 24)),
-    ((12,), (3, 12, 42), (), (0, 24), (13,), (9,), (9,), (), ()),
-    ((), (), (0, 24), (40,), (), (15,), (15, 11), (9, 15), ()),
-    ((), (), (), (), (), (), (), (), (10, 12)),
-    ((), (), (), (), (21, 25), (25,), (), (25,), (1, 22)),
-    ((), (16, 34), (16,), (16, 34, 2), (23,), (), (), (), (8, 38, 7)),
-    ((7,), (22,), (7, 22), (5,), (), (29,), (17,), (17, 29), ()),
-    ((20, 36), (), (36,), (20, 38), (), (), (19,), (), ()),
-    ((26, 42), (), (26, 10), (26,), (29,), (), (), (), (9, 30, 46)),
-    ((), (), (42,), (), (19, 31), (19, 31), (), (19,), (11, 30)),
-    ((), (44,), (30, 44), (44,), (), (), (25,), (), ()),
-    ((28, 15), (28, 13), (13,), (13, 28), (), (23,), (23, 27), (23, 27), ()),
-    ((16, 34, 18), (), (34,), (), (37, 41), (37, 41), (), (), (17, 49)),
-    ((), (32,), (), (32,), (39,), (51,), (), (), (17, 53, 21)),
-    ((38,), (20,), (38,), (), (), (45,), (), (45,), (21, 55, 29)),
-    ((), (36,), (), (36,), (), (), (), (), (21, 53, 55)),
-    ((), (), (), (42,), (45,), (), (), (), (27, 59)),
-    ((40,), (24, 40, 26), (40,), (), (35, 47), (35, 47), (), (35,), (27, 59, 57)),
-    ((), (46,), (46,), (46,), (), (), (41,), (41,), (31, 63)),
-    ((44,), (), (), (), (62,), (39,), (39,), (39,), (31, 57, 63)),
-    ((50,), (), (33, 50), (), (55, 60), (), (), (), ()),
-    ((33, 56, 54), (33, 48, 54, 56), (56,), (48, 33, 56), (52,), (), (), (), ()),
-    ((), (), (35,), (), (), (49, 55, 60), (), (60,), (45, 54)),
-    ((), (), (48, 37), (37, 50), (53,), (), (53, 60, 49), (49,), ()),
-    ((), (), (), (), (), (), (), (59,), (58,)),
-    ((51, 43), (43, 62), (43, 51), (51, 43), (57, 61), (63,), (57,), (), ()),
-    ((), (), (), (), (63,), (), (), (), (52, 62)),
-    ((), (52,), (47, 58), (47, 52, 58), (), (61,), (61, 59), (61,), ()),
+    ((2,), (), (18,), (2,), (8, 7), (7, 8), (), (8,), ()),
+    ((4, 16), (0, 4, 16), (0,), (), (), (), (), (), ()),
+    ((14,), (14,), (2, 14, 34), (0, 14), (), (), (7,), (1,), ()),
+    ((), (), (), (), (5,), (), (1, 8), (), (4, 18)),
+    ((), (), (), (), (11, 13), (11,), (11,), (), (10, 40)),
+    ((3, 12), (3, 12, 26), (3, 26), (3, 26), (15,), (), (), (9,), ()),
+    ((6,), (6,), (6, 10), (10,), (), (), (15,), (15,), ()),
+    ((), (), (), (), (), (), (9,), (11,), (6, 12, 24)),
+    ((18, 32), (18, 32), (), (), (21, 25), (), (), (25,), (1, 20)),
+    ((), (), (16,), (16, 34), (23,), (23,), (), (), (1, 22, 38)),
+    ((22, 38), (), (22, 36), (7, 38), (29,), (), (29, 17), (17, 29), ()),
+    ((36,), (5,), (5,), (5, 20), (), (), (), (19,), ()),
+    ((), (), (), (42,), (), (), (), (), (9, 44)),
+    ((24,), (24, 42), (24, 40), (), (19, 31), (31,), (19,), (), (9, 28)),
+    ((30,), (30, 46), (13, 30, 44), (13,), (), (21, 25, 60), (25,), (), ()),
+    ((), (13, 15), (), (28, 44), (), (), (23,), (23, 27), ()),
+    ((34,), (34,), (), (), (37, 41), (37, 45), (), (), (17, 53)),
+    ((), (), (32,), (32,), (), (39,), (), (), (29, 49)),
+    ((), (), (38,), (), (45, 54), (), (), (33, 45), (21, 53, 60)),
+    ((), (36, 20), (), (36,), (), (), (35,), (35,), (21, 53)),
+    ((42,), (), (42,), (), (), (), (), (), (27, 57)),
+    ((26,), (40,), (), (40,), (35,), (35, 47), (), (), (19, 57, 27)),
+    ((46,), (), (46,), (46,), (), (), (41,), (), (27, 61, 31)),
+    ((28,), (44,), (), (), (39,), (62,), (39, 43), (39, 43), (31, 61)),
+    ((33, 50, 56), (33,), (50, 56), (50, 56), (), (53, 17), (), (), ()),
+    ((), (48, 54, 56), (33,), (), (), (52,), (), (), ()),
+    ((), (), (), (), (55,), (55,), (55,), (55, 60, 49), (48, 54)),
+    ((), (), (45, 37), (37, 48), (60, 49), (), (49,), (), ()),
+    ((), (41,), (), (41,), (59, 63), (59, 61), (), (), (51, 58)),
+    ((62, 43), (43, 51), (51,), (51,), (), (), (57,), (57,), ()),
+    ((), (), (), (), (), (63,), (63, 59), (63, 59), (52, 58, 62)),
+    ((47, 52), (), (47,), (47, 52, 58), (61,), (), (), (), ()),
 )
 STEPS = (
-    (4, 0, 8, 2, 5, 1, 25, 3, 12, 6, 29, 10, 7, 14, 31, 27),
-    (2, 3, 0, 1, 10, 4, 12, 8, 5, 27, 29, 25, 14, 6, 15, 23),
-    (4, 5, 6, 7, 2, 12, 3, 29, 14, 31, 0, 10, 1, 8, 25, 27),
-    (6, 23, 4, 21, 12, 2, 29, 19, 0, 14, 10, 17, 8, 31, 25, 27),
-    (8, 2, 10, 14, 9, 11, 15, 0, 19, 12, 17, 13, 6, 4, 23, 21),
-    (2, 3, 0, 1, 6, 7, 10, 8, 27, 4, 14, 25, 12, 5, 31, 29),
-    (4, 21, 6, 23, 14, 2, 31, 12, 19, 29, 0, 10, 17, 8, 27, 25),
-    (6, 14, 4, 0, 15, 23, 12, 5, 1, 29, 2, 8, 3, 10, 25, 27),
-    (2, 10, 8, 3, 6, 9, 27, 14, 7, 12, 4, 31, 0, 5, 29, 17),
-    (2, 3, 6, 10, 7, 8, 4, 27, 5, 9, 0, 14, 12, 31, 17, 29),
-    (4, 5, 6, 7, 0, 14, 12, 1, 31, 10, 29, 8, 11, 25, 2, 19),
-    (6, 7, 4, 5, 0, 1, 14, 12, 31, 29, 8, 10, 2, 3, 27, 25),
-    (4, 0, 5, 1, 6, 10, 2, 7, 8, 25, 3, 27, 12, 14, 29, 31),
-    (10, 8, 4, 0, 11, 5, 9, 14, 17, 12, 6, 2, 15, 23, 19, 29),
-    (4, 5, 6, 7, 2, 0, 12, 14, 3, 1, 29, 31, 10, 8, 27, 25),
-    (6, 7, 4, 5, 2, 14, 0, 12, 3, 31, 1, 29, 10, 8, 27, 25),
-    (10, 11, 8, 4, 0, 9, 14, 2, 5, 17, 19, 15, 12, 6, 29, 23),
-    (10, 2, 4, 11, 0, 8, 19, 5, 9, 6, 12, 17, 14, 7, 31, 29),
-    (14, 2, 6, 3, 15, 10, 23, 4, 27, 5, 12, 8, 0, 9, 17, 29),
-    (2, 6, 3, 14, 7, 31, 12, 4, 13, 21, 10, 0, 8, 27, 1, 25),
-    (2, 10, 11, 6, 19, 8, 0, 12, 4, 9, 7, 13, 21, 14, 17, 31),
-    (10, 11, 2, 8, 9, 19, 14, 0, 4, 15, 6, 12, 5, 17, 29, 23),
-    (4, 5, 12, 0, 6, 29, 14, 1, 7, 2, 31, 3, 10, 27, 8, 25),
-    (14, 15, 4, 0, 12, 5, 29, 10, 1, 6, 11, 8, 23, 25, 2, 19),
-    (0, 1, 2, 3, 6, 8, 7, 4, 25, 5, 12, 10, 14, 27, 29, 31),
-    (2, 3, 0, 1, 6, 8, 7, 25, 4, 14, 31, 5, 10, 27, 12, 29),
-    (14, 6, 4, 10, 12, 7, 5, 11, 29, 31, 2, 19, 8, 0, 9, 17),
-    (6, 23, 4, 21, 12, 2, 10, 14, 29, 19, 31, 8, 0, 27, 17, 25),
-    (2, 3, 14, 8, 0, 10, 1, 25, 27, 6, 15, 12, 23, 4, 13, 21),
-    (2, 19, 0, 17, 10, 6, 8, 23, 14, 25, 4, 27, 21, 12, 31, 29),
-    (12, 14, 13, 4, 6, 10, 0, 8, 15, 21, 2, 9, 17, 3, 23, 27),
-    (6, 7, 4, 5, 2, 12, 3, 14, 29, 10, 31, 8, 0, 27, 9, 17),
+    (0, 1, 2, 3, 4, 10, 8, 6, 5, 27, 7, 25, 14, 31, 12, 29),
+    (2, 3, 0, 1, 10, 4, 27, 5, 8, 25, 6, 12, 7, 29, 14, 31),
+    (4, 21, 6, 23, 2, 14, 19, 0, 31, 17, 12, 29, 10, 8, 27, 25),
+    (6, 4, 14, 7, 5, 31, 2, 10, 12, 3, 8, 29, 0, 27, 1, 25),
+    (10, 8, 11, 9, 12, 2, 13, 0, 19, 14, 17, 15, 6, 4, 23, 21),
+    (2, 19, 0, 17, 4, 21, 10, 6, 8, 23, 27, 25, 12, 14, 29, 31),
+    (4, 5, 6, 7, 2, 12, 3, 29, 0, 14, 1, 31, 8, 10, 25, 27),
+    (4, 5, 12, 6, 29, 7, 14, 2, 31, 8, 3, 10, 0, 1, 25, 27),
+    (2, 3, 8, 0, 6, 1, 25, 14, 7, 4, 12, 10, 5, 31, 27, 29),
+    (2, 6, 10, 3, 0, 7, 4, 1, 8, 5, 27, 12, 25, 14, 31, 29),
+    (4, 5, 6, 7, 14, 0, 12, 31, 1, 29, 2, 8, 3, 10, 25, 27),
+    (6, 7, 4, 5, 2, 0, 3, 14, 1, 10, 31, 8, 12, 27, 25, 29),
+    (6, 2, 7, 3, 8, 4, 5, 9, 10, 14, 27, 0, 17, 12, 31, 29),
+    (2, 8, 12, 3, 10, 9, 4, 14, 5, 27, 6, 29, 15, 0, 23, 17),
+    (4, 5, 6, 7, 2, 10, 3, 14, 27, 12, 31, 0, 29, 8, 1, 25),
+    (6, 7, 4, 5, 14, 2, 31, 12, 8, 3, 10, 9, 29, 0, 27, 17),
+    (8, 9, 10, 2, 4, 11, 14, 19, 15, 5, 12, 6, 0, 29, 17, 23),
+    (4, 10, 11, 2, 5, 8, 6, 14, 19, 9, 15, 23, 12, 0, 29, 17),
+    (14, 4, 15, 2, 3, 5, 12, 8, 9, 6, 0, 10, 29, 23, 27, 17),
+    (2, 3, 4, 14, 15, 6, 5, 12, 29, 23, 10, 8, 0, 27, 9, 17),
+    (0, 8, 1, 10, 25, 2, 11, 6, 12, 14, 19, 4, 7, 5, 29, 31),
+    (10, 11, 8, 14, 0, 9, 15, 2, 12, 17, 6, 19, 13, 23, 4, 21),
+    (6, 4, 0, 7, 12, 5, 14, 1, 31, 2, 29, 10, 8, 3, 27, 25),
+    (14, 15, 6, 12, 4, 0, 13, 10, 23, 2, 8, 21, 11, 1, 25, 19),
+    (0, 1, 2, 3, 10, 6, 4, 27, 7, 5, 14, 12, 31, 8, 25, 29),
+    (2, 3, 0, 1, 10, 8, 6, 4, 27, 25, 14, 7, 5, 12, 31, 29),
+    (14, 12, 6, 4, 8, 15, 23, 5, 9, 29, 0, 10, 17, 2, 11, 19),
+    (6, 23, 4, 21, 2, 14, 12, 8, 19, 31, 25, 29, 10, 0, 17, 27),
+    (10, 8, 2, 0, 11, 9, 19, 17, 6, 4, 14, 12, 7, 31, 5, 29),
+    (2, 19, 0, 17, 6, 4, 10, 8, 23, 21, 27, 25, 14, 12, 31, 29),
+    (14, 12, 15, 13, 4, 10, 6, 11, 2, 8, 21, 0, 23, 9, 17, 19),
+    (6, 7, 4, 5, 0, 14, 1, 12, 31, 29, 8, 10, 2, 25, 11, 19),
 )
 PARTNERS = (
-    (1, 2, 4, 8, 3, 5, 6, 7),
-    (0, 3, 5, 9, 2, 16),
-    (3, 0, 6, 10, 1, 7, 16),
-    (2, 1, 7, 11, 0, 4, 9, 10),
-    (5, 6, 0, 12, 3, 9),
-    (4, 7, 1, 13, 0, 6, 12, 21),
-    (7, 4, 2, 14, 0, 5, 12, 15, 20),
-    (6, 5, 3, 15, 0, 2),
-    (9, 10, 12, 0, 16, 11, 17),
-    (8, 11, 13, 1, 17, 3, 4, 16, 19),
-    (11, 8, 14, 2, 18, 3, 17, 19),
-    (10, 9, 15, 3, 19, 8, 18),
-    (13, 14, 8, 4, 20, 5, 6, 15, 21, 23),
-    (12, 15, 9, 5, 21, 20),
-    (15, 12, 10, 6, 22, 18),
-    (14, 13, 11, 7, 23, 6, 12, 22),
-    (17, 18, 20, 8, 24, 1, 2, 9, 25),
-    (16, 19, 21, 9, 25, 8, 10, 26),
-    (19, 16, 22, 10, 26, 11, 14, 27),
+    (1, 2, 4, 8, 3, 9),
+    (0, 3, 5, 9, 2, 8),
+    (3, 0, 6, 10, 1, 7, 11, 17),
+    (2, 1, 7, 11, 0, 4, 6, 9, 10),
+    (5, 6, 0, 12, 3, 7, 13, 20),
+    (4, 7, 1, 13, 6),
+    (7, 4, 2, 14, 3, 5, 15),
+    (6, 5, 3, 15, 2, 4, 12),
+    (9, 10, 12, 0, 16, 1, 24),
+    (8, 11, 13, 1, 17, 0, 3, 19, 21),
+    (11, 8, 14, 2, 18, 3, 19),
+    (10, 9, 15, 3, 19, 2, 18),
+    (13, 14, 8, 4, 20, 7, 21, 22),
+    (12, 15, 9, 5, 21, 4, 14, 20, 22),
+    (15, 12, 10, 6, 22, 13, 17, 23, 30),
+    (14, 13, 11, 7, 23, 6, 22),
+    (17, 18, 20, 8, 24, 22, 25, 26),
+    (16, 19, 21, 9, 25, 2, 14, 24),
+    (19, 16, 22, 10, 26, 11, 27, 30),
     (18, 17, 23, 11, 27, 9, 10, 26),
-    (21, 22, 16, 12, 28, 6, 13, 29),
-    (20, 23, 17, 13, 29, 5, 12, 28),
-    (23, 20, 18, 14, 30, 15, 26, 31),
-    (22, 21, 19, 15, 31, 12, 28),
-    (25, 26, 28, 16, 27, 30),
+    (21, 22, 16, 12, 28, 4, 13),
+    (20, 23, 17, 13, 29, 9, 12, 28),
+    (23, 20, 18, 14, 30, 12, 13, 15, 16, 27),
+    (22, 21, 19, 15, 31, 14, 30),
+    (25, 26, 28, 16, 8, 17, 27),
     (24, 27, 29, 17, 16, 26, 28),
-    (27, 24, 30, 18, 17, 19, 22, 25, 31),
-    (26, 25, 31, 19, 18, 24, 30),
-    (29, 30, 24, 20, 21, 23, 25),
-    (28, 31, 25, 21, 20, 30),
-    (31, 28, 26, 22, 24, 27, 29),
-    (30, 29, 27, 23, 22, 26),
+    (27, 24, 30, 18, 16, 19, 25, 31),
+    (26, 25, 31, 19, 18, 22, 24, 30),
+    (29, 30, 24, 20, 21, 25, 31),
+    (28, 31, 25, 21, 30),
+    (31, 28, 26, 22, 14, 18, 23, 27, 29),
+    (30, 29, 27, 23, 26, 28),
 )
 NEAR = (4, 4, 4, 4, 4, 4, 4, 4, 5, 5, 5, 5, 5, 5, 5, 5, 5, 5, 5, 5, 5, 5, 5, 5, 4, 4, 4, 4, 4, 4, 4, 4)
 NEWS = (
+    (7, 12, 14),
+    (8, 12, 15),
+    (7, 11, 14),
+    (2, 8, 14),
+    (2, 6, 9),
+    (6, 11, 15),
+    (8, 12, 15),
+    (3, 8, 13),
     (3, 8, 14),
-    (5, 10, 13),
-    (7, 11, 14),
-    (7, 12, 15),
-    (1, 6, 10),
-    (7, 9, 15),
-    (7, 10, 15),
-    (3, 9, 14),
-    (3, 6, 13),
-    (2, 5, 9),
-    (7, 10, 14),
-    (6, 7, 9),
-    (2, 4, 10),
-    (2, 8, 14),
-    (4, 6, 12),
-    (8, 13, 15),
-    (2, 6, 12),
-    (0, 4, 12),
-    (1, 7, 14),
-    (2, 6, 10),
-    (0, 2, 10),
+    (3, 7, 13),
+    (7, 11, 15),
+    (5, 8, 11),
+    (0, 4, 9),
+    (2, 7, 13),
+    (5, 8, 12),
+    (5, 10, 12),
+    (2, 7, 13),
+    (0, 4, 11),
+    (4, 8, 13),
     (2, 6, 11),
-    (2, 5, 11),
-    (3, 9, 14),
-    (6, 10, 12),
-    (7, 10, 13),
-    (2, 8, 12),
-    (6, 10, 14),
+    (0, 3, 8),
+    (2, 7, 13),
+    (2, 8, 13),
+    (2, 11, 15),
+    (7, 10, 12),
+    (6, 11, 15),
+    (4, 9, 14),
+    (5, 10, 14),
+    (4, 8, 13),
+    (6, 11, 15),
     (2, 7, 11),
-    (7, 12, 14),
-    (0, 2, 8),
-    (7, 9, 11),
+    (5, 9, 13),
 )
 PLANS = {(8, 4): (TILES, ROUTES, STEPS, PARTNERS, NEAR, NEWS)}
 
@@ -500,6 +500,10 @@
     side_b = pick([t[1] for t in tiles], me)
     diag = pick([t[2] for t in tiles], me) == 1
     own_slot = jnp.where(side_a == v, p, jnp.where(side_b == v, n_aux + p, n_slots))
+    owns = []
+    for d, (a, b, _) in enumerate(tiles):
+        q = d % n_aux
+        owns.append(q if a == d // n_aux else n_aux + q if b == d // n_aux else n_slots)
     own = pltpu.make_async_copy(x_ref, raw, own_sem)
     own.start()
     eps = (
@@ -535,10 +539,6 @@
     if deep > rows:
         held[:, rows:, :] = jnp.zeros((n_slots + 1, deep - rows, cols), BF16)
     signal(barrier, most, n_folk)
-
-    kids = [pick([packed(r[s]) for r in routes], me) for s in range(n_slots + 1)]
-    spread_at = [pick([r[k] for r in news], me) for k in range(rounds - 1)]
-    todo = [pick([r[i] for r in steps], me) for i in range(2 * n_slots)]
 
     row = lax.broadcasted_iota(jnp.int32, (cols, cols), 0)
     col = lax.broadcasted_iota(jnp.int32, (cols, cols), 1)
@@ -550,11 +550,12 @@
     ).astype(BF16)
     pl.semaphore_wait(barrier, n_folk)
 
+    own_kids = pick([packed(r[o]) for r, o in zip(routes, owns)], me)
+
     def piece(slot, part):
         return held.at[slot, pl.ds(cuts[part][0], cuts[part][1])]
 
-    def copies(slot, part, act):
-        code = pick(kids, slot)
+    def copies(slot, part, code, act):
         q = jnp.where(slot == n_slots, p, lax.rem(slot, n_aux))
         for k in range(KIDS):
             this = lax.rem(code, CODE)
@@ -572,9 +573,12 @@
                 act(copy)
 
     for part in range(2):
-        copies(own_slot, part, lambda copy: copy.start())
+        copies(own_slot, part, own_kids, lambda copy: copy.start())
     close = max(n_near)
     signal(news_sem.at[0], close, near)
+    kids = [pick([packed(r[s]) for r in routes], me) for s in range(n_slots + 1)]
+    spread_at = [pick([r[k] for r in news], me) for k in range(rounds - 1)]
+    todo = [pick([r[i] for r in steps], me) for i in range(2 * n_slots)]
     for copy in eps:
         copy.wait()
 
@@ -637,7 +641,7 @@
             def _():
                 whole = piece(slot, part)
                 pltpu.make_async_copy(whole, whole, recv_sem.at[slot, part]).wait()
-                copies(slot, part, lambda copy: copy.start())
+                copies(slot, part, pick(kids, slot), lambda copy: copy.start())
 
         side = lax.div(slot, n_aux)
         mine = jnp.where(diag, side, 0)
@@ -751,25 +755,28 @@
     pl.semaphore_wait(news_sem.at[rounds - 1], near)
 
     def tell(k, c):
-        t = me + k
-        t = jnp.where(t >= n, t - n, t)
-        pltpu.make_async_remote_copy(
-            src_ref=message, dst_ref=slots.at[me],
-            send_sem=msg_send, recv_sem=msg_recv,
-            device_id=device(t), device_id_type=MESH,
-        ).start()
+        t = jnp.where(v * 2 < n_virt, n - 1 - k, k)
+
+        @pl.when(t != me)
+        def _():
+            pltpu.make_async_remote_copy(
+                src_ref=message, dst_ref=slots.at[me],
+                send_sem=msg_send, recv_sem=msg_recv,
+                device_id=device(t), device_id_type=MESH,
+            ).start()
+
         return c
 
-    lax.fori_loop(1, n, tell, 0)
+    lax.fori_loop(0, n, tell, 0)
     slots[me] = message[...]
     for part_at in range(2):
-        copies(own_slot, part_at, lambda copy: copy.wait_send())
+        copies(own_slot, part_at, own_kids, lambda copy: copy.wait_send())
 
     def flush(s, c):
         @pl.when(s != own_slot)
         def _():
             for part_at in range(2):
-                copies(s, part_at, lambda copy: copy.wait_send())
+                copies(s, part_at, pick(kids, s), lambda copy: copy.wait_send())
 
         return c
 

time: 27.1 us -> 28 us (1.033)
  Pallas kernels: 26.4 us -> 27.2 us
    pallas_call x1, Pallas kernels: 25.6 us -> 26.5 us  [table_call(): pl.pallas_call(functools.partial(table_kernel, n_virt, n_aux, occ, plan),...]
where the time goes in v5:
time: 28 us; the launch traced here: 27.8 us
  Pallas kernels  27.2 us (97%)
  between operations  0.64 us (2%)
    pallas_call x1, Pallas kernels, table_call(): pl.pallas_call(functools.partial(table_kernel, n_virt, n_aux, occ, plan),...  26.5 us
    pallas_call x1, Pallas kernels, table_call(): pl.pallas_call(functools.partial(table_unpack, occ, width), out_shape=(ja...  0.74 us

profile of v5, /device:TPU:0, one launch (start us, length us, event | category | flops | bytes accessed | tf_op | source)
XLA Modules:
  0.0 27.8 jit_solution(6713681099738450139)
XLA Ops:
  0.6 26.5 %shard_map.50.done_ref = f32[4,128]{1,0:T(4,128)S(1)} custom-call(bf16[150,640]{1,0:T(8,128)(2,1)} %x_ref.1, f32[20]{0:T(128)} %occ_hbm.1, f32[256]{0:T(256)} %virt_hbm.1), custom_call_target="tpu_custom_call" | custom-call | tf_op jit(solution)/shard_map/pallas_call | solution.py:823
  27.1 0.7 %shard_map.51 = (f32[32]{0:T(128)}, f32[20,20]{1,0:T(8,128)}) custom-call(f32[4,128]{1,0:T(4,128)S(1)} %shard_map.50.done_ref), custom_call_target="tpu_custom_call" | custom-call | tf_op jit(solution)/shard_map/pallas_call | solution.py:849

commit v6 on v5

--- a/solution.py
+++ b/solution.py
@@ -291,21 +291,21 @@
 
 
 TILES = (
+    (0, 2, 1),
     (0, 2, 0),
     (0, 1, 0),
-    (0, 2, 1),
     (1, 2, 0),
+    (1, 3, 1),
+    (0, 3, 0),
+    (1, 3, 0),
     (2, 3, 0),
-    (1, 3, 1),
-    (1, 3, 0),
-    (0, 3, 0),
     (0, 4, 0),
     (0, 5, 0),
     (2, 4, 0),
     (2, 5, 0),
     (1, 4, 0),
+    (3, 4, 0),
     (1, 5, 0),
-    (3, 4, 0),
     (3, 5, 0),
     (0, 6, 0),
     (0, 7, 0),
@@ -315,8 +315,8 @@
     (1, 7, 0),
     (3, 6, 0),
     (3, 7, 0),
+    (6, 7, 0),
     (6, 4, 0),
-    (6, 7, 0),
     (7, 4, 0),
     (6, 4, 1),
     (6, 5, 0),
@@ -325,141 +325,141 @@
     (7, 5, 0),
 )
 ROUTES = (
-    ((2,), (), (18,), (2,), (8, 7), (7, 8), (), (8,), ()),
-    ((4, 16), (0, 4, 16), (0,), (), (), (), (), (), ()),
-    ((14,), (14,), (2, 14, 34), (0, 14), (), (), (7,), (1,), ()),
-    ((), (), (), (), (5,), (), (1, 8), (), (4, 18)),
-    ((), (), (), (), (11, 13), (11,), (11,), (), (10, 40)),
-    ((3, 12), (3, 12, 26), (3, 26), (3, 26), (15,), (), (), (9,), ()),
-    ((6,), (6,), (6, 10), (10,), (), (), (15,), (15,), ()),
-    ((), (), (), (), (), (), (9,), (11,), (6, 12, 24)),
-    ((18, 32), (18, 32), (), (), (21, 25), (), (), (25,), (1, 20)),
-    ((), (), (16,), (16, 34), (23,), (23,), (), (), (1, 22, 38)),
-    ((22, 38), (), (22, 36), (7, 38), (29,), (), (29, 17), (17, 29), ()),
-    ((36,), (5,), (5,), (5, 20), (), (), (), (19,), ()),
-    ((), (), (), (42,), (), (), (), (), (9, 44)),
-    ((24,), (24, 42), (24, 40), (), (19, 31), (31,), (19,), (), (9, 28)),
-    ((30,), (30, 46), (13, 30, 44), (13,), (), (21, 25, 60), (25,), (), ()),
-    ((), (13, 15), (), (28, 44), (), (), (23,), (23, 27), ()),
-    ((34,), (34,), (), (), (37, 41), (37, 45), (), (), (17, 53)),
-    ((), (), (32,), (32,), (), (39,), (), (), (29, 49)),
-    ((), (), (38,), (), (45, 54), (), (), (33, 45), (21, 53, 60)),
-    ((), (36, 20), (), (36,), (), (), (35,), (35,), (21, 53)),
-    ((42,), (), (42,), (), (), (), (), (), (27, 57)),
-    ((26,), (40,), (), (40,), (35,), (35, 47), (), (), (19, 57, 27)),
-    ((46,), (), (46,), (46,), (), (), (41,), (), (27, 61, 31)),
-    ((28,), (44,), (), (), (39,), (62,), (39, 43), (39, 43), (31, 61)),
-    ((33, 50, 56), (33,), (50, 56), (50, 56), (), (53, 17), (), (), ()),
-    ((), (48, 54, 56), (33,), (), (), (52,), (), (), ()),
-    ((), (), (), (), (55,), (55,), (55,), (55, 60, 49), (48, 54)),
-    ((), (), (45, 37), (37, 48), (60, 49), (), (49,), (), ()),
-    ((), (41,), (), (41,), (59, 63), (59, 61), (), (), (51, 58)),
-    ((62, 43), (43, 51), (51,), (51,), (), (), (57,), (57,), ()),
-    ((), (), (), (), (), (63,), (63, 59), (63, 59), (52, 58, 62)),
-    ((47, 52), (), (47,), (47, 52, 58), (61,), (), (), (), ()),
+    ((2, 10, 18), (4, 10, 32), (2,), (16,), (3,), (3,), (), (3,), ()),
+    ((4,), (0,), (10, 18), (10,), (), (7,), (1,), (), ()),
+    ((), (), (0,), (2,), (), (), (6,), (6,), ()),
+    ((5,), (), (), (), (14,), (14, 20), (14, 3), (1, 14), (4, 18)),
+    ((12, 24), (12, 24), (24,), (), (11,), (15,), (), (26,), ()),
+    ((), (), (), (), (15,), (9,), (9,), (), (5, 8)),
+    ((6,), (6, 28), (5, 8, 28), (5, 8, 28), (), (), (15,), (15, 9, 11), ()),
+    ((), (), (), (), (13,), (13,), (), (), (12, 40)),
+    ((), (), (), (), (21, 27), (), (), (27,), (1, 22)),
+    ((16, 32), (16,), (16, 34), (0, 32), (23,), (), (), (), (1, 38)),
+    ((), (), (22, 38), (38,), (), (), (17, 25, 51), (), ()),
+    ((20, 36, 7), (), (7,), (7, 20), (), (19,), (19,), (19, 29), ()),
+    ((28, 42), (42,), (40,), (), (), (27,), (27,), (), (26,)),
+    ((9, 46), (11, 44), (11,), (), (25,), (17, 21), (), (25,), ()),
+    ((), (), (), (), (), (31, 61, 23), (23, 31), (31,), (26, 30)),
+    ((), (), (13, 44), (13, 44), (29,), (), (), (), ()),
+    ((34,), (18, 34), (), (34,), (), (37,), (), (41,), (17, 51)),
+    ((), (), (32,), (), (), (43,), (), (), (25, 51, 60)),
+    ((38,), (22,), (), (), (33,), (45,), (33, 45), (33, 45), (21, 60, 55)),
+    ((), (36,), (36,), (36,), (), (), (), (), (17, 53)),
+    ((), (), (42,), (42, 24), (45, 56), (), (), (), (19, 59, 31, 57)),
+    ((40,), (40,), (), (), (35, 47), (), (), (), (29, 57)),
+    ((), (46,), (46,), (46,), (), (), (41,), (), (29, 63)),
+    ((44, 30), (30,), (), (), (), (), (39, 43), (39, 43), (23, 61)),
+    ((50, 54), (54,), (), (50,), (), (35, 39), (), (), ()),
+    ((41,), (33, 48, 56), (48, 56), (56,), (55,), (53,), (), (), ()),
+    ((), (), (), (), (), (55,), (), (55, 60, 51), (50, 54)),
+    ((37,), (), (37,), (37, 48), (53, 60), (), (), (21,), ()),
+    ((), (41,), (), (), (), (59,), (), (), (43, 49, 58)),
+    ((62,), (49, 62), (49, 35), (35, 49), (63,), (), (57,), (57,), ()),
+    ((), (), (53,), (), (), (63,), (), (63,), (62,)),
+    ((39, 52), (47, 52), (47, 52, 58), (47, 52, 58), (61,), (), (61, 59), (59,), ()),
 )
 STEPS = (
-    (0, 1, 2, 3, 4, 10, 8, 6, 5, 27, 7, 25, 14, 31, 12, 29),
-    (2, 3, 0, 1, 10, 4, 27, 5, 8, 25, 6, 12, 7, 29, 14, 31),
-    (4, 21, 6, 23, 2, 14, 19, 0, 31, 17, 12, 29, 10, 8, 27, 25),
-    (6, 4, 14, 7, 5, 31, 2, 10, 12, 3, 8, 29, 0, 27, 1, 25),
-    (10, 8, 11, 9, 12, 2, 13, 0, 19, 14, 17, 15, 6, 4, 23, 21),
-    (2, 19, 0, 17, 4, 21, 10, 6, 8, 23, 27, 25, 12, 14, 29, 31),
-    (4, 5, 6, 7, 2, 12, 3, 29, 0, 14, 1, 31, 8, 10, 25, 27),
-    (4, 5, 12, 6, 29, 7, 14, 2, 31, 8, 3, 10, 0, 1, 25, 27),
-    (2, 3, 8, 0, 6, 1, 25, 14, 7, 4, 12, 10, 5, 31, 27, 29),
-    (2, 6, 10, 3, 0, 7, 4, 1, 8, 5, 27, 12, 25, 14, 31, 29),
-    (4, 5, 6, 7, 14, 0, 12, 31, 1, 29, 2, 8, 3, 10, 25, 27),
-    (6, 7, 4, 5, 2, 0, 3, 14, 1, 10, 31, 8, 12, 27, 25, 29),
-    (6, 2, 7, 3, 8, 4, 5, 9, 10, 14, 27, 0, 17, 12, 31, 29),
-    (2, 8, 12, 3, 10, 9, 4, 14, 5, 27, 6, 29, 15, 0, 23, 17),
-    (4, 5, 6, 7, 2, 10, 3, 14, 27, 12, 31, 0, 29, 8, 1, 25),
-    (6, 7, 4, 5, 14, 2, 31, 12, 8, 3, 10, 9, 29, 0, 27, 17),
-    (8, 9, 10, 2, 4, 11, 14, 19, 15, 5, 12, 6, 0, 29, 17, 23),
-    (4, 10, 11, 2, 5, 8, 6, 14, 19, 9, 15, 23, 12, 0, 29, 17),
-    (14, 4, 15, 2, 3, 5, 12, 8, 9, 6, 0, 10, 29, 23, 27, 17),
-    (2, 3, 4, 14, 15, 6, 5, 12, 29, 23, 10, 8, 0, 27, 9, 17),
-    (0, 8, 1, 10, 25, 2, 11, 6, 12, 14, 19, 4, 7, 5, 29, 31),
-    (10, 11, 8, 14, 0, 9, 15, 2, 12, 17, 6, 19, 13, 23, 4, 21),
-    (6, 4, 0, 7, 12, 5, 14, 1, 31, 2, 29, 10, 8, 3, 27, 25),
-    (14, 15, 6, 12, 4, 0, 13, 10, 23, 2, 8, 21, 11, 1, 25, 19),
-    (0, 1, 2, 3, 10, 6, 4, 27, 7, 5, 14, 12, 31, 8, 25, 29),
-    (2, 3, 0, 1, 10, 8, 6, 4, 27, 25, 14, 7, 5, 12, 31, 29),
-    (14, 12, 6, 4, 8, 15, 23, 5, 9, 29, 0, 10, 17, 2, 11, 19),
-    (6, 23, 4, 21, 2, 14, 12, 8, 19, 31, 25, 29, 10, 0, 17, 27),
-    (10, 8, 2, 0, 11, 9, 19, 17, 6, 4, 14, 12, 7, 31, 5, 29),
-    (2, 19, 0, 17, 6, 4, 10, 8, 23, 21, 27, 25, 14, 12, 31, 29),
-    (14, 12, 15, 13, 4, 10, 6, 11, 2, 8, 21, 0, 23, 9, 17, 19),
-    (6, 7, 4, 5, 0, 14, 1, 12, 31, 29, 8, 10, 2, 25, 11, 19),
+    (0, 17, 2, 19, 4, 10, 21, 8, 27, 25, 14, 6, 31, 23, 12, 29),
+    (2, 3, 0, 1, 4, 10, 8, 5, 6, 27, 7, 25, 14, 12, 31, 29),
+    (4, 5, 6, 7, 12, 10, 29, 14, 0, 2, 31, 11, 8, 1, 19, 25),
+    (14, 15, 4, 12, 5, 29, 6, 8, 0, 23, 9, 17, 10, 2, 11, 19),
+    (0, 17, 2, 19, 4, 10, 21, 27, 8, 6, 25, 23, 14, 12, 29, 31),
+    (10, 0, 11, 1, 2, 19, 8, 12, 4, 25, 13, 21, 14, 6, 15, 23),
+    (4, 5, 6, 7, 14, 0, 31, 1, 12, 2, 29, 3, 10, 27, 8, 25),
+    (14, 15, 6, 12, 23, 13, 10, 4, 11, 21, 8, 0, 9, 17, 2, 19),
+    (0, 8, 14, 1, 25, 15, 12, 4, 10, 5, 2, 29, 6, 11, 19, 23),
+    (0, 1, 6, 8, 7, 4, 14, 25, 5, 2, 31, 12, 3, 10, 29, 27),
+    (4, 5, 6, 7, 0, 12, 1, 29, 8, 25, 14, 10, 31, 2, 3, 27),
+    (6, 7, 4, 5, 0, 1, 14, 31, 12, 2, 8, 10, 3, 29, 27, 25),
+    (0, 1, 10, 2, 3, 27, 4, 8, 5, 12, 14, 25, 6, 29, 15, 23),
+    (2, 3, 0, 1, 4, 5, 10, 8, 27, 14, 25, 12, 6, 15, 29, 23),
+    (4, 12, 10, 5, 29, 11, 0, 6, 14, 8, 7, 1, 2, 31, 19, 25),
+    (6, 7, 4, 5, 12, 10, 8, 29, 2, 11, 0, 14, 19, 9, 17, 31),
+    (10, 11, 2, 14, 0, 15, 1, 19, 12, 6, 13, 23, 8, 25, 4, 21),
+    (8, 2, 14, 10, 0, 9, 17, 3, 15, 27, 6, 12, 4, 23, 13, 21),
+    (14, 4, 15, 2, 5, 12, 3, 6, 29, 10, 0, 8, 27, 23, 9, 17),
+    (4, 2, 5, 3, 6, 14, 15, 23, 12, 0, 10, 29, 1, 8, 27, 25),
+    (6, 8, 9, 10, 7, 0, 17, 11, 14, 2, 19, 4, 12, 31, 5, 29),
+    (8, 9, 14, 6, 0, 15, 17, 12, 23, 2, 13, 3, 10, 27, 4, 21),
+    (2, 6, 3, 7, 14, 0, 31, 4, 12, 1, 5, 8, 29, 25, 10, 27),
+    (14, 15, 2, 6, 12, 0, 3, 13, 8, 23, 10, 1, 25, 27, 4, 21),
+    (0, 1, 2, 3, 6, 10, 8, 4, 7, 27, 25, 14, 5, 31, 12, 29),
+    (2, 3, 0, 1, 10, 8, 4, 6, 25, 5, 27, 7, 14, 31, 12, 29),
+    (6, 14, 7, 4, 31, 5, 10, 2, 12, 8, 3, 9, 0, 27, 17, 29),
+    (6, 23, 4, 21, 0, 17, 14, 2, 12, 19, 31, 8, 10, 25, 29, 27),
+    (2, 10, 3, 27, 8, 4, 9, 12, 6, 0, 14, 13, 21, 17, 15, 23),
+    (2, 19, 0, 17, 6, 8, 23, 10, 4, 21, 27, 25, 12, 14, 29, 31),
+    (14, 4, 12, 15, 13, 2, 6, 21, 23, 10, 8, 3, 27, 0, 9, 17),
+    (6, 7, 4, 5, 2, 12, 3, 14, 29, 0, 31, 1, 8, 25, 10, 27),
 )
 PARTNERS = (
-    (1, 2, 4, 8, 3, 9),
-    (0, 3, 5, 9, 2, 8),
-    (3, 0, 6, 10, 1, 7, 11, 17),
-    (2, 1, 7, 11, 0, 4, 6, 9, 10),
-    (5, 6, 0, 12, 3, 7, 13, 20),
-    (4, 7, 1, 13, 6),
+    (1, 2, 4, 8, 3, 5, 9, 16),
+    (0, 3, 5, 9, 2),
+    (3, 0, 6, 10, 1, 5),
+    (2, 1, 7, 11, 0, 6, 9, 10),
+    (5, 6, 0, 12, 7, 13),
+    (4, 7, 1, 13, 0, 2, 6),
     (7, 4, 2, 14, 3, 5, 15),
-    (6, 5, 3, 15, 2, 4, 12),
-    (9, 10, 12, 0, 16, 1, 24),
-    (8, 11, 13, 1, 17, 0, 3, 19, 21),
-    (11, 8, 14, 2, 18, 3, 19),
-    (10, 9, 15, 3, 19, 2, 18),
-    (13, 14, 8, 4, 20, 7, 21, 22),
-    (12, 15, 9, 5, 21, 4, 14, 20, 22),
-    (15, 12, 10, 6, 22, 13, 17, 23, 30),
-    (14, 13, 11, 7, 23, 6, 22),
-    (17, 18, 20, 8, 24, 22, 25, 26),
-    (16, 19, 21, 9, 25, 2, 14, 24),
+    (6, 5, 3, 15, 4, 20),
+    (9, 10, 12, 0, 16, 11, 13, 19),
+    (8, 11, 13, 1, 17, 0, 3, 16, 19, 20),
+    (11, 8, 14, 2, 18, 3, 12, 13, 19, 25, 27),
+    (10, 9, 15, 3, 19, 8, 14, 18, 23),
+    (13, 14, 8, 4, 20, 10, 17, 21),
+    (12, 15, 9, 5, 21, 4, 8, 10, 14, 22, 23),
+    (15, 12, 10, 6, 22, 11, 13, 21, 30),
+    (14, 13, 11, 7, 23, 6, 20, 22),
+    (17, 18, 20, 8, 24, 0, 9, 25),
+    (16, 19, 21, 9, 25, 12, 24, 29, 30),
     (19, 16, 22, 10, 26, 11, 27, 30),
-    (18, 17, 23, 11, 27, 9, 10, 26),
-    (21, 22, 16, 12, 28, 4, 13),
-    (20, 23, 17, 13, 29, 9, 12, 28),
-    (23, 20, 18, 14, 30, 12, 13, 15, 16, 27),
-    (22, 21, 19, 15, 31, 14, 30),
-    (25, 26, 28, 16, 8, 17, 27),
-    (24, 27, 29, 17, 16, 26, 28),
-    (27, 24, 30, 18, 16, 19, 25, 31),
-    (26, 25, 31, 19, 18, 22, 24, 30),
-    (29, 30, 24, 20, 21, 25, 31),
-    (28, 31, 25, 21, 30),
-    (31, 28, 26, 22, 14, 18, 23, 27, 29),
-    (30, 29, 27, 23, 26, 28),
+    (18, 17, 23, 11, 27, 8, 9, 10, 24, 26, 31),
+    (21, 22, 16, 12, 28, 7, 9, 15, 25, 29),
+    (20, 23, 17, 13, 29, 12, 14, 28),
+    (23, 20, 18, 14, 30, 13, 15, 31),
+    (22, 21, 19, 15, 31, 11, 13, 30),
+    (25, 26, 28, 16, 17, 19, 27, 29),
+    (24, 27, 29, 17, 10, 16, 20, 26, 28),
+    (27, 24, 30, 18, 19, 25, 31),
+    (26, 25, 31, 19, 10, 18, 24, 30),
+    (29, 30, 24, 20, 21, 25),
+    (28, 31, 25, 21, 17, 20, 24),
+    (31, 28, 26, 22, 14, 17, 18, 23, 27),
+    (30, 29, 27, 23, 19, 22, 26),
 )
 NEAR = (4, 4, 4, 4, 4, 4, 4, 4, 5, 5, 5, 5, 5, 5, 5, 5, 5, 5, 5, 5, 5, 5, 5, 5, 4, 4, 4, 4, 4, 4, 4, 4)
 NEWS = (
+    (8, 12, 15),
+    (5, 11, 15),
+    (7, 12, 15),
+    (3, 10, 15),
+    (7, 13, 15),
+    (4, 10, 15),
+    (8, 12, 15),
+    (1, 8, 13),
+    (3, 6, 12),
+    (4, 6, 11),
+    (6, 8, 11),
+    (7, 10, 15),
+    (3, 7, 13),
+    (6, 8, 14),
+    (3, 8, 15),
+    (4, 9, 15),
+    (2, 6, 13),
+    (0, 4, 11),
+    (4, 13, 15),
+    (4, 8, 13),
+    (0, 5, 10),
+    (2, 6, 12),
+    (3, 8, 15),
+    (3, 12, 15),
+    (7, 12, 15),
+    (7, 13, 14),
+    (3, 7, 14),
+    (6, 11, 15),
+    (3, 6, 14),
+    (7, 13, 15),
+    (1, 6, 11),
     (7, 12, 14),
-    (8, 12, 15),
-    (7, 11, 14),
-    (2, 8, 14),
-    (2, 6, 9),
-    (6, 11, 15),
-    (8, 12, 15),
-    (3, 8, 13),
-    (3, 8, 14),
-    (3, 7, 13),
-    (7, 11, 15),
-    (5, 8, 11),
-    (0, 4, 9),
-    (2, 7, 13),
-    (5, 8, 12),
-    (5, 10, 12),
-    (2, 7, 13),
-    (0, 4, 11),
-    (4, 8, 13),
-    (2, 6, 11),
-    (0, 3, 8),
-    (2, 7, 13),
-    (2, 8, 13),
-    (2, 11, 15),
-    (7, 10, 12),
-    (6, 11, 15),
-    (4, 9, 14),
-    (5, 10, 14),
-    (4, 8, 13),
-    (6, 11, 15),
-    (2, 7, 11),
-    (5, 9, 13),
 )
 PLANS = {(8, 4): (TILES, ROUTES, STEPS, PARTNERS, NEAR, NEWS)}
 
@@ -473,7 +473,7 @@
     n_virt, n_aux, occ, plan,
     x_ref, occ_hbm, virt_hbm,
     done_ref,
-    raw, held, order, ints, over, sums, message, slots, occ_ref, virt_ref,
+    raw, held, order, ints, over, sums, message, slots, weigh, occ_ref, virt_ref,
     own_sem, eps_sem, send_sem, recv_sem, msg_send, msg_recv, news_sem,
 ):
     rows, cols = x_ref.shape
@@ -555,25 +555,30 @@
     def piece(slot, part):
         return held.at[slot, pl.ds(cuts[part][0], cuts[part][1])]
 
-    def copies(slot, part, code, act):
+    def decode(slot, code):
         q = jnp.where(slot == n_slots, p, lax.rem(slot, n_aux))
+        found = []
         for k in range(KIDS):
             this = lax.rem(code, CODE)
             code = lax.div(code, CODE)
-
-            @pl.when(this > 0)
+            t = jnp.maximum(this - 1, 0)
+            found.append((this > 0, lax.div(t, 2), lax.rem(t, 2) * n_aux + q))
+        return found
+
+    def copies(slot, part, found, act):
+        for there, t, to in found:
+
+            @pl.when(there)
             def _():
-                t = this - 1
-                to = lax.rem(t, 2) * n_aux + q
-                copy = pltpu.make_async_remote_copy(
+                act(pltpu.make_async_remote_copy(
                     src_ref=piece(slot, part), dst_ref=piece(to, part),
-                    send_sem=send_sem.at[slot, part, k], recv_sem=recv_sem.at[to, part],
-                    device_id=device(lax.div(t, 2)), device_id_type=MESH,
-                )
-                act(copy)
-
+                    send_sem=send_sem.at[slot], recv_sem=recv_sem.at[to, part],
+                    device_id=device(t), device_id_type=MESH,
+                ))
+
+    own_found = decode(own_slot, own_kids)
     for part in range(2):
-        copies(own_slot, part, own_kids, lambda copy: copy.start())
+        copies(own_slot, part, own_found, lambda copy: copy.start())
     close = max(n_near)
     signal(news_sem.at[0], close, near)
     kids = [pick([packed(r[s]) for r in routes], me) for s in range(n_slots + 1)]
@@ -622,6 +627,13 @@
 
     lax.fori_loop(0, n_tiles, prepare, 0)
 
+    keep = lax.broadcasted_iota(jnp.int32, (4, LANES), 1) < -(-occ // 4) * occ
+    upper = lax.broadcasted_iota(jnp.int32, (4, LANES), 0) < 2
+    for k in range(n):
+        row0 = jnp.where(v == tiles[k][0], 1.0, 0.0)
+        row1 = jnp.where(v == tiles[k][1], 1.0, 0.0)
+        weigh[k] = jnp.where(keep, 1.0, jnp.where(upper, row0, row1))
+
     def take(i, c):
         for r in range(1, rounds):
 
@@ -635,13 +647,14 @@
         meets = lax.div(entry, 4 * n_aux) == 1
         later = lax.rem(entry, 2)
         away = slot != own_slot
+        found = decode(slot, pick(kids, slot))
         for part in range(2):
 
             @pl.when(jnp.logical_and(later == part, away))
             def _():
                 whole = piece(slot, part)
                 pltpu.make_async_copy(whole, whole, recv_sem.at[slot, part]).wait()
-                copies(slot, part, pick(kids, slot), lambda copy: copy.start())
+                copies(slot, part, found, lambda copy: copy.start())
 
         side = lax.div(slot, n_aux)
         mine = jnp.where(diag, side, 0)
@@ -754,47 +767,40 @@
     lax.fori_loop(0, n_tiles, tile, 0)
     pl.semaphore_wait(news_sem.at[rounds - 1], near)
 
-    def tell(k, c):
-        t = jnp.where(v * 2 < n_virt, n - 1 - k, k)
-
-        @pl.when(t != me)
+    for t in range(n):
+
+        @pl.when(me != t)
         def _():
             pltpu.make_async_remote_copy(
                 src_ref=message, dst_ref=slots.at[me],
                 send_sem=msg_send, recv_sem=msg_recv,
-                device_id=device(t), device_id_type=MESH,
+                device_id={"virt": t // n_aux, "aux": t % n_aux}, device_id_type=MESH,
             ).start()
 
+    slots[me] = message[...]
+    sent = sum(cut[1] for cut in cuts)
+
+    def flush(s, c):
+        many = sum(jnp.where(there, 1, 0) for there, _, _ in decode(s, pick(kids, s)))
+        for m in range(1, KIDS + 1):
+
+            @pl.when(many == m)
+            def _():
+                gone = held.at[pl.ds(0, m), pl.ds(0, sent)]
+                pltpu.make_async_copy(gone, gone, send_sem.at[s]).wait()
+
         return c
 
-    lax.fori_loop(0, n, tell, 0)
-    slots[me] = message[...]
-    for part_at in range(2):
-        copies(own_slot, part_at, own_kids, lambda copy: copy.wait_send())
-
-    def flush(s, c):
-        @pl.when(s != own_slot)
-        def _():
-            for part_at in range(2):
-                copies(s, part_at, pick(kids, s), lambda copy: copy.wait_send())
-
-        return c
-
-    lax.fori_loop(0, n_slots, flush, 0)
+    lax.fori_loop(0, n_slots + 1, flush, 0)
     everyone = slots.at[pl.ds(0, n - 1)]
     pltpu.make_async_copy(everyone, everyone, msg_send).wait()
     pltpu.make_async_copy(everyone, everyone, msg_recv).wait()
 
-    keep = l8[0:4] < free
-    upper = r8[0:4] < 2
-    acc = None
+    accs = [None] * 4
     for k in range(n):
-        a, b, _ = tiles[k]
-        row0 = jnp.where(v == a, 1.0, 0.0)
-        row1 = jnp.where(v == b, 1.0, 0.0)
-        term = slots[k] * jnp.where(keep, 1.0, jnp.where(upper, row0, row1))
-        acc = term if acc is None else acc + term
-    done_ref[...] = acc
+        term = slots[k] * weigh[k]
+        accs[k % 4] = term if accs[k % 4] is None else accs[k % 4] + term
+    done_ref[...] = (accs[0] + accs[1]) + (accs[2] + accs[3])
 
 
 def table_unpack(occ, width, done_ref, share_ref, pair_ref):
@@ -834,11 +840,12 @@
             pltpu.VMEM((occ * 8, cols), F32),
             pltpu.VMEM((4, LANES), F32),
             pltpu.VMEM((n, 4, LANES), F32),
+            pltpu.VMEM((n, 4, LANES), F32),
             pltpu.SMEM(eps_occ.shape, F32),
             pltpu.SMEM(eps_virt.shape, F32),
             pltpu.SemaphoreType.DMA,
             pltpu.SemaphoreType.DMA((2,)),
-            pltpu.SemaphoreType.DMA((n_slots + 1, 2, KIDS)),
+            pltpu.SemaphoreType.DMA((n_slots + 1,)),
             pltpu.SemaphoreType.DMA((n_slots, 2)),
             pltpu.SemaphoreType.DMA,
             pltpu.SemaphoreType.DMA,

time: 28 us -> 26.4 us (0.943)
  Pallas kernels: 27.2 us -> 25.6 us
    pallas_call x1, Pallas kernels: 26.5 us -> 24.9 us  [table_call(): pl.pallas_call(functools.partial(table_kernel, n_virt, n_aux, occ, plan),...]
where the time goes in v6:
time: 26.4 us; the launch traced here: 26.2 us
  Pallas kernels  25.6 us (97%)
  between operations  0.64 us (2%)
    pallas_call x1, Pallas kernels, table_call(): pl.pallas_call(functools.partial(table_kernel, n_virt, n_aux, occ, plan),...  24.9 us
    pallas_call x1, Pallas kernels, table_call(): pl.pallas_call(functools.partial(table_unpack, occ, width), out_shape=(ja...  0.74 us

profile of v6, /device:TPU:0, one launch (start us, length us, event | category | flops | bytes accessed | tf_op | source)
XLA Modules:
  0.0 26.2 jit_solution(1736503942522821475)
XLA Ops:
  0.6 24.9 %shard_map.50.done_ref = f32[4,128]{1,0:T(4,128)S(1)} custom-call(bf16[150,640]{1,0:T(8,128)(2,1)} %x_ref.1, f32[20]{0:T(128)} %occ_hbm.1, f32[256]{0:T(256)} %virt_hbm.1), custom_call_target="tpu_custom_call" | custom-call | tf_op jit(solution)/shard_map/pallas_call | solution.py:829
  25.5 0.7 %shard_map.51 = (f32[32]{0:T(128)}, f32[20,20]{1,0:T(8,128)}) custom-call(f32[4,128]{1,0:T(4,128)S(1)} %shard_map.50.done_ref), custom_call_target="tpu_custom_call" | custom-call | tf_op jit(solution)/shard_map/pallas_call | solution.py:856

commit v7 on v6

--- a/solution.py
+++ b/solution.py
@@ -291,8 +291,8 @@
 
 
 TILES = (
+    (0, 2, 0),
     (0, 2, 1),
-    (0, 2, 0),
     (0, 1, 0),
     (1, 2, 0),
     (1, 3, 1),
@@ -325,143 +325,144 @@
     (7, 5, 0),
 )
 ROUTES = (
-    ((2, 10, 18), (4, 10, 32), (2,), (16,), (3,), (3,), (), (3,), ()),
-    ((4,), (0,), (10, 18), (10,), (), (7,), (1,), (), ()),
-    ((), (), (0,), (2,), (), (), (6,), (6,), ()),
-    ((5,), (), (), (), (14,), (14, 20), (14, 3), (1, 14), (4, 18)),
-    ((12, 24), (12, 24), (24,), (), (11,), (15,), (), (26,), ()),
-    ((), (), (), (), (15,), (9,), (9,), (), (5, 8)),
-    ((6,), (6, 28), (5, 8, 28), (5, 8, 28), (), (), (15,), (15, 9, 11), ()),
-    ((), (), (), (), (13,), (13,), (), (), (12, 40)),
-    ((), (), (), (), (21, 27), (), (), (27,), (1, 22)),
-    ((16, 32), (16,), (16, 34), (0, 32), (23,), (), (), (), (1, 38)),
-    ((), (), (22, 38), (38,), (), (), (17, 25, 51), (), ()),
-    ((20, 36, 7), (), (7,), (7, 20), (), (19,), (19,), (19, 29), ()),
-    ((28, 42), (42,), (40,), (), (), (27,), (27,), (), (26,)),
-    ((9, 46), (11, 44), (11,), (), (25,), (17, 21), (), (25,), ()),
-    ((), (), (), (), (), (31, 61, 23), (23, 31), (31,), (26, 30)),
-    ((), (), (13, 44), (13, 44), (29,), (), (), (), ()),
-    ((34,), (18, 34), (), (34,), (), (37,), (), (41,), (17, 51)),
-    ((), (), (32,), (), (), (43,), (), (), (25, 51, 60)),
-    ((38,), (22,), (), (), (33,), (45,), (33, 45), (33, 45), (21, 60, 55)),
-    ((), (36,), (36,), (36,), (), (), (), (), (17, 53)),
-    ((), (), (42,), (42, 24), (45, 56), (), (), (), (19, 59, 31, 57)),
-    ((40,), (40,), (), (), (35, 47), (), (), (), (29, 57)),
-    ((), (46,), (46,), (46,), (), (), (41,), (), (29, 63)),
-    ((44, 30), (30,), (), (), (), (), (39, 43), (39, 43), (23, 61)),
-    ((50, 54), (54,), (), (50,), (), (35, 39), (), (), ()),
-    ((41,), (33, 48, 56), (48, 56), (56,), (55,), (53,), (), (), ()),
-    ((), (), (), (), (), (55,), (), (55, 60, 51), (50, 54)),
-    ((37,), (), (37,), (37, 48), (53, 60), (), (), (21,), ()),
-    ((), (41,), (), (), (), (59,), (), (), (43, 49, 58)),
-    ((62,), (49, 62), (49, 35), (35, 49), (63,), (), (57,), (57,), ()),
-    ((), (), (53,), (), (), (63,), (), (63,), (62,)),
-    ((39, 52), (47, 52), (47, 52, 58), (47, 52, 58), (61,), (), (61, 59), (59,), ()),
+    ((2, 4, 10, 18), (10, 4), (2, 10, 18), (), (3,), (), (3,), (), ()),
+    ((), (0, 34), (), (0, 10), (7, 14), (), (), (1,), ()),
+    ((), (), (0,), (2,), (), (), (), (), ()),
+    ((5,), (), (5,), (), (), (), (1, 14), (14, 3), (4, 18)),
+    ((12, 24), (12, 24), (24,), (24,), (11,), (), (), (), ()),
+    ((), (), (), (), (), (9, 13), (), (9,), (5, 8)),
+    ((6, 28), (6, 28), (6, 8, 28), (8, 6, 28), (), (15,), (9, 15), (15,), ()),
+    ((), (), (), (), (13,), (), (), (), (5, 12, 40)),
+    ((), (18,), (), (), (), (27, 21), (), (27, 21), (1, 22)),
+    ((16, 34), (), (16, 34), (16, 34), (23, 31), (), (), (), (1, 22, 36, 3)),
+    ((36,), (), (7, 22), (7,), (), (), (17, 27), (), ()),
+    ((20,), (7, 20, 14), (36, 38), (20, 36), (), (), (19,), (19,), ()),
+    ((42,), (42,), (42,), (), (), (), (), (), (26, 30)),
+    ((9, 46), (11, 44), (11,), (11,), (17, 25), (25,), (25,), (25,), ()),
+    ((), (), (), (), (), (31, 61, 23), (31,), (23, 31), (30,)),
+    ((15,), (), (13, 26, 46), (13, 26, 44), (29,), (), (), (), ()),
+    ((), (), (), (), (), (), (41,), (), (27, 51)),
+    ((32,), (16, 32), (32,), (32,), (), (), (), (), (17, 51, 60)),
+    ((38,), (38,), (), (38,), (), (33,), (33, 45), (33, 45), (21, 55)),
+    ((), (), (), (), (47, 52), (), (), (35,), (17, 55)),
+    ((), (), (), (42,), (33, 56, 45), (45,), (), (), (19, 57)),
+    ((40,), (40,), (40,), (), (), (39,), (35,), (), (29, 57, 59)),
+    ((), (46, 30), (), (46,), (), (), (), (), (23, 61, 29)),
+    ((44,), (), (44,), (), (), (), (), (39, 43, 52), (29, 63)),
+    ((41, 50), (), (50, 56), (50, 56, 41), (35,), (35,), (), (), ()),
+    ((54,), (41, 48, 54, 56), (), (), (55,), (53,), (), (), ()),
+    ((), (), (), (), (), (55,), (), (), (54,)),
+    ((37,), (37,), (37, 48), (37, 48), (53, 60, 21), (), (53, 60, 51), (53, 60, 51), ()),
+    ((), (), (), (), (59, 63), (19,), (), (), (39, 58)),
+    ((49, 62), (43, 49, 62), (43, 49), (49,), (), (63,), (57,), (57,), ()),
+    ((), (), (), (), (), (), (63, 59), (59,), (39, 58, 62)),
+    ((43,), (52, 47), (52, 47), (47, 58), (61,), (), (), (61,), ()),
 )
 STEPS = (
-    (0, 17, 2, 19, 4, 10, 21, 8, 27, 25, 14, 6, 31, 23, 12, 29),
-    (2, 3, 0, 1, 4, 10, 8, 5, 6, 27, 7, 25, 14, 12, 31, 29),
-    (4, 5, 6, 7, 12, 10, 29, 14, 0, 2, 31, 11, 8, 1, 19, 25),
-    (14, 15, 4, 12, 5, 29, 6, 8, 0, 23, 9, 17, 10, 2, 11, 19),
-    (0, 17, 2, 19, 4, 10, 21, 27, 8, 6, 25, 23, 14, 12, 29, 31),
-    (10, 0, 11, 1, 2, 19, 8, 12, 4, 25, 13, 21, 14, 6, 15, 23),
-    (4, 5, 6, 7, 14, 0, 31, 1, 12, 2, 29, 3, 10, 27, 8, 25),
-    (14, 15, 6, 12, 23, 13, 10, 4, 11, 21, 8, 0, 9, 17, 2, 19),
-    (0, 8, 14, 1, 25, 15, 12, 4, 10, 5, 2, 29, 6, 11, 19, 23),
-    (0, 1, 6, 8, 7, 4, 14, 25, 5, 2, 31, 12, 3, 10, 29, 27),
-    (4, 5, 6, 7, 0, 12, 1, 29, 8, 25, 14, 10, 31, 2, 3, 27),
-    (6, 7, 4, 5, 0, 1, 14, 31, 12, 2, 8, 10, 3, 29, 27, 25),
-    (0, 1, 10, 2, 3, 27, 4, 8, 5, 12, 14, 25, 6, 29, 15, 23),
-    (2, 3, 0, 1, 4, 5, 10, 8, 27, 14, 25, 12, 6, 15, 29, 23),
-    (4, 12, 10, 5, 29, 11, 0, 6, 14, 8, 7, 1, 2, 31, 19, 25),
-    (6, 7, 4, 5, 12, 10, 8, 29, 2, 11, 0, 14, 19, 9, 17, 31),
-    (10, 11, 2, 14, 0, 15, 1, 19, 12, 6, 13, 23, 8, 25, 4, 21),
-    (8, 2, 14, 10, 0, 9, 17, 3, 15, 27, 6, 12, 4, 23, 13, 21),
-    (14, 4, 15, 2, 5, 12, 3, 6, 29, 10, 0, 8, 27, 23, 9, 17),
-    (4, 2, 5, 3, 6, 14, 15, 23, 12, 0, 10, 29, 1, 8, 27, 25),
-    (6, 8, 9, 10, 7, 0, 17, 11, 14, 2, 19, 4, 12, 31, 5, 29),
-    (8, 9, 14, 6, 0, 15, 17, 12, 23, 2, 13, 3, 10, 27, 4, 21),
-    (2, 6, 3, 7, 14, 0, 31, 4, 12, 1, 5, 8, 29, 25, 10, 27),
-    (14, 15, 2, 6, 12, 0, 3, 13, 8, 23, 10, 1, 25, 27, 4, 21),
-    (0, 1, 2, 3, 6, 10, 8, 4, 7, 27, 25, 14, 5, 31, 12, 29),
-    (2, 3, 0, 1, 10, 8, 4, 6, 25, 5, 27, 7, 14, 31, 12, 29),
-    (6, 14, 7, 4, 31, 5, 10, 2, 12, 8, 3, 9, 0, 27, 17, 29),
-    (6, 23, 4, 21, 0, 17, 14, 2, 12, 19, 31, 8, 10, 25, 29, 27),
-    (2, 10, 3, 27, 8, 4, 9, 12, 6, 0, 14, 13, 21, 17, 15, 23),
-    (2, 19, 0, 17, 6, 8, 23, 10, 4, 21, 27, 25, 12, 14, 29, 31),
-    (14, 4, 12, 15, 13, 2, 6, 21, 23, 10, 8, 3, 27, 0, 9, 17),
-    (6, 7, 4, 5, 2, 12, 3, 14, 29, 0, 31, 1, 8, 25, 10, 27),
+    (0, 1, 2, 3, 4, 10, 5, 8, 6, 25, 12, 27, 29, 7, 14, 31),
+    (2, 19, 0, 17, 4, 6, 8, 21, 10, 23, 25, 27, 12, 14, 29, 31),
+    (4, 5, 6, 7, 14, 0, 10, 12, 31, 1, 11, 29, 2, 19, 8, 25),
+    (12, 4, 13, 14, 21, 15, 10, 6, 23, 8, 0, 11, 1, 25, 2, 19),
+    (0, 17, 2, 19, 4, 10, 21, 27, 8, 6, 25, 23, 14, 12, 31, 29),
+    (10, 0, 11, 1, 2, 19, 8, 14, 25, 4, 15, 6, 12, 5, 29, 23),
+    (4, 5, 6, 7, 14, 0, 31, 1, 12, 2, 29, 10, 3, 8, 27, 25),
+    (14, 15, 4, 12, 5, 8, 29, 10, 6, 9, 11, 2, 23, 0, 19, 17),
+    (10, 14, 0, 6, 11, 15, 1, 2, 23, 12, 4, 8, 5, 29, 19, 25),
+    (0, 6, 8, 1, 7, 25, 4, 12, 5, 2, 10, 14, 3, 29, 27, 31),
+    (4, 5, 6, 7, 12, 2, 0, 29, 3, 1, 10, 14, 27, 8, 31, 25),
+    (6, 7, 4, 5, 2, 0, 12, 3, 1, 14, 8, 29, 10, 31, 25, 27),
+    (0, 1, 2, 8, 3, 4, 25, 5, 10, 12, 6, 7, 14, 29, 27, 31),
+    (2, 3, 0, 1, 6, 7, 8, 4, 5, 25, 10, 12, 14, 29, 27, 31),
+    (14, 4, 10, 15, 5, 12, 11, 6, 23, 0, 29, 8, 1, 2, 19, 25),
+    (6, 7, 4, 5, 0, 14, 10, 1, 31, 12, 11, 8, 2, 29, 19, 25),
+    (2, 14, 15, 3, 0, 12, 8, 6, 13, 1, 25, 23, 10, 4, 21, 27),
+    (2, 3, 0, 6, 10, 1, 7, 27, 14, 4, 12, 8, 5, 25, 31, 29),
+    (6, 14, 7, 31, 2, 4, 12, 13, 3, 21, 10, 27, 0, 8, 1, 25),
+    (6, 12, 7, 8, 4, 2, 14, 13, 9, 3, 10, 31, 21, 27, 0, 17),
+    (10, 8, 6, 11, 9, 7, 0, 14, 17, 31, 2, 19, 12, 4, 13, 21),
+    (10, 11, 6, 14, 0, 1, 12, 7, 31, 2, 19, 13, 4, 8, 21, 25),
+    (2, 6, 3, 7, 14, 0, 31, 10, 4, 1, 12, 8, 27, 5, 29, 25),
+    (14, 2, 6, 0, 3, 15, 23, 12, 4, 1, 13, 10, 21, 8, 27, 25),
+    (0, 1, 2, 3, 6, 10, 7, 27, 4, 8, 5, 25, 14, 12, 31, 29),
+    (2, 3, 0, 1, 10, 8, 6, 7, 25, 4, 27, 14, 5, 12, 31, 29),
+    (4, 14, 12, 5, 2, 15, 10, 29, 0, 3, 6, 8, 9, 27, 17, 23),
+    (6, 23, 4, 21, 2, 14, 12, 19, 0, 31, 29, 17, 8, 10, 25, 27),
+    (2, 10, 8, 3, 9, 6, 27, 7, 12, 0, 14, 17, 4, 13, 21, 31),
+    (2, 19, 0, 17, 6, 4, 8, 10, 23, 21, 25, 12, 14, 27, 29, 31),
+    (12, 14, 13, 6, 15, 2, 4, 23, 10, 8, 21, 0, 11, 19, 1, 25),
+    (6, 7, 4, 5, 2, 14, 3, 12, 31, 0, 29, 8, 1, 25, 10, 27),
 )
 PARTNERS = (
-    (1, 2, 4, 8, 3, 5, 9, 16),
+    (1, 2, 4, 8, 3, 9),
     (0, 3, 5, 9, 2),
-    (3, 0, 6, 10, 1, 5),
-    (2, 1, 7, 11, 0, 6, 9, 10),
-    (5, 6, 0, 12, 7, 13),
-    (4, 7, 1, 13, 0, 2, 6),
-    (7, 4, 2, 14, 3, 5, 15),
-    (6, 5, 3, 15, 4, 20),
-    (9, 10, 12, 0, 16, 11, 13, 19),
-    (8, 11, 13, 1, 17, 0, 3, 16, 19, 20),
-    (11, 8, 14, 2, 18, 3, 12, 13, 19, 25, 27),
-    (10, 9, 15, 3, 19, 8, 14, 18, 23),
-    (13, 14, 8, 4, 20, 10, 17, 21),
-    (12, 15, 9, 5, 21, 4, 8, 10, 14, 22, 23),
-    (15, 12, 10, 6, 22, 11, 13, 21, 30),
-    (14, 13, 11, 7, 23, 6, 20, 22),
-    (17, 18, 20, 8, 24, 0, 9, 25),
-    (16, 19, 21, 9, 25, 12, 24, 29, 30),
-    (19, 16, 22, 10, 26, 11, 27, 30),
-    (18, 17, 23, 11, 27, 8, 9, 10, 24, 26, 31),
-    (21, 22, 16, 12, 28, 7, 9, 15, 25, 29),
-    (20, 23, 17, 13, 29, 12, 14, 28),
-    (23, 20, 18, 14, 30, 13, 15, 31),
-    (22, 21, 19, 15, 31, 11, 13, 30),
-    (25, 26, 28, 16, 17, 19, 27, 29),
-    (24, 27, 29, 17, 10, 16, 20, 26, 28),
-    (27, 24, 30, 18, 19, 25, 31),
-    (26, 25, 31, 19, 10, 18, 24, 30),
+    (3, 0, 6, 10, 5, 7),
+    (2, 1, 7, 11, 6, 10),
+    (5, 6, 0, 12, 13),
+    (4, 7, 1, 13, 0),
+    (7, 4, 2, 14, 5, 15),
+    (6, 5, 3, 15, 1, 11),
+    (9, 10, 12, 0, 16, 13, 17, 19),
+    (8, 11, 13, 1, 17, 0, 3, 20, 28),
+    (11, 8, 14, 2, 18, 27),
+    (10, 9, 15, 3, 19, 8, 14, 22),
+    (13, 14, 8, 4, 20),
+    (12, 15, 9, 5, 21, 8, 10, 16),
+    (15, 12, 10, 6, 22, 21, 23),
+    (14, 13, 11, 7, 23, 9, 12, 22),
+    (17, 18, 20, 8, 24),
+    (16, 19, 21, 9, 25, 1, 24),
+    (19, 16, 22, 10, 26, 9, 11, 27),
+    (18, 17, 23, 11, 27, 21, 28, 30),
+    (21, 22, 16, 12, 28, 7, 24, 25),
+    (20, 23, 17, 13, 29, 12, 31),
+    (23, 20, 18, 14, 30, 13, 15),
+    (22, 21, 19, 15, 31, 13),
+    (25, 26, 28, 16, 27, 29),
+    (24, 27, 29, 17, 16),
+    (27, 24, 30, 18, 19, 23, 25, 31),
+    (26, 25, 31, 19, 18),
     (29, 30, 24, 20, 21, 25),
-    (28, 31, 25, 21, 17, 20, 24),
-    (31, 28, 26, 22, 14, 17, 18, 23, 27),
-    (30, 29, 27, 23, 19, 22, 26),
+    (28, 31, 25, 21, 30),
+    (31, 28, 26, 22, 14, 17, 27),
+    (30, 29, 27, 23, 28),
 )
 NEAR = (4, 4, 4, 4, 4, 4, 4, 4, 5, 5, 5, 5, 5, 5, 5, 5, 5, 5, 5, 5, 5, 5, 5, 5, 4, 4, 4, 4, 4, 4, 4, 4)
+AWAITED = (6, 6, 5, 6, 4, 6, 5, 6, 7, 8, 7, 7, 7, 9, 7, 7, 7, 7, 6, 7, 6, 8, 7, 7, 6, 7, 4, 8, 7, 5, 6, 6)
 NEWS = (
-    (8, 12, 15),
-    (5, 11, 15),
+    (8, 12, 14),
+    (5, 9, 15),
+    (6, 12, 14),
+    (3, 8, 12),
     (7, 12, 15),
-    (3, 10, 15),
-    (7, 13, 15),
     (4, 10, 15),
     (8, 12, 15),
-    (1, 8, 13),
-    (3, 6, 12),
-    (4, 6, 11),
-    (6, 8, 11),
-    (7, 10, 15),
-    (3, 7, 13),
-    (6, 8, 14),
-    (3, 8, 15),
-    (4, 9, 15),
-    (2, 6, 13),
-    (0, 4, 11),
-    (4, 13, 15),
-    (4, 8, 13),
-    (0, 5, 10),
+    (1, 7, 13),
+    (1, 7, 15),
+    (1, 7, 11),
+    (5, 10, 12),
+    (6, 9, 14),
+    (2, 5, 11),
+    (6, 10, 14),
+    (2, 7, 11),
+    (5, 9, 12),
+    (0, 2, 10),
+    (0, 3, 7),
+    (3, 9, 14),
+    (1, 8, 14),
+    (0, 4, 9),
+    (1, 5, 10),
     (2, 6, 12),
-    (3, 8, 15),
-    (3, 12, 15),
-    (7, 12, 15),
-    (7, 13, 14),
-    (3, 7, 14),
+    (1, 7, 14),
+    (6, 12, 15),
     (6, 11, 15),
-    (3, 6, 14),
-    (7, 13, 15),
-    (1, 6, 11),
-    (7, 12, 14),
+    (0, 6, 12),
+    (8, 12, 15),
+    (3, 7, 11),
+    (5, 10, 15),
+    (1, 5, 11),
+    (6, 10, 13),
 )
-PLANS = {(8, 4): (TILES, ROUTES, STEPS, PARTNERS, NEAR, NEWS)}
+PLANS = {(8, 4): (TILES, ROUTES, STEPS, PARTNERS, NEAR, NEWS, AWAITED)}
 
 
 TN = (((0,), (0,)), ((), ()))
@@ -485,7 +486,7 @@
     v = lax.axis_index("virt")
     p = lax.axis_index("aux")
     me = v * n_aux + p
-    tiles, routes, steps, partners, n_near, news = plan
+    tiles, routes, steps, partners, n_near, news, awaited = plan
     rounds = len(news[0]) + 1
     half = -(-rows // 32) * 16
     cuts = ((0, half), (half, -(-rows // 8) * 8 - half))
@@ -548,7 +549,7 @@
     held[own_slot, 0:rows, :] = lax.dot_general(
         raw[...], order[...], NN, preferred_element_type=F32
     ).astype(BF16)
-    pl.semaphore_wait(barrier, n_folk)
+    pl.semaphore_wait(barrier, pick(awaited, me))
 
     own_kids = pick([packed(r[o]) for r, o in zip(routes, owns)], me)
 

time: 26.4 us -> 26.2 us (level)
  no operation moved by 1% of the time
where the time goes in v7:
time: 26.2 us; the launch traced here: 26 us
  Pallas kernels  25.4 us (97%)
  between operations  0.64 us (2%)
    pallas_call x1, Pallas kernels, table_call(): pl.pallas_call(functools.partial(table_kernel, n_virt, n_aux, occ, plan),...  24.6 us
    pallas_call x1, Pallas kernels, table_call(): pl.pallas_call(functools.partial(table_unpack, occ, width), out_shape=(ja...  0.74 us

profile of v7, /device:TPU:0, one launch (start us, length us, event | category | flops | bytes accessed | tf_op | source)
XLA Modules:
  0.0 26.0 jit_solution(11658893910128500337)
XLA Ops:
  0.6 24.6 %shard_map.50.done_ref = f32[4,128]{1,0:T(4,128)S(1)} custom-call(bf16[150,640]{1,0:T(8,128)(2,1)} %x_ref.1, f32[20]{0:T(128)} %occ_hbm.1, f32[256]{0:T(256)} %virt_hbm.1), custom_call_target="tpu_custom_call" | custom-call | tf_op jit(solution)/shard_map/pallas_call | solution.py:830
  25.3 0.7 %shard_map.51 = (f32[32]{0:T(128)}, f32[20,20]{1,0:T(8,128)}) custom-call(f32[4,128]{1,0:T(4,128)S(1)} %shard_map.50.done_ref), custom_call_target="tpu_custom_call" | custom-call | tf_op jit(solution)/shard_map/pallas_call | solution.py:857

commit v8 on v7

--- a/solution.py
+++ b/solution.py
@@ -497,6 +497,41 @@
 
     barrier = pltpu.get_barrier_semaphore()
 
+    own = pltpu.make_async_copy(x_ref, raw, own_sem)
+    own.start()
+    if deep > rows:
+        held[:, rows:, :] = jnp.zeros((n_slots + 1, deep - rows, cols), BF16)
+
+    def packed(codes):
+        got = 0
+        for c in reversed(codes):
+            got = got * CODE + c + 1
+        return got
+
+    most = max(len(r) for r in partners)
+    folk = [
+        pick([packed(r[at:at + KIDS]) for r in partners], me) for at in range(0, most, KIDS)
+    ]
+    n_folk = pick([len(r) for r in partners], me)
+    near = pick(n_near, me)
+
+    def signal(sem, amount, limit):
+        code = None
+        for k in range(amount):
+            code = folk[k // KIDS] if k % KIDS == 0 else lax.div(code, CODE)
+
+            @pl.when(k < limit)
+            def _():
+                t = lax.rem(code, CODE) - 1
+                pl.semaphore_signal(sem, inc=1, device_id=device(t), device_id_type=MESH)
+
+    signal(barrier, most, n_folk)
+    eps = (
+        pltpu.make_async_copy(occ_hbm, occ_ref, eps_sem.at[0]),
+        pltpu.make_async_copy(virt_hbm, virt_ref, eps_sem.at[1]),
+    )
+    for copy in eps:
+        copy.start()
     side_a = pick([t[0] for t in tiles], me)
     side_b = pick([t[1] for t in tiles], me)
     diag = pick([t[2] for t in tiles], me) == 1
@@ -505,41 +540,6 @@
     for d, (a, b, _) in enumerate(tiles):
         q = d % n_aux
         owns.append(q if a == d // n_aux else n_aux + q if b == d // n_aux else n_slots)
-    own = pltpu.make_async_copy(x_ref, raw, own_sem)
-    own.start()
-    eps = (
-        pltpu.make_async_copy(occ_hbm, occ_ref, eps_sem.at[0]),
-        pltpu.make_async_copy(virt_hbm, virt_ref, eps_sem.at[1]),
-    )
-    for copy in eps:
-        copy.start()
-
-    def packed(codes):
-        got = 0
-        for c in reversed(codes):
-            got = got * CODE + c + 1
-        return got
-
-    most = max(len(r) for r in partners)
-    folk = [
-        pick([packed(r[at:at + KIDS]) for r in partners], me) for at in range(0, most, KIDS)
-    ]
-    n_folk = pick([len(r) for r in partners], me)
-    near = pick(n_near, me)
-
-    def signal(sem, amount, limit):
-        code = None
-        for k in range(amount):
-            code = folk[k // KIDS] if k % KIDS == 0 else lax.div(code, CODE)
-
-            @pl.when(k < limit)
-            def _():
-                t = lax.rem(code, CODE) - 1
-                pl.semaphore_signal(sem, inc=1, device_id=device(t), device_id_type=MESH)
-
-    if deep > rows:
-        held[:, rows:, :] = jnp.zeros((n_slots + 1, deep - rows, cols), BF16)
-    signal(barrier, most, n_folk)
 
     row = lax.broadcasted_iota(jnp.int32, (cols, cols), 0)
     col = lax.broadcasted_iota(jnp.int32, (cols, cols), 1)

time: 26.2 us -> 26.1 us (level)
  no operation moved by 1% of the time
where the time goes in v8:
time: 26.1 us; the launch traced here: 26 us
  Pallas kernels  25.3 us (97%)
  between operations  0.64 us (2%)
    pallas_call x1, Pallas kernels, table_call(): pl.pallas_call(functools.partial(table_kernel, n_virt, n_aux, occ, plan),...  24.6 us
    pallas_call x1, Pallas kernels, table_call(): pl.pallas_call(functools.partial(table_unpack, occ, width), out_shape=(ja...  0.74 us

profile of v8, /device:TPU:0, one launch (start us, length us, event | category | flops | bytes accessed | tf_op | source)
XLA Modules:
  0.0 26.0 jit_solution(15852872591311247209)
XLA Ops:
  0.6 24.6 %shard_map.50.done_ref = f32[4,128]{1,0:T(4,128)S(1)} custom-call(bf16[150,640]{1,0:T(8,128)(2,1)} %x_ref.1, f32[20]{0:T(128)} %occ_hbm.1, f32[256]{0:T(256)} %virt_hbm.1), custom_call_target="tpu_custom_call" | custom-call | tf_op jit(solution)/shard_map/pallas_call | solution.py:830
  25.2 0.7 %shard_map.51 = (f32[32]{0:T(128)}, f32[20,20]{1,0:T(8,128)}) custom-call(f32[4,128]{1,0:T(4,128)S(1)} %shard_map.50.done_ref), custom_call_target="tpu_custom_call" | custom-call | tf_op jit(solution)/shard_map/pallas_call | solution.py:857
